TPU v7x, 512 devices: a 8x2x16 block of a 8x8x16 slice. The times are simulated.
512 devices in a mesh: groups: 2 (over y), ep: 32 (over z, core), tp: 8 (over x).
Axes of the slice: x: 8, y: 2, z: 16, core: 2. Of those that a mesh axis runs over, the one named last changes fastest.
The devices are a block of a 8x8x16 slice.
Arguments:
- tokens: bfloat16 [8192, 2560], P(('groups', 'ep')), parts along dimension 0, may hold values from -6 to 6
- device_choice: int32 [8192, 3], P(('groups', 'ep')), parts along dimension 0, may hold values from 0 to 31, as said below
- local_expert: int32 [8192, 6], P(('groups', 'ep')), parts along dimension 0, may hold values from 0 to 1, as said below
- route_weight: float32 [8192, 6], P(('groups', 'ep')), parts along dimension 0, may hold values from 0.1 to 1
- prefill_ranks: int32 [32], P('groups'), parts along dimension 0, may hold values from 0 to 31, as said below
- w_gate: bfloat16 [64, 1024, 2560], P('ep', 'tp'), may hold values from -0.125 to 0.125
- w_up: bfloat16 [64, 1024, 2560], P('ep', 'tp'), may hold values from -0.125 to 0.125
- w_down: bfloat16 [64, 1024, 2560], P('ep', 'tp'), may hold values from -0.1875 to 0.1875
Outputs:
- moe_out: bfloat16 [8192, 2560], P(('groups', 'ep', 'tp')), parts along dimension 0
There are 2 independent parts, one for each index of `groups`. A program takes and returns all parts, laid end to end along the dimension named above; an argument that names none is the same for every part. Nothing has to cross between parts.
Inputs may be any that keep to these rules, and one draw needn't show every extreme that they name: `device_choice`: each row names 3 different ranks. The rows of one rank (aligned blocks of 128 rows) name any one rank at most 12 times, and every block names some rank exactly 12 times. `local_expert`: picks 2k and 2k + 1 of a row are two different experts of the rank in column k of device_choice. So the rows of one rank choose one expert at most 12 times, and some expert is chosen exactly 12 times by the rows of every rank. `prefill_ranks`: 16 different ranks.
All inputs are finite; a program needn't handle non-finite values.
Results may differ from a plain program's by a relative error of at most 0.014.
Values may be sent and summed in bfloat16 or wider, within the bound.
No kernel may reach another device: no remote copies, remote signals or barrier semaphores. Data moves between devices by JAX's collectives and lax.ppermute only.
A program may use at most 128 MiB of HBM per device.

v0:
```python
import jax
import jax.numpy as jnp
from jax import lax
from jax.sharding import PartitionSpec as P

TOPK = 6
DEV_TOP = 3
DEC_RANK = 8


def joined_along(parts, dim):
    dims = list(parts.shape[1:])
    dims[dim] *= parts.shape[0]
    return jnp.moveaxis(parts, 0, dim).reshape(dims)


def copy_for_each(array, axis):
    peers = lax.axis_size(axis)
    return lax.all_to_all(
        jnp.broadcast_to(array[None], (peers, *array.shape)), axis, 0, 0, tiled=True
    )


def collect(array, axis, dim):
    return joined_along(copy_for_each(array, axis), dim)


def count_slots(slot_keys, is_live, bin_count):
    hits = (
        slot_keys[:, :, None] == jnp.arange(bin_count, dtype=jnp.int32)[None, None, :]
    ) & is_live[:, None, None]
    flat_hits = hits.astype(jnp.int32).reshape(-1, bin_count)
    before = jnp.cumsum(flat_hits, axis=0) - flat_hits
    return jnp.sum(before * flat_hits, axis=1).reshape(slot_keys.shape)


def on_device(
    tokens, device_choice, local_expert, route_weight, prefill_ranks, w_gate, w_up, w_down
):
    rank_count = lax.axis_size("ep")
    lane_count = lax.axis_size("tp")
    own_rank = lax.axis_index("ep")
    rank_rows = tokens.shape[0]
    model_width = tokens.shape[1]
    experts_here = w_gate.shape[0]
    capacity = (DEV_TOP * rank_rows + rank_count - 1) // rank_count
    row_ids = jnp.arange(rank_rows, dtype=jnp.int32)
    is_live = (row_ids < DEC_RANK) | jnp.any(prefill_ranks == own_rank)
    pair_rank = jnp.repeat(device_choice, 2, axis=1)
    expert_keys = pair_rank * experts_here + local_expert
    positions = count_slots(device_choice, is_live, rank_count)
    send_ids = device_choice * capacity + positions
    send_count = rank_count * capacity
    pick_index = expert_keys * capacity + jnp.repeat(positions, 2, axis=1)
    block_shape = (rank_count, 1, capacity, model_width)
    slot_ids = jnp.arange(send_count, dtype=jnp.int32)
    select = jnp.any(
        (send_ids[None, :, :] == slot_ids[:, None, None]) & is_live[None, :, None], axis=2
    ).astype(jnp.bfloat16)
    outgoing = (
        jnp.dot(select, tokens, preferred_element_type=jnp.float32)
        .astype(jnp.bfloat16)
        .reshape(block_shape)
    )
    column_width = model_width // lane_count
    lane_slice = lax.dynamic_slice_in_dim(
        outgoing, lax.axis_index("tp") * column_width, column_width, 3
    )
    blocks = lax.all_to_all(lane_slice, "ep", split_axis=0, concat_axis=0, tiled=True)
    blocks = collect(blocks, "tp", 3)
    gate_act = jnp.einsum("scd,efd->secf", blocks[:, 0], w_gate, preferred_element_type=jnp.float32)
    up_act = jnp.einsum("scd,efd->secf", blocks[:, 0], w_up, preferred_element_type=jnp.float32)
    hidden = (jax.nn.silu(gate_act) * up_act).astype(jnp.bfloat16)
    partial_value = jnp.einsum(
        "secf,efd->secd", hidden, w_down, preferred_element_type=jnp.float32
    ).astype(jnp.bfloat16)
    columns = lax.psum_scatter(
        partial_value.astype(jnp.float32).astype(jnp.bfloat16),
        "tp",
        scatter_dimension=3,
        tiled=True,
    ).astype(jnp.float32)
    returned = lax.all_to_all(
        columns.astype(jnp.bfloat16), "ep", split_axis=0, concat_axis=0, tiled=True
    ).astype(columns.dtype)
    back_width = returned.shape[3]
    flat_back = returned.reshape(-1, back_width)
    weights = jnp.where(is_live[:, None], route_weight, jnp.zeros_like(route_weight))
    shares = jnp.zeros((rank_rows, back_width), jnp.float32)
    for pick_slot in range(TOPK):
        picked_rows = flat_back[pick_index[:, pick_slot]]
        shares = shares + weights[:, pick_slot : pick_slot + 1] * picked_rows
    return lax.all_to_all(
        shares.astype(jnp.bfloat16), "tp", split_axis=0, concat_axis=1, tiled=True
    )


def solution(mesh):
    in_specs = (
        P(("groups", "ep"), None),
        P(("groups", "ep"), None),
        P(("groups", "ep"), None),
        P(("groups", "ep"), None),
        P("groups"),
        P("ep", "tp", None),
        P("ep", "tp", None),
        P("ep", "tp", None),
    )
    out_specs = P(("groups", "ep", "tp"), None)
    return jax.shard_map(
        on_device, mesh=mesh, in_specs=in_specs, out_specs=out_specs, check_vma=False
    )
```

profile of v0, /device:TPU:80, one launch (start us, length us, event | category | flops | bytes accessed | tf_op | source)
XLA Modules:
  0.0 356.2 jit_solution(18115210274925047271)
XLA Ops:
  6.6 0.9 copy.62
  7.9 1.3 compare_reduce_fusion
  10.4 0.9 reduce-window.6
  12.7 1.7 convolution_convert_fusion.1
  14.4 2.2 reshape.102
  16.6 1.3 dynamic-slice_bitcast_fusion
  17.9 71.8 %all_to_all.31 = bf16[32,1,12,320]{3,2,1,0:T(8,128)(2,1)S(1)} all-to-all(bf16[32,1,12,320]{3,2,1,0:T(8,128)(2,1)S(1)} %dynamic-slice_bitcast_fusion), channel_id=1, replica_groups=mesh['groups'=2,'ep'=32,'tp'=8] {'ep'}, dimensions={0} | all-to-all | bytes 491520 | tf_op jit(solution)/shard_map/all_to_all | solution.py:69
  90.0 63.9 %all_to_all.32 = bf16[8,32,1,12,320]{4,1,3,2,0:T(8,128)(2,1)S(1)} all-to-all(bf16[8,32,1,12,320]{4,1,3,2,0:T(8,128)(2,1)S(1)} %broadcast_in_dim.21), channel_id=1, replica_groups=mesh['groups'=2,'ep'=32,'tp'=8] {'tp'}, dimensions={0} | all-to-all | bytes 3932160 | tf_op jit(solution)/shard_map/all_to_all | solution.py:19
  153.9 2.8 copy.68
  156.7 3.4 reshape.156
  160.2 2.1 fusion.8
  163.0 3.0 fusion
  166.1 28.8 %copy.77 = bf16[32,2,12,2560]{0,2,1,3:T(8,128)(2,1)} copy(bf16[32,2,12,2560]{3,0,2,1:T(8,128)(2,1)} %fusion) | data formatting | bytes 7864320
  194.9 25.3 %reshape.161 = bf16[2560,768]{1,0:T(8,128)(2,1)} reshape(bf16[2560,2,12,32]{3,2,1,0:T(8,128)(2,1)} %bitcast.98) | data formatting | bytes 7864320
  220.2 45.1 %reduce-scatter.4.cloned.1.call-done = bf16[320,768]{1,0:T(8,128)(2,1)} async-done(((bf16[2560,768]{1,0:T(8,128)(2,1)}), bf16[320,768]{1,0:T(8,128)(2,1)}) %reduce-scatter.4.cloned.1.call-update) | async-done | bytes 491536
  265.3 4.4 %reshape.162 = bf16[320,2,12,32]{3,2,1,0:T(8,128)(2,1)} reshape(bf16[320,768]{1,0:T(8,128)(2,1)} %reduce-scatter.4.cloned.1.call-done) | data formatting | bytes 983040
  269.7 6.0 %copy.70 = bf16[32,2,12,320]{3,1,2,0:T(2,128)(2,1)} copy(bf16[32,2,12,320]{0,2,1,3:T(8,128)(2,1)} %bitcast.99) | data formatting | bytes 983040 | tf_op jit(solution)/shard_map/reduce_scatter | solution.py:77
  275.6 14.1 %all-to-all-start.2 = ((bf16[32,2,12,320]{3,1,2,0:T(2,128)(2,1)}), bf16[32,2,12,320]{3,1,2,0:T(2,128)(2,1)S(1)}, u32[]{:S(2)}, u32[]{:S(2)}) async-start(bf16[32,2,12,320]{3,1,2,0:T(2,128)(2,1)} %copy.70), calls=%async_computation.2 | async-start | bytes 1179648 | tf_op jit(solution)/shard_map/all_to_all | solution.py:83
  290.4 35.0 %all-to-all-done.2 = bf16[32,2,12,320]{3,1,2,0:T(2,128)(2,1)S(1)} async-done(((bf16[32,2,12,320]{3,1,2,0:T(2,128)(2,1)}), bf16[32,2,12,320]{3,1,2,0:T(2,128)(2,1)S(1)}, u32[]{:S(2)}, u32[]{:S(2)}) %all-to-all-start.2) | async-done | bytes 491552 | tf_op jit(solution)/shard_map/all_to_all | solution.py:83
  325.5 1.9 copy.72
  327.4 1.5 reshape.107
  332.7 1.4 gather_fusion
  334.1 1.1 add_convert_fusion
  335.2 13.4 %all_to_all.33 = bf16[8,16,320]{2,1,0:T(8,128)(2,1)S(1)} all-to-all(bf16[8,16,320]{2,1,0:T(8,128)(2,1)S(1)} %add_convert_fusion), channel_id=1, replica_groups=mesh['groups'=2,'ep'=32,'tp'=8] {'tp'}, dimensions={0} | all-to-all | bytes 163840 | tf_op jit(solution)/shard_map/all_to_all | solution.py:93
  (52 shorter events, 9.4 us)
Async XLA Ops:
  6.5 156.5 %copy-start = (bf16[2,128,2560]{2,1,0:T(8,128)(2,1)S(1)}, bf16[2,128,2560]{2,1,0:T(8,128)(2,1)}, u32[]{:S(2)}) copy-start(bf16[2,128,2560]{2,1,0:T(8,128)(2,1)} %param.15) | copy-start | bytes 3932164
  6.6 258.8 %reduce-scatter.4.cloned.1.call-start = ((), (), s32[]{:S(2)}) async-start(), calls=%async_computation.5 | async-start | bytes 4423680
  160.2 2.1 copy-start.3
  269.7 20.1 %copy-start.1 = (f32[128,6]{0,1:T(8,128)S(1)}, f32[128,6]{0,1:T(8,128)}, u32[]{:S(2)}) copy-start(f32[128,6]{0,1:T(8,128)} %param.11) | copy-start | bytes 9220
  269.7 20.6 %copy-start.2 = (s32[128,6]{0,1:T(8,128)S(1)}, s32[128,6]{0,1:T(8,128)}, u32[]{:S(2)}) copy-start(s32[128,6]{0,1:T(8,128)} %param.10) | copy-start | bytes 9220
  275.6 49.8 %all-to-all-start.2 = ((bf16[32,2,12,320]{3,1,2,0:T(2,128)(2,1)}), bf16[32,2,12,320]{3,1,2,0:T(2,128)(2,1)S(1)}, u32[]{:S(2)}, u32[]{:S(2)}) async-start(bf16[32,2,12,320]{3,1,2,0:T(2,128)(2,1)} %copy.70), calls=%async_computation.2 | async-start | bytes 1179648 | tf_op jit(solution)/shard_map/all_to_all | solution.py:83
Sparse Core Ops, SparseCore 0:
  220.3 44.9 reduce-scatter.3
where the time goes:
time: 358 us; the launch traced here: 356 us
  blocking collectives  149 us (42%)
  local copies, waits for them, and re-layouts  86.5 us (24%)
  waiting for transfers between devices  80.2 us (22%)
  starting transfers between devices  14.1 us (4%)
  between operations  13.7 us (4%)
  matrix products  7.61 us (2%)
  other arithmetic  5.08 us (1%)
    all_to_all x1, blocking collectives, on_device(): lax.all_to_all(lane_slice, 'ep', split_axis=0, concat_axis=0, tiled=True)  71.8 us
    all_to_all x1, blocking collectives, copy_for_each(): lax.all_to_all(jnp.broadcast_to(array[None], (peers, *array.shape)), axis...  63.9 us
    unnamed x12, local copies, waits for them, and re-layouts  59.3 us
    unnamed x2, waiting for transfers between devices  45.2 us
    all_to_all x1, waiting for transfers between devices, on_device(): lax.all_to_all(columns.astype(jnp.bfloat16), 'ep', split_axis=0, concat_a...  35 us
    all_to_all x1, starting transfers between devices, on_device(): lax.all_to_all(columns.astype(jnp.bfloat16), 'ep', split_axis=0, concat_a...  14.1 us
    all_to_all x1, blocking collectives, on_device(): lax.all_to_all(shares.astype(jnp.bfloat16), 'tp', split_axis=0, concat_ax...  13.4 us
  transfers between devices with their start and end apart: 2, of which 2 were waited for; matrix products, arithmetic and copies ran while one was open for 0% of the time, Pallas kernels for 0%

commit v1 on v0

v1 whole, which is shorter than its diff:
```python
import jax
import jax.numpy as jnp
from jax import lax
from jax.experimental import pallas as pl
from jax.experimental.pallas import tpu as pltpu
from jax.sharding import PartitionSpec as P

TOPK = 6
DEV_TOP = 3
DEC_RANK = 8
LANE = 128
F32, BF16, I32 = jnp.float32, jnp.bfloat16, jnp.int32
INTERPRET = False


class Plan:
    def __init__(self, ranks, lanes, rows, width, prefill):
        self.ranks, self.lanes, self.rows, self.width = ranks, lanes, rows, width
        self.cap = (DEV_TOP * rows + ranks - 1) // ranks
        self.prefill = prefill
        self.half_pre = self.cap // 2
        self.half_dec = DEC_RANK // 2
        self.half = prefill * self.half_pre + (ranks - prefill) * self.half_dec
        self.slots = 2 * self.half
        self.packed = 5 * self.half
        self.chunk = 2 * self.cap + self.half_pre + 2
        self.own_rows = rows // lanes
        assert width == (2 * lanes + lanes // 2) * LANE and self.chunk % 8 == 0
        assert 4 * ranks <= LANE or ranks * 3 <= LANE
        assert rows == LANE


def iota(shape, dim):
    return lax.broadcasted_iota(I32, shape, dim)


def one_hot(mask):
    return jnp.where(mask, 1.0, 0.0).astype(BF16)


def dot(a, b):
    return jnp.dot(a, b, preferred_element_type=F32)


def is_prefill(pre_ref, plan, own):
    found = pre_ref[0] == own
    for i in range(1, plan.prefill):
        found = found | (pre_ref[i] == own)
    return found


def earlier(plan):
    shape = (plan.rows, plan.rows)
    return one_hot(iota(shape, 0) < iota(shape, 1))


def chunk_index(j, plan, parity, half_slots):
    cap = plan.cap
    block = jnp.where(j < cap, 0, jnp.where(j < 2 * cap, 1, 2))
    slot = jnp.where(j < cap, j, jnp.where(j < 2 * cap, j - cap, j - 2 * cap + parity * half_slots))
    kept = (j < 2 * cap) | (j - 2 * cap < half_slots)
    return jnp.where(kept, block, 3), slot


def pack_kernel(plan, meta_ref, pre_ref, dc_ref, le_ref, rw_ref, tok_ref, tail_ref, out_ref):
    lane, own = meta_ref[0], meta_ref[1]
    full = is_prefill(pre_ref, plan, own)
    half_slots = jnp.where(full, plan.half_pre, plan.half_dec)
    rows, ranks = plan.rows, plan.ranks
    shape = (rows, LANE)
    limit = jnp.where(full, rows, DEC_RANK)
    live = iota(shape, 0) < limit
    col = iota(shape, 1)
    which, rank = col // ranks, col % ranks
    table = jnp.zeros(shape, F32)
    for k in range(DEV_TOP):
        hit = (dc_ref[:, k : k + 1] == rank) & live
        value = jnp.where(which == 0, 1.0, 0.0)
        for j in (2 * k, 2 * k + 1):
            value += jnp.where(le_ref[:, j : j + 1] == which - 1, rw_ref[:, j : j + 1], 0.0)
        table += jnp.where(hit, value, 0.0)
    turned = table.T
    named = turned[:ranks]
    before = dot(named.astype(BF16), earlier(plan))
    place = jnp.where(named > 0.5, before, -1.0).astype(I32)
    full_shape = (ranks, plan.chunk, LANE)
    j = iota(full_shape, 1)
    block, slot = chunk_index(j, plan, lane % 2, half_slots)
    match = place[:, None, :] == slot
    blocks = (tok_ref[:, :LANE], tok_ref[:, LANE:], tail_ref[...])
    total = jnp.zeros((ranks * plan.chunk, LANE), F32)
    for b in range(3):
        pick = one_hot(match & (block == b)).reshape(ranks * plan.chunk, LANE)
        total += dot(pick, blocks[b])
    total = total.reshape(full_shape)
    first = turned[ranks : 2 * ranks][:, None, :]
    second = turned[2 * ranks : 3 * ranks][:, None, :]
    total = jnp.where(j == plan.chunk - 2, first, jnp.where(j == plan.chunk - 1, second, total))
    out_ref[...] = total.astype(BF16)


def target_row(pre_ref, plan, shape, dim):
    c = iota(shape, dim)
    src, j = c // plan.chunk, c % plan.chunk
    hits = jnp.zeros(shape, I32)
    lower = jnp.zeros(shape, I32)
    for i in range(plan.prefill):
        hits += jnp.where(src == pre_ref[i], 1, 0)
        lower += jnp.where(src > pre_ref[i], 1, 0)
    full = hits > 0
    n = jnp.where(full, plan.half_pre, plan.half_dec)
    base = jnp.where(
        full, lower * plan.half_pre, plan.prefill * plan.half_pre + (src - lower) * plan.half_dec
    )
    b = jnp.where(j < plan.cap, 0, jnp.where(j < 2 * plan.cap, 1, 2))
    jj = j - b * plan.cap
    second = jnp.where((jj >= n) & (b < 2), 1, 0)
    kept = (jj - second * n) < n
    return jnp.where(kept, (2 * b + second) * plan.half + base + jj - second * n, -1)


def compact_kernel(plan, pre_ref, in_ref, out_ref, weight_ref):
    total = plan.ranks * plan.chunk
    target = target_row(pre_ref, plan, (1, total), 1)
    data = in_ref[...].reshape(total, LANE)
    ranks = plan.ranks
    pick_shape = (ranks, total)
    where_first = iota(pick_shape, 0) * plan.chunk + plan.chunk - 2
    col = iota(pick_shape, 1)
    first = dot(one_hot(col == where_first), data)
    second = dot(one_hot(col == where_first + 1), data)
    named = first > 0.0
    before = dot(one_hot(named), earlier(plan))
    place = jnp.where(named, before, -1.0).astype(I32)
    full_shape = (ranks, plan.chunk, LANE)
    j = iota(full_shape, 1)
    match = (place[:, None, :] == j) & (j < plan.cap)
    wide = []
    for value in (first, second):
        kept = jnp.where(match, value[:, None, :], 0.0)
        column = jnp.sum(kept, axis=2, keepdims=True)
        wide.append(jnp.broadcast_to(column, full_shape).reshape(total, LANE).astype(BF16))
    for piece in range(5):
        shape = (plan.half, total)
        take = one_hot(iota(shape, 0) + piece * plan.half == target)
        at = pl.ds(piece * plan.half, plan.half)
        out_ref[at, :] = dot(take, data).astype(BF16)
        if piece < 2:
            for e in range(2):
                weight_ref[at, e * LANE : (e + 1) * LANE] = dot(take, wide[e])


def expert_kernel(plan, offsets, meta_ref, *refs):
    n = len(offsets)
    parts = refs[:n]
    weight_ref, wg_ref, wu_ref, wd_ref, out_ref, x_ref = refs[n:]
    me = meta_ref[0]
    lanes, half, slots = plan.lanes, plan.half, plan.slots
    for offset, part in zip(offsets, parts):
        lane = lax.rem(me + offset + lanes, lanes)
        at = pl.multiple_of(lane * (2 * LANE), 2 * LANE)
        x_ref[:, pl.ds(at, LANE)] = part[0:slots, :]
        x_ref[:, pl.ds(pl.multiple_of(at + LANE, LANE), LANE)] = part[slots : 2 * slots, :]
        tail = pl.multiple_of((2 * lanes + lane // 2) * LANE, LANE)
        start = pl.multiple_of(lax.rem(lane, 2) * half, half)
        x_ref[pl.ds(start, half), pl.ds(tail, LANE)] = part[2 * slots : 2 * slots + half, :]
    x = x_ref[...]
    turned = (((1,), (1,)), ((), ()))
    gate = lax.dot_general(x, wg_ref[...], turned, preferred_element_type=F32)
    up = lax.dot_general(x, wu_ref[...], turned, preferred_element_type=F32)
    hidden = gate / (1.0 + jnp.exp(-gate)) * up * weight_ref[...]
    hidden = hidden.astype(BF16)
    for lane in range(lanes):
        at = lane * 2 * LANE
        y = dot(hidden, wd_ref[:, at : at + 2 * LANE]).astype(BF16)
        out_ref[lane, 0:slots, :] = y[:, :LANE]
        out_ref[lane, slots : 2 * slots, :] = y[:, LANE:]
    for pair in range(lanes // 2):
        at = (2 * lanes + pair) * LANE
        y = dot(hidden, wd_ref[:, at : at + LANE]).astype(BF16)
        out_ref[2 * pair, 2 * slots : 2 * slots + half, :] = y[:half]
        out_ref[2 * pair + 1, 2 * slots : 2 * slots + half, :] = y[half:]


def spread_kernel(plan, pre_ref, in_ref, out_ref):
    total = in_ref[0].astype(F32)
    for lane in range(1, plan.lanes):
        total += in_ref[lane].astype(F32)
    total = total.astype(BF16)
    chunk_rows = plan.ranks * plan.chunk
    target = target_row(pre_ref, plan, (chunk_rows, 1), 0)
    shape = (chunk_rows, plan.packed)
    take = one_hot(iota(shape, 1) == target)
    out_ref[...] = dot(take, total).astype(BF16).reshape(plan.ranks, plan.chunk, LANE)


def combine_kernel(plan, meta_ref, pre_ref, dc_ref, in_ref, out_ref):
    lane, own = meta_ref[0], meta_ref[1]
    full = is_prefill(pre_ref, plan, own)
    half_slots = jnp.where(full, plan.half_pre, plan.half_dec)
    rows, ranks = plan.rows, plan.ranks
    shape = (rows, ranks)
    live = iota(shape, 0) < jnp.where(full, rows, DEC_RANK)
    rank = iota(shape, 1)
    named = jnp.zeros(shape, F32)
    for k in range(DEV_TOP):
        named += jnp.where((dc_ref[:, k : k + 1] == rank) & live, 1.0, 0.0)
    square = (rows, rows)
    before = dot(one_hot(iota(square, 1) < iota(square, 0)), named.astype(BF16))
    place = jnp.where(named > 0.5, before, -1.0).astype(BF16)
    total = ranks * plan.chunk
    spread = (ranks, total)
    wide = dot(place, one_hot(iota(spread, 1) // plan.chunk == iota(spread, 0))).astype(I32)
    j = iota((1, total), 1) % plan.chunk
    block, slot = chunk_index(j, plan, lane % 2, half_slots)
    data = in_ref[...].reshape(total, LANE)
    own_rows = plan.own_rows
    match = wide == slot
    for b in range(3):
        mine = dot(one_hot(match & (block == b)), data).astype(BF16)
        for to in range(plan.lanes):
            out_ref[to, b * own_rows : (b + 1) * own_rows, :] = mine[
                to * own_rows : (to + 1) * own_rows
            ]


def finish_kernel(plan, in_ref, out_ref):
    n = plan.own_rows
    for lane in range(plan.lanes):
        at = lane * 2 * LANE
        out_ref[:, at : at + LANE] = in_ref[lane, 0:n, :]
        out_ref[:, at + LANE : at + 2 * LANE] = in_ref[lane, n : 2 * n, :]
    for pair in range(plan.lanes // 2):
        at = (2 * plan.lanes + pair) * LANE
        first = in_ref[2 * pair, 2 * n : 3 * n, :].astype(F32)
        second = in_ref[2 * pair + 1, 2 * n : 3 * n, :].astype(F32)
        out_ref[:, at : at + LANE] = (first + second).astype(BF16)


SMEM = pl.BlockSpec(memory_space=pltpu.SMEM)
VMEM = pl.BlockSpec(memory_space=pltpu.VMEM)


def call(kernel, name, out, specs, *args, scratch=(), limit=24 << 20, **kw):
    return pl.pallas_call(
        kernel,
        out_shape=out,
        in_specs=specs,
        out_specs=jax.tree.map(lambda _: VMEM, out),
        scratch_shapes=scratch,
        compiler_params=pltpu.CompilerParams(vmem_limit_bytes=limit),
        interpret=INTERPRET,
        name=name,
        **kw,
    )(*args)


def pack(plan, meta, prefill_ranks, device_choice, local_expert, route_weight, tokens):
    def whole(i, meta, pre):
        return (0, 0)

    rows = plan.rows
    grid_spec = pltpu.PrefetchScalarGridSpec(
        num_scalar_prefetch=2,
        grid=(1,),
        in_specs=[
            pl.BlockSpec((rows, DEV_TOP), whole),
            pl.BlockSpec((rows, TOPK), whole),
            pl.BlockSpec((rows, TOPK), whole),
            pl.BlockSpec((rows, 2 * LANE), lambda i, meta, pre: (0, meta[0])),
            pl.BlockSpec(
                (rows, LANE), lambda i, meta, pre: (0, 2 * plan.lanes + meta[0] // 2)
            ),
        ],
        out_specs=pl.BlockSpec((plan.ranks, plan.chunk, LANE), lambda i, meta, pre: (0, 0, 0)),
    )
    return pl.pallas_call(
        lambda *refs: pack_kernel(plan, *refs),
        grid_spec=grid_spec,
        out_shape=jax.ShapeDtypeStruct((plan.ranks, plan.chunk, LANE), BF16),
        compiler_params=pltpu.CompilerParams(vmem_limit_bytes=24 << 20),
        interpret=INTERPRET,
        name="pack",
    )(meta, prefill_ranks, device_choice, local_expert, route_weight, tokens, tokens)


def compact(plan, prefill_ranks, received):
    return call(
        lambda *refs: compact_kernel(plan, *refs),
        "compact",
        (
            jax.ShapeDtypeStruct((plan.packed, LANE), BF16),
            jax.ShapeDtypeStruct((plan.slots, 2 * LANE), F32),
        ),
        [SMEM, VMEM],
        prefill_ranks,
        received,
    )


def experts(plan, offsets, meta, parts, weights, w_gate, w_up, w_down):
    hidden = w_gate.shape[0] * w_gate.shape[1]
    flat = [w.reshape(hidden, plan.width) for w in (w_gate, w_up, w_down)]
    return call(
        lambda *refs: expert_kernel(plan, offsets, *refs),
        "experts",
        jax.ShapeDtypeStruct((plan.lanes, plan.packed, LANE), BF16),
        [SMEM] + [VMEM] * (len(parts) + 4),
        meta,
        *parts,
        weights,
        *flat,
        scratch=[pltpu.VMEM((plan.slots, plan.width), BF16)],
        limit=32 << 20,
    )


def spread(plan, prefill_ranks, returned):
    return call(
        lambda *refs: spread_kernel(plan, *refs),
        "spread",
        jax.ShapeDtypeStruct((plan.ranks, plan.chunk, LANE), BF16),
        [SMEM, VMEM],
        prefill_ranks,
        returned,
    )


def combine(plan, meta, prefill_ranks, device_choice, back):
    return call(
        lambda *refs: combine_kernel(plan, *refs),
        "combine",
        jax.ShapeDtypeStruct((plan.lanes, 3 * plan.own_rows, LANE), BF16),
        [SMEM, SMEM, VMEM, VMEM],
        meta,
        prefill_ranks,
        device_choice,
        back,
    )


def finish(plan, shares):
    return call(
        lambda *refs: finish_kernel(plan, *refs),
        "finish",
        jax.ShapeDtypeStruct((plan.own_rows, plan.width), BF16),
        [VMEM],
        shares,
    )


def gather_ring(packed, lanes):
    right = [(i, (i + 1) % lanes) for i in range(lanes)]
    left = [(i, (i - 1) % lanes) for i in range(lanes)]
    parts, offsets = [packed], [0]
    from_left = from_right = packed
    for hop in range(1, lanes // 2 + 1):
        from_left = lax.ppermute(from_left, "tp", right)
        parts.append(from_left)
        offsets.append(-hop)
        if hop < lanes // 2:
            from_right = lax.ppermute(from_right, "tp", left)
            parts.append(from_right)
            offsets.append(hop)
    return parts, offsets


def on_device(
    tokens, device_choice, local_expert, route_weight, prefill_ranks, w_gate, w_up, w_down
):
    plan = Plan(
        lax.axis_size("ep"),
        lax.axis_size("tp"),
        tokens.shape[0],
        tokens.shape[1],
        prefill_ranks.shape[0],
    )
    meta = jnp.stack([lax.axis_index("tp"), lax.axis_index("ep")]).astype(I32)
    outgoing = pack(
        plan, meta, prefill_ranks, device_choice, local_expert, route_weight, tokens
    )
    received = lax.all_to_all(outgoing, "ep", 0, 0, tiled=True)
    packed, weights = compact(plan, prefill_ranks, received)
    parts, offsets = gather_ring(packed, plan.lanes)
    partial = experts(plan, offsets, meta, parts, weights, w_gate, w_up, w_down)
    returned = lax.all_to_all(partial, "tp", 0, 0, tiled=True)
    back = spread(plan, prefill_ranks, returned)
    back = lax.all_to_all(back, "ep", 0, 0, tiled=True)
    shares = combine(plan, meta, prefill_ranks, device_choice, back)
    shares = lax.all_to_all(shares, "tp", 0, 0, tiled=True)
    return finish(plan, shares)


def solution(mesh):
    in_specs = (
        P(("groups", "ep"), None),
        P(("groups", "ep"), None),
        P(("groups", "ep"), None),
        P(("groups", "ep"), None),
        P("groups"),
        P("ep", "tp", None),
        P("ep", "tp", None),
        P("ep", "tp", None),
    )
    out_specs = P(("groups", "ep", "tp"), None)
    return jax.shard_map(
        on_device, mesh=mesh, in_specs=in_specs, out_specs=out_specs, check_vma=False
    )
```

time: 358 us -> 205 us (0.57)
  local copies, waits for them, and re-layouts: 86.5 us -> 6.77 us
  waiting for transfers between devices: 80.2 us -> 14.2 us
  between operations: 13.7 us -> 0.13 us
  Pallas kernels: 0 us -> 11 us
  starting transfers between devices: 14.1 us -> 23.9 us
  matrix products: 7.61 us -> 0 us
  other arithmetic: 5.08 us -> 0.07 us
    unnamed x12 -> x15, local copies, waits for them, and re-layouts: 59.3 us -> 6.77 us
    unnamed x2 -> x0, waiting for transfers between devices: 45.2 us -> none
    all_to_all x1 -> x0, waiting for transfers between devices: 35 us -> none  [on_device(): lax.all_to_all(columns.astype(jnp.bfloat16), 'ep', split_axis=0, concat_a...]
    ppermute x0 -> x7, starting transfers between devices: none -> 23.9 us  [the longest x3 14.5 us: gather_ring(): from_right = lax.ppermute(from_right, 'tp', left)]
    ppermute x0 -> x7, waiting for transfers between devices: none -> 14.2 us  [the longest x4 14.2 us: gather_ring(): from_left = lax.ppermute(from_left, 'tp', right)]
    all_to_all x1 -> x0, starting transfers between devices: 14.1 us -> none  [on_device(): lax.all_to_all(columns.astype(jnp.bfloat16), 'ep', split_axis=0, concat_a...]
    pallas_call x0 -> x6, Pallas kernels: none -> 11 us  [the longest x5 9.45 us: call(): pl.pallas_call(kernel, out_shape=out, in_specs=specs, out_specs=jax.tree....]
    dot_general x4 -> x0, matrix products: 7.61 us -> none  [the longest x1 3.04 us: on_device(): jnp.einsum('secf,efd->secd', hidden, w_down, preferred_element_type=jnp.f...]
  transfers between devices with their start and end apart: 2 -> 7, of which waited for: 2 -> 4; matrix products, arithmetic and copies ran while one was open for 0% -> 0% of each run, Pallas kernels for 0% -> 0%
where the time goes in v1:
time: 205 us
  blocking collectives  149 us (73%)
  starting transfers between devices  23.9 us (12%)
  waiting for transfers between devices  14.2 us (7%)
  Pallas kernels  11 us (5%)
  local copies, waits for them, and re-layouts  6.77 us (3%)
    all_to_all x1, blocking collectives, on_device(): received = lax.all_to_all(outgoing, 'ep', 0, 0, tiled=True)  66.2 us
    all_to_all x1, blocking collectives, on_device(): returned = lax.all_to_all(partial, 'tp', 0, 0, tiled=True)  43.4 us
    all_to_all x1, blocking collectives, on_device(): back = lax.all_to_all(back, 'ep', 0, 0, tiled=True)  27.8 us
    ppermute x3, starting transfers between devices, gather_ring(): from_right = lax.ppermute(from_right, 'tp', left)  14.5 us
    ppermute x4, waiting for transfers between devices, gather_ring(): from_left = lax.ppermute(from_left, 'tp', right)  14.2 us
    all_to_all x1, blocking collectives, on_device(): shares = lax.all_to_all(shares, 'tp', 0, 0, tiled=True)  11.2 us
    pallas_call x5, Pallas kernels, call(): pl.pallas_call(kernel, out_shape=out, in_specs=specs, out_specs=jax.tree....  9.45 us
    ppermute x4, starting transfers between devices, gather_ring(): from_left = lax.ppermute(from_left, 'tp', right)  9.39 us
  transfers between devices with their start and end apart: 7, of which 4 were waited for; matrix products, arithmetic and copies ran while one was open for 0% of the time, Pallas kernels for 0%

profile of v1, /device:TPU:80, one launch (start us, length us, event | category | flops | bytes accessed | tf_op | source)
XLA Modules:
  0.0 204.7 jit_solution(12240430385216346195)
XLA Ops:
  0.0 0.8 copy.12.refs_2_
  2.5 1.1 copy-done
  4.2 1.5 pack.1
  5.8 66.2 %all_to_all.20.refs_1_ = bf16[32,32,128]{2,1,0:T(8,128)(2,1)S(1)} all-to-all(bf16[32,32,128]{2,1,0:T(8,128)(2,1)S(1)} %pack.1), channel_id=1, replica_groups=mesh['groups'=2,'ep'=32,'tp'=8] {'ep'}, dimensions={0} | all-to-all | bytes 524288 | tf_op jit(solution)/shard_map/all_to_all | solution.py:382
  72.0 1.9 compact.1
  73.9 3.6 %collective-permute-start = (bf16[800,128]{1,0:T(8,128)(2,1)S(1)}, bf16[800,128]{1,0:T(8,128)(2,1)S(1)}, u32[]{:S(2)}, u32[]{:S(2)}) collective-permute-start(bf16[800,128]{1,0:T(8,128)(2,1)S(1)} %get-tuple-element.7.refs_1_), channel_id=1, source_target_pairs={{0,1},{1,2},{2,3},{3,4},{4,5},{5,6},{6,7},{7,0},{8,9},{9,10},{10,1... | collective-permute-start | bytes 614408 | tf_op jit(solution)/shard_map/ppermute | solution.py:358
  77.5 4.1 %collective-permute-start.1 = (bf16[800,128]{1,0:T(8,128)(2,1)S(1)}, bf16[800,128]{1,0:T(8,128)(2,1)S(1)}, u32[]{:S(2)}, u32[]{:S(2)}) collective-permute-start(bf16[800,128]{1,0:T(8,128)(2,1)S(1)} %get-tuple-element.7.refs_1_), channel_id=1, source_target_pairs={{0,7},{1,0},{2,1},{3,2},{4,3},{5,4},{6,5},{7,6},{8,15},{9,8},{10,9... | collective-permute-start | bytes 614408 | tf_op jit(solution)/shard_map/ppermute | solution.py:362
  81.7 3.2 %collective-permute-done.refs_2_ = bf16[800,128]{1,0:T(8,128)(2,1)S(1)} collective-permute-done((bf16[800,128]{1,0:T(8,128)(2,1)S(1)}, bf16[800,128]{1,0:T(8,128)(2,1)S(1)}, u32[]{:S(2)}, u32[]{:S(2)}) %collective-permute-start) | collective-permute-done | bytes 204832 | tf_op jit(solution)/shard_map/ppermute | solution.py:358
  84.8 1.9 collective-permute-start.2
  86.8 5.2 %collective-permute-start.3 = (bf16[800,128]{1,0:T(8,128)(2,1)S(1)}, bf16[800,128]{1,0:T(8,128)(2,1)S(1)}, u32[]{:S(2)}, u32[]{:S(2)}) collective-permute-start(bf16[800,128]{1,0:T(8,128)(2,1)S(1)} %collective-permute-done.1.refs_3_), channel_id=1, source_target_pairs={{0,7},{1,0},{2,1},{3,2},{4,3},{5,4},{6,5},{7,6},{8,15},{9,8},{10,9... | collective-permute-start | bytes 614408 | tf_op jit(solution)/shard_map/ppermute | solution.py:362
  92.0 2.3 %collective-permute-done.2.refs_4_ = bf16[800,128]{1,0:T(8,128)(2,1)S(1)} collective-permute-done((bf16[800,128]{1,0:T(8,128)(2,1)S(1)}, bf16[800,128]{1,0:T(8,128)(2,1)S(1)}, u32[]{:S(2)}, u32[]{:S(2)}) %collective-permute-start.2) | collective-permute-done | bytes 204832 | tf_op jit(solution)/shard_map/ppermute | solution.py:358
  94.3 1.9 collective-permute-start.4
  96.2 5.2 %collective-permute-start.5 = (bf16[800,128]{1,0:T(8,128)(2,1)S(1)}, bf16[800,128]{1,0:T(8,128)(2,1)S(1)}, u32[]{:S(2)}, u32[]{:S(2)}) collective-permute-start(bf16[800,128]{1,0:T(8,128)(2,1)S(1)} %collective-permute-done.3.refs_5_), channel_id=1, source_target_pairs={{0,7},{1,0},{2,1},{3,2},{4,3},{5,4},{6,5},{7,6},{8,15},{9,8},{10,9... | collective-permute-start | bytes 614408 | tf_op jit(solution)/shard_map/ppermute | solution.py:362
  101.4 1.8 collective-permute-done.4.refs_6_
  103.2 1.9 collective-permute-start.6
  105.1 6.9 %collective-permute-done.6.refs_8_ = bf16[800,128]{1,0:T(8,128)(2,1)S(1)} collective-permute-done((bf16[800,128]{1,0:T(8,128)(2,1)S(1)}, bf16[800,128]{1,0:T(8,128)(2,1)S(1)}, u32[]{:S(2)}, u32[]{:S(2)}) %collective-permute-start.6) | collective-permute-done | bytes 204832 | tf_op jit(solution)/shard_map/ppermute | solution.py:358
  112.0 1.3 copy-done.2
  113.4 1.3 copy-done.3
  114.7 2.5 %experts.1 = bf16[8,800,128]{2,1,0:T(8,128)(2,1)S(1)} custom-call(s32[2]{0:T(128)S(1)} %pad_add_fusion.refs_0_, bf16[800,128]{1,0:T(8,128)(2,1)S(1)} %get-tuple-element.7.refs_1_, bf16[800,128]{1,0:T(8,128)(2,1)S(1)} %collective-permute-done.refs_2_, bf16[800,128]{1,0:T(8,128)(2,1)S(1)} %collective-permute-done.1.refs_3_, ...), custom_call_target="tpu_custom_call" | custom-call | tf_op jit(solution)/shard_map/experts/pallas_call | solution.py:245
  117.1 43.4 %all_to_all.21.refs_1_ = bf16[8,800,128]{2,1,0:T(8,128)(2,1)S(1)} all-to-all(bf16[8,800,128]{2,1,0:T(8,128)(2,1)S(1)} %experts.1), channel_id=1, replica_groups=mesh['groups'=2,'ep'=32,'tp'=8] {'tp'}, dimensions={0} | all-to-all | bytes 3276800 | tf_op jit(solution)/shard_map/all_to_all | solution.py:386
  160.5 3.1 %spread.1 = bf16[32,32,128]{2,1,0:T(8,128)(2,1)S(1)} custom-call(s32[16]{0:T(128)S(1)} %copy-done.5, bf16[8,800,128]{2,1,0:T(8,128)(2,1)S(1)} %all_to_all.21.refs_1_), custom_call_target="tpu_custom_call" | custom-call | tf_op jit(solution)/shard_map/spread/pallas_call | solution.py:245
  163.7 27.8 %all_to_all.22.refs_3_ = bf16[32,32,128]{2,1,0:T(8,128)(2,1)S(1)} all-to-all(bf16[32,32,128]{2,1,0:T(8,128)(2,1)S(1)} %spread.1), channel_id=1, replica_groups=mesh['groups'=2,'ep'=32,'tp'=8] {'ep'}, dimensions={0} | all-to-all | bytes 524288 | tf_op jit(solution)/shard_map/all_to_all | solution.py:388
  191.5 1.3 combine.1
  192.8 11.2 %all_to_all.23.refs_0_ = bf16[8,48,128]{2,1,0:T(8,128)(2,1)S(1)} all-to-all(bf16[8,48,128]{2,1,0:T(8,128)(2,1)S(1)} %combine.1), channel_id=1, replica_groups=mesh['groups'=2,'ep'=32,'tp'=8] {'tp'}, dimensions={0} | all-to-all | bytes 196608 | tf_op jit(solution)/shard_map/all_to_all | solution.py:390
  (16 shorter events, 3.0 us)
Async XLA Ops:
  0.0 72.0 %copy-start.5 = (s32[16]{0:T(128)S(1)}, s32[16]{0:T(128)}, u32[]{:S(2)}) copy-start(s32[16]{0:T(128)} %refs_1_.3) | copy-start | bytes 196
  2.5 1.1 copy-start
  3.6 0.7 copy-start.4
  4.2 107.8 %copy-start.1 = (bf16[2,128,2560]{2,1,0:T(8,128)(2,1)S(1)}, bf16[2,128,2560]{2,1,0:T(8,128)(2,1)}, u32[]{:S(2)}) copy-start(bf16[2,128,2560]{2,1,0:T(8,128)(2,1)} %param.13) | copy-start | bytes 3932164
  73.9 10.9 %collective-permute-start = (bf16[800,128]{1,0:T(8,128)(2,1)S(1)}, bf16[800,128]{1,0:T(8,128)(2,1)S(1)}, u32[]{:S(2)}, u32[]{:S(2)}) collective-permute-start(bf16[800,128]{1,0:T(8,128)(2,1)S(1)} %get-tuple-element.7.refs_1_), channel_id=1, source_target_pairs={{0,1},{1,2},{2,3},{3,4},{4,5},{5,6},{6,7},{7,0},{8,9},{9,10},{10,1... | collective-permute-start | bytes 614408 | tf_op jit(solution)/shard_map/ppermute | solution.py:358
  77.5 9.3 %collective-permute-start.1 = (bf16[800,128]{1,0:T(8,128)(2,1)S(1)}, bf16[800,128]{1,0:T(8,128)(2,1)S(1)}, u32[]{:S(2)}, u32[]{:S(2)}) collective-permute-start(bf16[800,128]{1,0:T(8,128)(2,1)S(1)} %get-tuple-element.7.refs_1_), channel_id=1, source_target_pairs={{0,7},{1,0},{2,1},{3,2},{4,3},{5,4},{6,5},{7,6},{8,15},{9,8},{10,9... | collective-permute-start | bytes 614408 | tf_op jit(solution)/shard_map/ppermute | solution.py:362
  84.8 9.4 %collective-permute-start.2 = (bf16[800,128]{1,0:T(8,128)(2,1)S(1)}, bf16[800,128]{1,0:T(8,128)(2,1)S(1)}, u32[]{:S(2)}, u32[]{:S(2)}) collective-permute-start(bf16[800,128]{1,0:T(8,128)(2,1)S(1)} %collective-permute-done.refs_2_), channel_id=1, source_target_pairs={{0,1},{1,2},{2,3},{3,4},{4,5},{5,6},{6,7},{7,0},{8,9},{9,10},{10,1... | collective-permute-start | bytes 614408 | tf_op jit(solution)/shard_map/ppermute | solution.py:358
  86.8 9.4 %collective-permute-start.3 = (bf16[800,128]{1,0:T(8,128)(2,1)S(1)}, bf16[800,128]{1,0:T(8,128)(2,1)S(1)}, u32[]{:S(2)}, u32[]{:S(2)}) collective-permute-start(bf16[800,128]{1,0:T(8,128)(2,1)S(1)} %collective-permute-done.1.refs_3_), channel_id=1, source_target_pairs={{0,7},{1,0},{2,1},{3,2},{4,3},{5,4},{6,5},{7,6},{8,15},{9,8},{10,9... | collective-permute-start | bytes 614408 | tf_op jit(solution)/shard_map/ppermute | solution.py:362
  94.3 8.9 %collective-permute-start.4 = (bf16[800,128]{1,0:T(8,128)(2,1)S(1)}, bf16[800,128]{1,0:T(8,128)(2,1)S(1)}, u32[]{:S(2)}, u32[]{:S(2)}) collective-permute-start(bf16[800,128]{1,0:T(8,128)(2,1)S(1)} %collective-permute-done.2.refs_4_), channel_id=1, source_target_pairs={{0,1},{1,2},{2,3},{3,4},{4,5},{5,6},{6,7},{7,0},{8,9},{9,10},{10,1... | collective-permute-start | bytes 614408 | tf_op jit(solution)/shard_map/ppermute | solution.py:358
  96.2 8.9 %collective-permute-start.5 = (bf16[800,128]{1,0:T(8,128)(2,1)S(1)}, bf16[800,128]{1,0:T(8,128)(2,1)S(1)}, u32[]{:S(2)}, u32[]{:S(2)}) collective-permute-start(bf16[800,128]{1,0:T(8,128)(2,1)S(1)} %collective-permute-done.3.refs_5_), channel_id=1, source_target_pairs={{0,7},{1,0},{2,1},{3,2},{4,3},{5,4},{6,5},{7,6},{8,15},{9,8},{10,9... | collective-permute-start | bytes 614408 | tf_op jit(solution)/shard_map/ppermute | solution.py:362
  103.2 8.9 %collective-permute-start.6 = (bf16[800,128]{1,0:T(8,128)(2,1)S(1)}, bf16[800,128]{1,0:T(8,128)(2,1)S(1)}, u32[]{:S(2)}, u32[]{:S(2)}) collective-permute-start(bf16[800,128]{1,0:T(8,128)(2,1)S(1)} %collective-permute-done.4.refs_6_), channel_id=1, source_target_pairs={{0,1},{1,2},{2,3},{3,4},{4,5},{5,6},{6,7},{7,0},{8,9},{9,10},{10,1... | collective-permute-start | bytes 614408 | tf_op jit(solution)/shard_map/ppermute | solution.py:358
  112.0 1.3 copy-start.2
  113.4 1.3 copy-start.3

commit v2 on v1

v2 whole, which is shorter than its diff:
```python
import jax
import jax.numpy as jnp
from jax import lax
from jax.experimental import pallas as pl
from jax.experimental.pallas import tpu as pltpu
from jax.sharding import PartitionSpec as P

TOPK = 6
DEV_TOP = 3
DEC_RANK = 8
LANE = 128
F32, BF16, I32 = jnp.float32, jnp.bfloat16, jnp.int32
INTERPRET = False


class Plan:
    def __init__(self, ranks, lanes, rows, width, prefill):
        self.ranks, self.lanes, self.rows, self.width = ranks, lanes, rows, width
        self.cap = (DEV_TOP * rows + ranks - 1) // ranks
        self.prefill = prefill
        self.half_pre = self.cap // 2
        self.half_dec = DEC_RANK // 2
        self.half = prefill * self.half_pre + (ranks - prefill) * self.half_dec
        self.slots = 2 * self.half
        self.packed = 5 * self.half
        self.packed_up = -(-self.packed // LANE) * LANE
        self.side = self.packed // 2
        self.step = next(n for n in range(200, 0, -8) if self.side % n == 0)
        self.chunk = 2 * self.cap + self.half_pre + 2
        self.own_rows = rows // lanes
        assert width == (2 * lanes + lanes // 2) * LANE and self.chunk % 8 == 0
        assert 4 * ranks <= LANE or ranks * 3 <= LANE
        assert rows == LANE


def iota(shape, dim):
    return lax.broadcasted_iota(I32, shape, dim)


def one_hot(mask):
    return jnp.where(mask, 1.0, 0.0).astype(BF16)


def dot(a, b):
    return jnp.dot(a, b, preferred_element_type=F32)


def is_prefill(pre_ref, plan, own):
    found = pre_ref[0] == own
    for i in range(1, plan.prefill):
        found = found | (pre_ref[i] == own)
    return found


def earlier(plan):
    shape = (plan.rows, plan.rows)
    return one_hot(iota(shape, 0) < iota(shape, 1))


def chunk_index(j, plan, parity, half_slots):
    cap = plan.cap
    block = jnp.where(j < cap, 0, jnp.where(j < 2 * cap, 1, 2))
    slot = jnp.where(j < cap, j, jnp.where(j < 2 * cap, j - cap, j - 2 * cap + parity * half_slots))
    kept = (j < 2 * cap) | (j - 2 * cap < half_slots)
    return jnp.where(kept, block, 3), slot


def named_ranks(plan, full, dc_ref):
    shape = (plan.ranks, plan.rows)
    live = iota(shape, 1) < jnp.where(full, plan.rows, DEC_RANK)
    rank = iota(shape, 0)
    hits = [(dc_ref[k : k + 1, :] == rank) & live for k in range(DEV_TOP)]
    named = sum(jnp.where(hit, 1.0, 0.0) for hit in hits)
    return hits, named, places(plan, named)


def places(plan, named):
    before = dot(named.astype(BF16), earlier(plan))
    return jnp.where(named > 0.5, before, -1.0)


def pack_kernel(plan, meta_ref, pre_ref, dc_ref, le_ref, rw_ref, tok_ref, out_ref, x_ref, sems):
    lane, own = meta_ref[0], meta_ref[1]
    first_at = pl.multiple_of(lane * (2 * LANE), LANE)
    tail_at = pl.multiple_of((2 * plan.lanes + lane // 2) * LANE, LANE)
    copies = [
        pltpu.make_async_copy(
            tok_ref.at[:, pl.ds(first_at, 2 * LANE)], x_ref.at[:, 0 : 2 * LANE], sems.at[0]
        ),
        pltpu.make_async_copy(
            tok_ref.at[:, pl.ds(tail_at, LANE)], x_ref.at[:, 2 * LANE : 3 * LANE], sems.at[1]
        ),
    ]
    for copy in copies:
        copy.start()
    full = is_prefill(pre_ref, plan, own)
    half_slots = jnp.where(full, plan.half_pre, plan.half_dec)
    hits, named, place = named_ranks(plan, full, dc_ref)
    weights = []
    for e in range(2):
        total = jnp.zeros(named.shape, F32)
        for k, hit in enumerate(hits):
            for j in (2 * k, 2 * k + 1):
                chosen = hit & (le_ref[j : j + 1, :] == e)
                total += jnp.where(chosen, rw_ref[j : j + 1, :], 0.0)
        weights.append(total)
    full_shape = (plan.ranks, plan.chunk, LANE)
    flat = plan.ranks * plan.chunk
    j = iota(full_shape, 1)
    block, slot = chunk_index(j, plan, lane % 2, half_slots)
    match = place.astype(I32)[:, None, :] == slot
    picks = [one_hot(match & (block == b)).reshape(flat, LANE) for b in range(3)]
    for copy in copies:
        copy.wait()
    total = sum(dot(picks[b], x_ref[:, b * LANE : (b + 1) * LANE]) for b in range(3))
    total = total.reshape(full_shape)
    total = jnp.where(j == plan.chunk - 2, weights[0][:, None, :], total)
    total = jnp.where(j == plan.chunk - 1, weights[1][:, None, :], total)
    out_ref[...] = total.astype(BF16)


def target_row(pre_ref, plan, shape, dim):
    c = iota(shape, dim)
    src, j = c // plan.chunk, c % plan.chunk
    hits = jnp.zeros(shape, I32)
    lower = jnp.zeros(shape, I32)
    for i in range(plan.prefill):
        hits += jnp.where(src == pre_ref[i], 1, 0)
        lower += jnp.where(src > pre_ref[i], 1, 0)
    full = hits > 0
    n = jnp.where(full, plan.half_pre, plan.half_dec)
    base = jnp.where(
        full, lower * plan.half_pre, plan.prefill * plan.half_pre + (src - lower) * plan.half_dec
    )
    b = jnp.where(j < plan.cap, 0, jnp.where(j < 2 * plan.cap, 1, 2))
    jj = j - b * plan.cap
    second = jnp.where((jj >= n) & (b < 2), 1, 0)
    kept = (jj - second * n) < n
    return jnp.where(kept, (2 * b + second) * plan.half + base + jj - second * n, -1)


def compact_kernel(plan, pre_ref, in_ref, a_ref, b_ref):
    total = plan.ranks * plan.chunk
    target = target_row(pre_ref, plan, (1, total), 1)
    data = in_ref[...].reshape(total, LANE)
    side = plan.side
    for ref, begin in ((a_ref, 0), (b_ref, side)):
        for at in range(0, side, plan.step):
            shape = (plan.step, total)
            take = one_hot(iota(shape, 0) + (begin + at) == target)
            ref[at : at + plan.step, :] = dot(take, data).astype(BF16)


def tables_kernel(plan, meta_ref, pre_ref, dc_ref, in_ref, weight_ref, spread_ref, combine_ref):
    lane, own = meta_ref[0], meta_ref[1]
    ranks, rows = plan.ranks, plan.rows
    total = ranks * plan.chunk
    data = in_ref[...].reshape(total, LANE)
    target = target_row(pre_ref, plan, (1, total), 1)
    pick_shape = (ranks, total)
    where_first = iota(pick_shape, 0) * plan.chunk + plan.chunk - 2
    col = iota(pick_shape, 1)
    first = dot(one_hot(col == where_first), data)
    second = dot(one_hot(col == where_first + 1), data)
    place = places(plan, jnp.where(first > 0.0, 1.0, 0.0)).astype(I32)
    full_shape = (ranks, plan.chunk, LANE)
    j = iota(full_shape, 1)
    match = (place[:, None, :] == j) & (j < plan.cap)
    wide = []
    for value in (first, second):
        kept = jnp.where(match, value[:, None, :], 0.0)
        column = jnp.sum(kept, axis=2, keepdims=True)
        wide.append(jnp.broadcast_to(column, full_shape).reshape(total, LANE).astype(BF16))
    for piece in range(2):
        shape = (plan.half, total)
        take = one_hot(iota(shape, 0) + piece * plan.half == target)
        for e in range(2):
            at = piece * plan.half
            weight_ref[at : at + plan.half, e * LANE : (e + 1) * LANE] = dot(take, wide[e])
    column = target_row(pre_ref, plan, (total, LANE), 0)
    for at in range(0, plan.packed_up, LANE):
        spread_ref[:, at : at + LANE] = one_hot(iota((total, LANE), 1) + at == column)
    full = is_prefill(pre_ref, plan, own)
    half_slots = jnp.where(full, plan.half_pre, plan.half_dec)
    _, _, place = named_ranks(plan, full, dc_ref)
    square = jnp.concatenate([place, jnp.zeros((rows - ranks, rows), F32)], axis=0)
    turned = square.T[:, :ranks].astype(BF16)
    expand = one_hot(col // plan.chunk == iota(pick_shape, 0))
    spots = dot(turned, expand).astype(I32)
    j = iota((1, total), 1) % plan.chunk
    block, slot = chunk_index(j, plan, lane % 2, half_slots)
    match = spots == slot
    for b in range(3):
        combine_ref[:, b * total : (b + 1) * total] = one_hot(match & (block == b))


def lane_at(plan, me, sign, steps):
    return lax.rem(me + sign * steps + plan.lanes, plan.lanes)


def expert_kernel(plan, meta_ref, *refs):
    n = len(GATHERED)
    a_refs, b_refs = refs[:n], refs[n : 2 * n]
    weight_ref, wg_ref, wu_ref, wd_ref = refs[2 * n : 2 * n + 4]
    outs = refs[2 * n + 4 : -6]
    x_ref, h_ref, wg, wu, wd, sems = refs[-6:]
    loads = [
        pltpu.make_async_copy(src, dst, sems.at[i])
        for i, (src, dst) in enumerate(((wg_ref, wg), (wu_ref, wu), (wd_ref, wd)))
    ]
    for load in loads:
        load.start()
    me = meta_ref[0]
    sign = 1 - 2 * lax.rem(me, 2)
    lanes, half, slots, side = plan.lanes, plan.half, plan.slots, plan.side
    over = side - slots

    def columns(lane):
        first = pl.multiple_of(lane * (2 * LANE), LANE)
        tail = pl.multiple_of((2 * lanes + lane // 2) * LANE, LANE)
        start = pl.multiple_of(lax.rem(lane, 2) * half, 8)
        return (
            pl.ds(first, LANE),
            pl.ds(pl.multiple_of(first + LANE, LANE), LANE),
            pl.ds(tail, LANE),
            pl.ds(start, half),
        )

    for refs_of, turn in ((a_refs, sign), (b_refs, -sign)):
        for ref, steps in zip(refs_of, GATHERED):
            for i, step in enumerate(steps):
                first, second, tail, rows = columns(lane_at(plan, me, turn, step))
                at = i * side
                if refs_of is a_refs:
                    x_ref[:, first] = ref[at : at + slots, :]
                    x_ref[0:over, second] = ref[at + slots : at + side, :]
                else:
                    x_ref[over:slots, second] = ref[at : at + slots - over, :]
                    x_ref[rows, tail] = ref[at + slots - over : at + side, :]
    turned = (((1,), (1,)), ((), ()))
    x = x_ref[...]
    loads[0].wait()
    gate = lax.dot_general(x, wg[...], turned, preferred_element_type=F32)
    loads[1].wait()
    up = lax.dot_general(x, wu[...], turned, preferred_element_type=F32)
    hidden = gate / (1.0 + jnp.exp(-gate)) * up * weight_ref[...]
    h_ref[...] = hidden.astype(BF16)
    loads[2].wait()
    out = 0
    for steps in SCATTERED:
        for turn in (sign, -sign):
            for i, step in enumerate(steps):
                first, second, tail, rows = columns(lane_at(plan, me, turn, step))
                ref, at = outs[out], i * side
                if turn is sign:
                    ref[at : at + slots, :] = dot(h_ref[...], wd[:, first]).astype(BF16)
                    ref[at + slots : at + side, :] = dot(h_ref[0:over, :], wd[:, second]).astype(BF16)
                else:
                    ref[at : at + slots - over, :] = dot(h_ref[over:slots, :], wd[:, second]).astype(BF16)
                    ref[at + slots - over : at + side, :] = dot(h_ref[rows, :], wd[:, tail]).astype(BF16)
            out += 1


def spread_kernel(plan, take_ref, own_a, got_a, own_b, got_b, out_ref, sum_ref):
    side = plan.side
    sum_ref[0:side, :] = (own_a[...].astype(F32) + got_a[...].astype(F32)).astype(BF16)
    sum_ref[side : 2 * side, :] = (own_b[...].astype(F32) + got_b[...].astype(F32)).astype(BF16)
    sum_ref[2 * side :, :] = jnp.zeros((plan.packed_up - 2 * side, LANE), BF16)
    spread = dot(take_ref[...], sum_ref[...]).astype(BF16)
    out_ref[...] = spread.reshape(plan.ranks, plan.chunk, LANE)


def combine_kernel(plan, take_ref, in_ref, out_ref):
    total = plan.ranks * plan.chunk
    data = in_ref[...].reshape(total, LANE)
    own_rows = plan.own_rows
    for b in range(3):
        mine = dot(take_ref[:, b * total : (b + 1) * total], data).astype(BF16)
        for to in range(plan.lanes):
            out_ref[to, b * own_rows : (b + 1) * own_rows, :] = mine[
                to * own_rows : (to + 1) * own_rows
            ]


def finish_kernel(plan, in_ref, out_ref):
    n = plan.own_rows
    for lane in range(plan.lanes):
        at = lane * 2 * LANE
        out_ref[:, at : at + LANE] = in_ref[lane, 0:n, :]
        out_ref[:, at + LANE : at + 2 * LANE] = in_ref[lane, n : 2 * n, :]
    for pair in range(plan.lanes // 2):
        at = (2 * plan.lanes + pair) * LANE
        first = in_ref[2 * pair, 2 * n : 3 * n, :].astype(F32)
        second = in_ref[2 * pair + 1, 2 * n : 3 * n, :].astype(F32)
        out_ref[:, at : at + LANE] = (first + second).astype(BF16)


SMEM = pl.BlockSpec(memory_space=pltpu.SMEM)
VMEM = pl.BlockSpec(memory_space=pltpu.VMEM)
HBM = pl.BlockSpec(memory_space=pltpu.HBM)
GATHERED = ((0,), (1,), (-1, -2), (2, 3), (-3, -4))
SCATTERED = ((-3, -4), (2, 3), (-1, -2), (0,), (1,))


def call(kernel, name, out, specs, *args, scratch=(), limit=24 << 20, flops=0):
    cost = None
    if flops:
        cost = pl.CostEstimate(flops=flops, bytes_accessed=1 << 20, transcendentals=0)
    return pl.pallas_call(
        kernel,
        out_shape=out,
        in_specs=specs,
        out_specs=jax.tree.map(lambda _: VMEM, out),
        scratch_shapes=scratch,
        compiler_params=pltpu.CompilerParams(vmem_limit_bytes=limit),
        cost_estimate=cost,
        interpret=INTERPRET,
        name=name,
    )(*args)


def pack(plan, meta, prefill_ranks, choice, local_expert, route_weight, tokens):
    return call(
        lambda *refs: pack_kernel(plan, *refs),
        "pack",
        jax.ShapeDtypeStruct((plan.ranks, plan.chunk, LANE), BF16),
        [SMEM, SMEM, VMEM, VMEM, VMEM, HBM],
        meta,
        prefill_ranks,
        choice,
        local_expert,
        route_weight,
        tokens,
        scratch=[pltpu.VMEM((plan.rows, 3 * LANE), BF16), pltpu.SemaphoreType.DMA((2,))],
    )


def compact(plan, prefill_ranks, received):
    share = jax.ShapeDtypeStruct((plan.side, LANE), BF16)
    return call(
        lambda *refs: compact_kernel(plan, *refs),
        "compact",
        (share, share),
        [SMEM, VMEM],
        prefill_ranks,
        received,
    )


def tables(plan, meta, prefill_ranks, choice, received):
    total = plan.ranks * plan.chunk
    return call(
        lambda *refs: tables_kernel(plan, *refs),
        "tables",
        (
            jax.ShapeDtypeStruct((plan.slots, 2 * LANE), F32),
            jax.ShapeDtypeStruct((total, plan.packed_up), BF16),
            jax.ShapeDtypeStruct((plan.rows, 3 * total), BF16),
        ),
        [SMEM, SMEM, VMEM, VMEM],
        meta,
        prefill_ranks,
        choice,
        received,
        flops=1 << 30,
    )


def experts(plan, meta, a_parts, b_parts, weights, w_gate, w_up, w_down):
    hidden = w_gate.shape[0] * w_gate.shape[1]
    flat = [w.reshape(hidden, plan.width) for w in (w_gate, w_up, w_down)]
    out = []
    for steps in SCATTERED:
        out += [jax.ShapeDtypeStruct((len(steps) * plan.side, LANE), BF16)] * 2
    weight = pltpu.VMEM((hidden, plan.width), BF16)
    outs = call(
        lambda *refs: expert_kernel(plan, *refs),
        "experts",
        tuple(out),
        [SMEM] + [VMEM] * (2 * len(a_parts) + 1) + [HBM] * 3,
        meta,
        *a_parts,
        *b_parts,
        weights,
        *flat,
        scratch=[
            pltpu.VMEM((plan.slots, plan.width), BF16),
            pltpu.VMEM((plan.slots, hidden), BF16),
            weight,
            weight,
            weight,
            pltpu.SemaphoreType.DMA((3,)),
        ],
        limit=32 << 20,
    )
    return outs[0::2], outs[1::2]


def spread(plan, take, own_a, got_a, own_b, got_b):
    return call(
        lambda *refs: spread_kernel(plan, *refs),
        "spread",
        jax.ShapeDtypeStruct((plan.ranks, plan.chunk, LANE), BF16),
        [VMEM] * 5,
        take,
        own_a,
        got_a,
        own_b,
        got_b,
        scratch=[pltpu.VMEM((plan.packed_up, LANE), BF16)],
    )


def combine(plan, take, back):
    return call(
        lambda *refs: combine_kernel(plan, *refs),
        "combine",
        jax.ShapeDtypeStruct((plan.lanes, 3 * plan.own_rows, LANE), BF16),
        [VMEM, VMEM],
        take,
        back,
    )


def finish(plan, shares):
    return call(
        lambda *refs: finish_kernel(plan, *refs),
        "finish",
        jax.ShapeDtypeStruct((plan.own_rows, plan.width), BF16),
        [VMEM],
        shares,
    )


def neighbours(lanes):
    near = [(i, i ^ 1) for i in range(lanes)]
    far = [(i, (i - 1 + 2 * (i % 2)) % lanes) for i in range(lanes)]
    return near, far


def swap(arrays, pairs):
    return [lax.ppermute(x, "tp", p) for x, p in zip(arrays, pairs)]


def gather_lanes(shares, lanes):
    near, far = neighbours(lanes)
    own = list(shares)
    first = swap(own, (near, far))
    held = [jnp.concatenate([x, y]) for x, y in zip(own, first)]
    parts = [own, first]
    for hop in range(lanes // 2 - 1):
        held = swap(held, (far, near) if hop % 2 == 0 else (near, far))
        parts.append(held)
    return [p[0] for p in parts], [p[1] for p in parts]


def plus(x, y):
    return (x.astype(F32) + y.astype(F32)).astype(BF16)


def reduce_lanes(a_outs, b_outs, side, lanes):
    near, far = neighbours(lanes)
    stages = list(zip(a_outs, b_outs))
    held = list(stages[0])
    for hop in range(lanes // 2 - 2):
        got = swap(held, (far, near) if hop % 2 == 0 else (near, far))
        held = [plus(x, y) for x, y in zip(stages[hop + 1], got)]
    got = swap(held, (far, near))
    away = [plus(x, y[side:]) for x, y in zip(stages[-1], got)]
    home = [plus(x, y[:side]) for x, y in zip(stages[-2], got)]
    last = swap(away, (near, far))
    return home[0], last[0], home[1], last[1]


def on_device(
    tokens, device_choice, local_expert, route_weight, prefill_ranks, w_gate, w_up, w_down
):
    plan = Plan(
        lax.axis_size("ep"),
        lax.axis_size("tp"),
        tokens.shape[0],
        tokens.shape[1],
        prefill_ranks.shape[0],
    )
    meta = jnp.stack([lax.axis_index("tp"), lax.axis_index("ep")]).astype(I32)
    choice = device_choice.T
    outgoing = pack(
        plan, meta, prefill_ranks, choice, local_expert.T, route_weight.T, tokens
    )
    received = lax.all_to_all(outgoing, "ep", 0, 0, tiled=True)
    shares = compact(plan, prefill_ranks, received)
    weights, take_out, take_in = tables(plan, meta, prefill_ranks, choice, received)
    a_parts, b_parts = gather_lanes(shares, plan.lanes)
    a_outs, b_outs = experts(plan, meta, a_parts, b_parts, weights, w_gate, w_up, w_down)
    sums = reduce_lanes(a_outs, b_outs, plan.side, plan.lanes)
    back = lax.all_to_all(spread(plan, take_out, *sums), "ep", 0, 0, tiled=True)
    shares = lax.all_to_all(combine(plan, take_in, back), "tp", 0, 0, tiled=True)
    return finish(plan, shares)


def solution(mesh):
    in_specs = (
        P(("groups", "ep"), None),
        P(("groups", "ep"), None),
        P(("groups", "ep"), None),
        P(("groups", "ep"), None),
        P("groups"),
        P("ep", "tp", None),
        P("ep", "tp", None),
        P("ep", "tp", None),
    )
    out_specs = P(("groups", "ep", "tp"), None)
    return jax.shard_map(
        on_device, mesh=mesh, in_specs=in_specs, out_specs=out_specs, check_vma=False
    )
```

time: 205 us -> 197 us (0.961)
  blocking collectives: 149 us -> 108 us
  starting transfers between devices: 23.9 us -> 54.7 us
  local copies, waits for them, and re-layouts: 6.77 us -> 3.81 us
  waiting for transfers between devices: 14.2 us -> 16.8 us
    all_to_all x3 -> x2, blocking collectives: 82.4 us -> 41.4 us  [the longest x1 29 us: on_device(): back = lax.all_to_all(spread(plan, take_out, *sums), 'ep', 0, 0, tiled=True)]
    ppermute x7 -> x16, starting transfers between devices: 23.9 us -> 54.7 us  [swap(): return [lax.ppermute(x, 'tp', p) for x, p in zip(arrays, pairs)]]
    pallas_call x5 -> x7, Pallas kernels: 9.45 us -> 12.9 us  [call(): pl.pallas_call(kernel, out_shape=out, in_specs=specs, out_specs=jax.tree....]
    unnamed x15 -> x16, local copies, waits for them, and re-layouts: 6.77 us -> 3.81 us
    ppermute x7 -> x16, waiting for transfers between devices: 14.2 us -> 16.8 us  [swap(): return [lax.ppermute(x, 'tp', p) for x, p in zip(arrays, pairs)]]
  transfers between devices with their start and end apart: 7 -> 16, of which waited for: 4 -> 9; matrix products, arithmetic and copies ran while one was open for 0% -> 0% of each run, Pallas kernels for 0% -> 2%
where the time goes in v2:
time: 197 us
  blocking collectives  108 us (55%)
  starting transfers between devices  54.7 us (28%)
  waiting for transfers between devices  16.8 us (9%)
  Pallas kernels  12.9 us (7%)
  local copies, waits for them, and re-layouts  3.81 us (2%)
    all_to_all x1, blocking collectives, on_device(): received = lax.all_to_all(outgoing, 'ep', 0, 0, tiled=True)  66.2 us
    ppermute x16, starting transfers between devices, swap(): return [lax.ppermute(x, 'tp', p) for x, p in zip(arrays, pairs)]  54.7 us
    all_to_all x1, blocking collectives, on_device(): back = lax.all_to_all(spread(plan, take_out, *sums), 'ep', 0, 0, tiled=True)  29 us
    ppermute x16, waiting for transfers between devices, swap(): return [lax.ppermute(x, 'tp', p) for x, p in zip(arrays, pairs)]  16.8 us
    pallas_call x7, Pallas kernels, call(): pl.pallas_call(kernel, out_shape=out, in_specs=specs, out_specs=jax.tree....  12.9 us
    all_to_all x1, blocking collectives, on_device(): lax.all_to_all(combine(plan, take_in, back), 'tp', 0, 0, tiled=True)  12.4 us
  transfers between devices with their start and end apart: 16, of which 9 were waited for; matrix products, arithmetic and copies ran while one was open for 0% of the time, Pallas kernels for 2%

profile of v2, /device:TPU:80, one launch (start us, length us, event | category | flops | bytes accessed | tf_op | source)
XLA Modules:
  0.0 196.6 jit_solution(5188955865655660421)
XLA Ops:
  5.0 66.2 %all_to_all.15.refs_3_.refs_1_ = bf16[32,32,128]{2,1,0:T(8,128)(2,1)S(1)} all-to-all(bf16[32,32,128]{2,1,0:T(8,128)(2,1)S(1)} %pack.1), channel_id=1, replica_groups=mesh['groups'=2,'ep'=32,'tp'=8] {'ep'}, dimensions={0} | all-to-all | bytes 524288 | tf_op jit(solution)/shard_map/all_to_all | solution.py:490
  72.5 3.6 %collective-permute-start = (bf16[400,128]{1,0:T(8,128)(2,1)S(1)}, bf16[400,128]{1,0:T(8,128)(2,1)S(1)}, u32[]{:S(2)}, u32[]{:S(2)}) collective-permute-start(bf16[400,128]{1,0:T(8,128)(2,1)S(1)} %get-tuple-element.22.refs_1_), channel_id=1, source_target_pairs={{0,1},{1,0},{2,3},{3,2},{4,5},{5,4},{6,7},{7,6},{8,9},{9,8},{10,11... | collective-permute-start | bytes 307208 | tf_op jit(solution)/shard_map/ppermute | solution.py:442
  76.1 5.4 %collective-permute-start.4 = (bf16[400,128]{1,0:T(8,128)(2,1)S(1)}, bf16[400,128]{1,0:T(8,128)(2,1)S(1)}, u32[]{:S(2)}, u32[]{:S(2)}) collective-permute-start(bf16[400,128]{1,0:T(8,128)(2,1)S(1)} %get-tuple-element.23.refs_6_), channel_id=1, source_target_pairs={{0,7},{1,2},{2,1},{3,4},{4,3},{5,6},{6,5},{7,0},{8,15},{9,10},{10,... | collective-permute-start | bytes 307208 | tf_op jit(solution)/shard_map/ppermute | solution.py:442
  81.5 3.4 %collective-permute-start.1 = (bf16[800,128]{1,0:T(8,128)(2,1)S(1)}, bf16[800,128]{1,0:T(8,128)(2,1)S(1)}, u32[]{:S(2)}, u32[]{:S(2)}) collective-permute-start(bf16[800,128]{1,0:T(8,128)(2,1)S(1)} %pad_maximum_fusion), channel_id=1, source_target_pairs={{0,7},{1,2},{2,1},{3,4},{4,3},{5,6},{6,5},{7,0},{8,15},{9,10},{10,... | collective-permute-start | bytes 614408 | tf_op jit(solution)/shard_map/ppermute | solution.py:442
  85.0 2.2 %collective-permute-start.5 = (bf16[800,128]{1,0:T(8,128)(2,1)S(1)}, bf16[800,128]{1,0:T(8,128)(2,1)S(1)}, u32[]{:S(2)}, u32[]{:S(2)}) collective-permute-start(bf16[800,128]{1,0:T(8,128)(2,1)S(1)} %pad_maximum_fusion.1), channel_id=1, source_target_pairs={{0,1},{1,0},{2,3},{3,2},{4,5},{5,4},{6,7},{7,6},{8,9},{9,8},{10,11... | collective-permute-start | bytes 614408 | tf_op jit(solution)/shard_map/ppermute | solution.py:442
  87.2 3.8 %collective-permute-done.1.refs_3_ = bf16[800,128]{1,0:T(8,128)(2,1)S(1)} collective-permute-done((bf16[800,128]{1,0:T(8,128)(2,1)S(1)}, bf16[800,128]{1,0:T(8,128)(2,1)S(1)}, u32[]{:S(2)}, u32[]{:S(2)}) %collective-permute-start.1) | collective-permute-done | bytes 204832 | tf_op jit(solution)/shard_map/ppermute | solution.py:442
  91.0 1.9 collective-permute-start.2
  93.0 4.8 %collective-permute-start.6 = (bf16[800,128]{1,0:T(8,128)(2,1)S(1)}, bf16[800,128]{1,0:T(8,128)(2,1)S(1)}, u32[]{:S(2)}, u32[]{:S(2)}) collective-permute-start(bf16[800,128]{1,0:T(8,128)(2,1)S(1)} %collective-permute-done.5.refs_8_), channel_id=1, source_target_pairs={{0,7},{1,2},{2,1},{3,4},{4,3},{5,6},{6,5},{7,0},{8,15},{9,10},{10,... | collective-permute-start | bytes 614408 | tf_op jit(solution)/shard_map/ppermute | solution.py:442
  98.7 3.1 %collective-permute-start.3 = (bf16[800,128]{1,0:T(8,128)(2,1)S(1)}, bf16[800,128]{1,0:T(8,128)(2,1)S(1)}, u32[]{:S(2)}, u32[]{:S(2)}) collective-permute-start(bf16[800,128]{1,0:T(8,128)(2,1)S(1)} %collective-permute-done.2.refs_4_), channel_id=1, source_target_pairs={{0,7},{1,2},{2,1},{3,4},{4,3},{5,6},{6,5},{7,0},{8,15},{9,10},{10,... | collective-permute-start | bytes 614408 | tf_op jit(solution)/shard_map/ppermute | solution.py:442
  102.7 3.4 %collective-permute-start.7 = (bf16[800,128]{1,0:T(8,128)(2,1)S(1)}, bf16[800,128]{1,0:T(8,128)(2,1)S(1)}, u32[]{:S(2)}, u32[]{:S(2)}) collective-permute-start(bf16[800,128]{1,0:T(8,128)(2,1)S(1)} %collective-permute-done.6.refs_9_), channel_id=1, source_target_pairs={{0,1},{1,0},{2,3},{3,2},{4,5},{5,4},{6,7},{7,6},{8,9},{9,8},{10,11... | collective-permute-start | bytes 614408 | tf_op jit(solution)/shard_map/ppermute | solution.py:442
  106.1 4.4 %tables.1 = (f32[320,256]{1,0:T(8,128)S(1)}, bf16[1024,896]{1,0:T(8,128)(2,1)S(1)}, bf16[128,3072]{1,0:T(8,128)(2,1)S(1)}) custom-call(s32[2]{0:T(128)S(1)} %pad_add_fusion.refs_0_, s32[16]{0:T(128)S(1)} %copy-done.7, s32[3,128]{1,0:T(4,128)S(1)} %bitcast.14, bf16[32,32,128]{2,1,0:T(8,128)(2,1)S(1)} %all_to_all.15.refs_3_.refs_1_), custom_call_target="tpu_custom_call" | custom-call | flops 1073741824 | bytes 1048576 | tf_op jit(solution)/shard_map/tables/pallas_call | solution.py:309
  110.6 4.4 %experts.1 = (bf16[800,128]{1,0:T(8,128)(2,1)S(1)}, bf16[800,128]{1,0:T(8,128)(2,1)S(1)}, bf16[800,128]{1,0:T(8,128)(2,1)S(1)}, bf16[800,128]{1,0:T(8,128)(2,1)S...) custom-call(s32[2]{0:T(128)S(1)} %pad_add_fusion.refs_0_, ...), custom_call_target="tpu_custom_call" | custom-call | tf_op jit(solution)/shard_map/experts/pallas_call | solution.py:309
  115.0 5.4 %collective-permute-start.8 = (bf16[800,128]{1,0:T(8,128)(2,1)S(1)}, bf16[800,128]{1,0:T(8,128)(2,1)S(1)}, u32[]{:S(2)}, u32[]{:S(2)}) collective-permute-start(bf16[800,128]{1,0:T(8,128)(2,1)S(1)} %get-tuple-element.28), channel_id=1, source_target_pairs={{0,7},{1,2},{2,1},{3,4},{4,3},{5,6},{6,5},{7,0},{8,15},{9,10},{10,... | collective-permute-start | bytes 614408 | tf_op jit(solution)/shard_map/ppermute | solution.py:442
  120.4 2.0 collective-permute-start.12
  124.2 2.2 %collective-permute-start.9 = (bf16[800,128]{1,0:T(8,128)(2,1)S(1)}, bf16[800,128]{1,0:T(8,128)(2,1)S(1)}, u32[]{:S(2)}, u32[]{:S(2)}) collective-permute-start(bf16[800,128]{1,0:T(8,128)(2,1)S(1)} %add_convert_fusion.3), channel_id=1, source_target_pairs={{0,1},{1,0},{2,3},{3,2},{4,5},{5,4},{6,7},{7,6},{8,9},{9,8},{10,11... | collective-permute-start | bytes 614408 | tf_op jit(solution)/shard_map/ppermute | solution.py:442
  128.1 3.2 %collective-permute-start.13 = (bf16[800,128]{1,0:T(8,128)(2,1)S(1)}, bf16[800,128]{1,0:T(8,128)(2,1)S(1)}, u32[]{:S(2)}, u32[]{:S(2)}) collective-permute-start(bf16[800,128]{1,0:T(8,128)(2,1)S(1)} %add_convert_fusion.1), channel_id=1, source_target_pairs={{0,7},{1,2},{2,1},{3,4},{4,3},{5,6},{6,5},{7,0},{8,15},{9,10},{10,... | collective-permute-start | bytes 614408 | tf_op jit(solution)/shard_map/ppermute | solution.py:442
  131.9 5.9 %collective-permute-start.10 = (bf16[800,128]{1,0:T(8,128)(2,1)S(1)}, bf16[800,128]{1,0:T(8,128)(2,1)S(1)}, u32[]{:S(2)}, u32[]{:S(2)}) collective-permute-start(bf16[800,128]{1,0:T(8,128)(2,1)S(1)} %add_convert_fusion.2), channel_id=1, source_target_pairs={{0,7},{1,2},{2,1},{3,4},{4,3},{5,6},{6,5},{7,0},{8,15},{9,10},{10,... | collective-permute-start | bytes 614408 | tf_op jit(solution)/shard_map/ppermute | solution.py:442
  137.9 2.0 collective-permute-start.14
  139.9 2.3 %collective-permute-done.10 = bf16[800,128]{1,0:T(8,128)(2,1)S(1)} collective-permute-done((bf16[800,128]{1,0:T(8,128)(2,1)S(1)}, bf16[800,128]{1,0:T(8,128)(2,1)S(1)}, u32[]{:S(2)}, u32[]{:S(2)}) %collective-permute-start.10) | collective-permute-done | bytes 204832 | tf_op jit(solution)/shard_map/ppermute | solution.py:442
  142.3 2.0 collective-permute-start.11
  145.7 4.3 %collective-permute-start.15 = (bf16[400,128]{1,0:T(8,128)(2,1)S(1)}, bf16[400,128]{1,0:T(8,128)(2,1)S(1)}, u32[]{:S(2)}, u32[]{:S(2)}) collective-permute-start(bf16[400,128]{1,0:T(8,128)(2,1)S(1)} %get-tuple-element.35), channel_id=1, source_target_pairs={{0,7},{1,2},{2,1},{3,4},{4,3},{5,6},{6,5},{7,0},{8,15},{9,10},{10,... | collective-permute-start | bytes 307208 | tf_op jit(solution)/shard_map/ppermute | solution.py:442
  149.9 3.5 %collective-permute-done.15.refs_4_ = bf16[400,128]{1,0:T(8,128)(2,1)S(1)} collective-permute-done((bf16[400,128]{1,0:T(8,128)(2,1)S(1)}, bf16[400,128]{1,0:T(8,128)(2,1)S(1)}, u32[]{:S(2)}, u32[]{:S(2)}) %collective-permute-start.15) | collective-permute-done | bytes 102432 | tf_op jit(solution)/shard_map/ppermute | solution.py:442
  154.2 29.0 %all_to_all.16.refs_1_ = bf16[32,32,128]{2,1,0:T(8,128)(2,1)S(1)} all-to-all(bf16[32,32,128]{2,1,0:T(8,128)(2,1)S(1)} %spread.1), channel_id=1, replica_groups=mesh['groups'=2,'ep'=32,'tp'=8] {'ep'}, dimensions={0} | all-to-all | bytes 524288 | tf_op jit(solution)/shard_map/all_to_all | solution.py:496
  183.5 12.4 %all_to_all.17.refs_0_ = bf16[8,48,128]{2,1,0:T(8,128)(2,1)S(1)} all-to-all(bf16[8,48,128]{2,1,0:T(8,128)(2,1)S(1)} %combine.1), channel_id=1, replica_groups=mesh['groups'=2,'ep'=32,'tp'=8] {'tp'}, dimensions={0} | all-to-all | bytes 196608 | tf_op jit(solution)/shard_map/all_to_all | solution.py:497
  (43 shorter events, 15.5 us)
Async XLA Ops:
  0.1 1.1 copy-start.3
  1.2 0.7 copy-start.4
  1.9 0.7 copy-start.5
  2.5 0.7 copy-start.6
  3.2 0.7 copy-start.7
  72.5 9.0 %collective-permute-start = (bf16[400,128]{1,0:T(8,128)(2,1)S(1)}, bf16[400,128]{1,0:T(8,128)(2,1)S(1)}, u32[]{:S(2)}, u32[]{:S(2)}) collective-permute-start(bf16[400,128]{1,0:T(8,128)(2,1)S(1)} %get-tuple-element.22.refs_1_), channel_id=1, source_target_pairs={{0,1},{1,0},{2,3},{3,2},{4,5},{5,4},{6,7},{7,6},{8,9},{9,8},{10,11... | collective-permute-start | bytes 307208 | tf_op jit(solution)/shard_map/ppermute | solution.py:442
  76.1 8.8 %collective-permute-start.4 = (bf16[400,128]{1,0:T(8,128)(2,1)S(1)}, bf16[400,128]{1,0:T(8,128)(2,1)S(1)}, u32[]{:S(2)}, u32[]{:S(2)}) collective-permute-start(bf16[400,128]{1,0:T(8,128)(2,1)S(1)} %get-tuple-element.23.refs_6_), channel_id=1, source_target_pairs={{0,7},{1,2},{2,1},{3,4},{4,3},{5,6},{6,5},{7,0},{8,15},{9,10},{10,... | collective-permute-start | bytes 307208 | tf_op jit(solution)/shard_map/ppermute | solution.py:442
  81.5 9.5 %collective-permute-start.1 = (bf16[800,128]{1,0:T(8,128)(2,1)S(1)}, bf16[800,128]{1,0:T(8,128)(2,1)S(1)}, u32[]{:S(2)}, u32[]{:S(2)}) collective-permute-start(bf16[800,128]{1,0:T(8,128)(2,1)S(1)} %pad_maximum_fusion), channel_id=1, source_target_pairs={{0,7},{1,2},{2,1},{3,4},{4,3},{5,6},{6,5},{7,0},{8,15},{9,10},{10,... | collective-permute-start | bytes 614408 | tf_op jit(solution)/shard_map/ppermute | solution.py:442
  85.0 25.7 %copy-start = (bf16[2,128,2560]{2,1,0:T(8,128)(2,1)S(1)}, bf16[2,128,2560]{2,1,0:T(8,128)(2,1)}, u32[]{:S(2)}) copy-start(bf16[2,128,2560]{2,1,0:T(8,128)(2,1)} %param.13) | copy-start | bytes 3932164
  85.0 25.6 %copy-start.1 = (bf16[2,128,2560]{2,1,0:T(8,128)(2,1)S(1)}, bf16[2,128,2560]{2,1,0:T(8,128)(2,1)}, u32[]{:S(2)}) copy-start(bf16[2,128,2560]{2,1,0:T(8,128)(2,1)} %param.14) | copy-start | bytes 3932164
  85.0 25.6 %copy-start.2 = (bf16[2,128,2560]{2,1,0:T(8,128)(2,1)S(1)}, bf16[2,128,2560]{2,1,0:T(8,128)(2,1)}, u32[]{:S(2)}) copy-start(bf16[2,128,2560]{2,1,0:T(8,128)(2,1)} %param.15) | copy-start | bytes 3932164
  85.0 8.0 %collective-permute-start.5 = (bf16[800,128]{1,0:T(8,128)(2,1)S(1)}, bf16[800,128]{1,0:T(8,128)(2,1)S(1)}, u32[]{:S(2)}, u32[]{:S(2)}) collective-permute-start(bf16[800,128]{1,0:T(8,128)(2,1)S(1)} %pad_maximum_fusion.1), channel_id=1, source_target_pairs={{0,1},{1,0},{2,3},{3,2},{4,5},{5,4},{6,7},{7,6},{8,9},{9,8},{10,11... | collective-permute-start | bytes 614408 | tf_op jit(solution)/shard_map/ppermute | solution.py:442
  91.0 7.7 %collective-permute-start.2 = (bf16[800,128]{1,0:T(8,128)(2,1)S(1)}, bf16[800,128]{1,0:T(8,128)(2,1)S(1)}, u32[]{:S(2)}, u32[]{:S(2)}) collective-permute-start(bf16[800,128]{1,0:T(8,128)(2,1)S(1)} %collective-permute-done.1.refs_3_), channel_id=1, source_target_pairs={{0,1},{1,0},{2,3},{3,2},{4,5},{5,4},{6,7},{7,6},{8,9},{9,8},{10,11... | collective-permute-start | bytes 614408 | tf_op jit(solution)/shard_map/ppermute | solution.py:442
  93.0 9.7 %collective-permute-start.6 = (bf16[800,128]{1,0:T(8,128)(2,1)S(1)}, bf16[800,128]{1,0:T(8,128)(2,1)S(1)}, u32[]{:S(2)}, u32[]{:S(2)}) collective-permute-start(bf16[800,128]{1,0:T(8,128)(2,1)S(1)} %collective-permute-done.5.refs_8_), channel_id=1, source_target_pairs={{0,7},{1,2},{2,1},{3,4},{4,3},{5,6},{6,5},{7,0},{8,15},{9,10},{10,... | collective-permute-start | bytes 614408 | tf_op jit(solution)/shard_map/ppermute | solution.py:442
  98.7 11.9 %collective-permute-start.3 = (bf16[800,128]{1,0:T(8,128)(2,1)S(1)}, bf16[800,128]{1,0:T(8,128)(2,1)S(1)}, u32[]{:S(2)}, u32[]{:S(2)}) collective-permute-start(bf16[800,128]{1,0:T(8,128)(2,1)S(1)} %collective-permute-done.2.refs_4_), channel_id=1, source_target_pairs={{0,7},{1,2},{2,1},{3,4},{4,3},{5,6},{6,5},{7,0},{8,15},{9,10},{10,... | collective-permute-start | bytes 614408 | tf_op jit(solution)/shard_map/ppermute | solution.py:442
  102.7 7.9 %collective-permute-start.7 = (bf16[800,128]{1,0:T(8,128)(2,1)S(1)}, bf16[800,128]{1,0:T(8,128)(2,1)S(1)}, u32[]{:S(2)}, u32[]{:S(2)}) collective-permute-start(bf16[800,128]{1,0:T(8,128)(2,1)S(1)} %collective-permute-done.6.refs_9_), channel_id=1, source_target_pairs={{0,1},{1,0},{2,3},{3,2},{4,5},{5,4},{6,7},{7,6},{8,9},{9,8},{10,11... | collective-permute-start | bytes 614408 | tf_op jit(solution)/shard_map/ppermute | solution.py:442
  115.0 9.1 %collective-permute-start.8 = (bf16[800,128]{1,0:T(8,128)(2,1)S(1)}, bf16[800,128]{1,0:T(8,128)(2,1)S(1)}, u32[]{:S(2)}, u32[]{:S(2)}) collective-permute-start(bf16[800,128]{1,0:T(8,128)(2,1)S(1)} %get-tuple-element.28), channel_id=1, source_target_pairs={{0,7},{1,2},{2,1},{3,4},{4,3},{5,6},{6,5},{7,0},{8,15},{9,10},{10,... | collective-permute-start | bytes 614408 | tf_op jit(solution)/shard_map/ppermute | solution.py:442
  120.4 7.7 %collective-permute-start.12 = (bf16[800,128]{1,0:T(8,128)(2,1)S(1)}, bf16[800,128]{1,0:T(8,128)(2,1)S(1)}, u32[]{:S(2)}, u32[]{:S(2)}) collective-permute-start(bf16[800,128]{1,0:T(8,128)(2,1)S(1)} %get-tuple-element.33), channel_id=1, source_target_pairs={{0,1},{1,0},{2,3},{3,2},{4,5},{5,4},{6,7},{7,6},{8,9},{9,8},{10,11... | collective-permute-start | bytes 614408 | tf_op jit(solution)/shard_map/ppermute | solution.py:442
  124.2 7.7 %collective-permute-start.9 = (bf16[800,128]{1,0:T(8,128)(2,1)S(1)}, bf16[800,128]{1,0:T(8,128)(2,1)S(1)}, u32[]{:S(2)}, u32[]{:S(2)}) collective-permute-start(bf16[800,128]{1,0:T(8,128)(2,1)S(1)} %add_convert_fusion.3), channel_id=1, source_target_pairs={{0,1},{1,0},{2,3},{3,2},{4,5},{5,4},{6,7},{7,6},{8,9},{9,8},{10,11... | collective-permute-start | bytes 614408 | tf_op jit(solution)/shard_map/ppermute | solution.py:442
  128.1 9.7 %collective-permute-start.13 = (bf16[800,128]{1,0:T(8,128)(2,1)S(1)}, bf16[800,128]{1,0:T(8,128)(2,1)S(1)}, u32[]{:S(2)}, u32[]{:S(2)}) collective-permute-start(bf16[800,128]{1,0:T(8,128)(2,1)S(1)} %add_convert_fusion.1), channel_id=1, source_target_pairs={{0,7},{1,2},{2,1},{3,4},{4,3},{5,6},{6,5},{7,0},{8,15},{9,10},{10,... | collective-permute-start | bytes 614408 | tf_op jit(solution)/shard_map/ppermute | solution.py:442
  131.9 10.3 %collective-permute-start.10 = (bf16[800,128]{1,0:T(8,128)(2,1)S(1)}, bf16[800,128]{1,0:T(8,128)(2,1)S(1)}, u32[]{:S(2)}, u32[]{:S(2)}) collective-permute-start(bf16[800,128]{1,0:T(8,128)(2,1)S(1)} %add_convert_fusion.2), channel_id=1, source_target_pairs={{0,7},{1,2},{2,1},{3,4},{4,3},{5,6},{6,5},{7,0},{8,15},{9,10},{10,... | collective-permute-start | bytes 614408 | tf_op jit(solution)/shard_map/ppermute | solution.py:442
  137.9 7.7 %collective-permute-start.14 = (bf16[800,128]{1,0:T(8,128)(2,1)S(1)}, bf16[800,128]{1,0:T(8,128)(2,1)S(1)}, u32[]{:S(2)}, u32[]{:S(2)}) collective-permute-start(bf16[800,128]{1,0:T(8,128)(2,1)S(1)} %add_convert_fusion), channel_id=1, source_target_pairs={{0,1},{1,0},{2,3},{3,2},{4,5},{5,4},{6,7},{7,6},{8,9},{9,8},{10,11... | collective-permute-start | bytes 614408 | tf_op jit(solution)/shard_map/ppermute | solution.py:442
  142.3 7.7 %collective-permute-start.11 = (bf16[400,128]{1,0:T(8,128)(2,1)S(1)}, bf16[400,128]{1,0:T(8,128)(2,1)S(1)}, u32[]{:S(2)}, u32[]{:S(2)}) collective-permute-start(bf16[400,128]{1,0:T(8,128)(2,1)S(1)} %get-tuple-element.37), channel_id=1, source_target_pairs={{0,1},{1,0},{2,3},{3,2},{4,5},{5,4},{6,7},{7,6},{8,9},{9,8},{10,11... | collective-permute-start | bytes 307208 | tf_op jit(solution)/shard_map/ppermute | solution.py:442
  145.7 7.8 %collective-permute-start.15 = (bf16[400,128]{1,0:T(8,128)(2,1)S(1)}, bf16[400,128]{1,0:T(8,128)(2,1)S(1)}, u32[]{:S(2)}, u32[]{:S(2)}) collective-permute-start(bf16[400,128]{1,0:T(8,128)(2,1)S(1)} %get-tuple-element.35), channel_id=1, source_target_pairs={{0,7},{1,2},{2,1},{3,4},{4,3},{5,6},{6,5},{7,0},{8,15},{9,10},{10,... | collective-permute-start | bytes 307208 | tf_op jit(solution)/shard_map/ppermute | solution.py:442

commit v3 on v2

v3 whole, which is shorter than its diff:
```python
import jax
import jax.numpy as jnp
from jax import lax
from jax.experimental import pallas as pl
from jax.experimental.pallas import tpu as pltpu
from jax.sharding import PartitionSpec as P

TOPK = 6
DEV_TOP = 3
DEC_RANK = 8
USUAL_DECODE = 32
LANE = 128
F32, BF16, I32 = jnp.float32, jnp.bfloat16, jnp.int32
INTERPRET = False


class Plan:
    def __init__(self, ranks, lanes, rows, width, prefill, decode):
        self.ranks, self.lanes, self.rows, self.width = ranks, lanes, rows, width
        self.cap = (DEV_TOP * rows + ranks - 1) // ranks
        self.prefill, self.decode = prefill, decode
        self.half_pre = self.cap // 2
        self.half_dec = DEC_RANK // 2
        self.half = prefill * self.half_pre + decode // 2
        self.slots = 2 * self.half
        self.packed = 5 * self.half
        self.packed_up = -(-self.packed // LANE) * LANE
        self.side = self.packed // 2
        self.step = next(n for n in range(200, 0, -8) if self.side % n == 0)
        self.chunk = 2 * self.cap + self.half_pre + 2
        self.own_rows = rows // lanes
        assert width == (2 * lanes + lanes // 2) * LANE and self.chunk % 8 == 0
        assert rows == LANE and self.half_dec <= self.cap - DEC_RANK and ranks <= LANE


def iota(shape, dim):
    return lax.broadcasted_iota(I32, shape, dim)


def one_hot(mask):
    return jnp.where(mask, 1.0, 0.0).astype(BF16)


def dot(a, b):
    return jnp.dot(a, b, preferred_element_type=F32)


def is_prefill(info_ref, plan, own):
    found = info_ref[2] == own
    for i in range(1, plan.prefill):
        found = found | (info_ref[2 + i] == own)
    return found


def earlier(plan):
    shape = (plan.rows, plan.rows)
    return one_hot(iota(shape, 0) < iota(shape, 1))


def chunk_index(j, plan, parity, full):
    cap = plan.cap
    spill = (j >= DEC_RANK) & (j < cap) & jnp.logical_not(full)
    last = j >= 2 * cap
    block = jnp.where(last | spill, 2, jnp.where(j < cap, 0, 1))
    start = jnp.where(full, parity * plan.half_pre, 0)
    slot = jnp.where(
        spill, j - DEC_RANK + plan.half_dec, jnp.where(last, j - 2 * cap + start, j - block * cap)
    )
    kept = jnp.logical_not(last) | (j - 2 * cap < jnp.where(full, plan.half_pre, plan.half_dec))
    return jnp.where(kept, block, 3), slot


def named_ranks(plan, full, routes_ref):
    shape = (plan.ranks, plan.rows)
    live = iota(shape, 1) < jnp.where(full, plan.rows, DEC_RANK)
    rank = iota(shape, 0)
    hits = [(routes_ref[k : k + 1, :].astype(I32) == rank) & live for k in range(DEV_TOP)]
    named = sum(jnp.where(hit, 1.0, 0.0) for hit in hits)
    return hits, named, places(plan, named)


def places(plan, named):
    before = dot(named.astype(BF16), earlier(plan))
    return jnp.where(named > 0.5, before, -1.0)


def pack_kernel(plan, info_ref, routes_ref, tok_ref, out_ref, x_ref, sems):
    lane, own = info_ref[0], info_ref[1]
    first_at = pl.multiple_of(lane * (2 * LANE), LANE)
    tail_at = pl.multiple_of((2 * plan.lanes + lane // 2) * LANE, LANE)
    copies = [
        pltpu.make_async_copy(
            tok_ref.at[:, pl.ds(first_at, 2 * LANE)], x_ref.at[:, 0 : 2 * LANE], sems.at[0]
        ),
        pltpu.make_async_copy(
            tok_ref.at[:, pl.ds(tail_at, LANE)], x_ref.at[:, 2 * LANE : 3 * LANE], sems.at[1]
        ),
    ]
    for copy in copies:
        copy.start()
    full = is_prefill(info_ref, plan, own)
    hits, named, place = named_ranks(plan, full, routes_ref)
    weights = []
    for e in range(2):
        total = jnp.zeros(named.shape, F32)
        for k, hit in enumerate(hits):
            for j in (2 * k, 2 * k + 1):
                at = DEV_TOP + j
                chosen = hit & (routes_ref[at : at + 1, :] == float(e))
                at += TOPK
                total += jnp.where(chosen, routes_ref[at : at + 1, :], 0.0)
        weights.append(total)
    full_shape = (plan.ranks, plan.chunk, LANE)
    flat = plan.ranks * plan.chunk
    j = iota(full_shape, 1)
    block, slot = chunk_index(j, plan, lane % 2, full)
    match = place.astype(I32)[:, None, :] == slot
    picks = [one_hot(match & (block == b)).reshape(flat, LANE) for b in range(3)]
    for copy in copies:
        copy.wait()
    total = sum(dot(picks[b], x_ref[:, b * LANE : (b + 1) * LANE]) for b in range(3))
    total = total.reshape(full_shape)
    total = jnp.where(j == plan.chunk - 2, weights[0][:, None, :], total)
    total = jnp.where(j == plan.chunk - 1, weights[1][:, None, :], total)
    out_ref[...] = total.astype(BF16)


def weight_rows(plan, data):
    shape = (plan.ranks, plan.ranks * plan.chunk)
    at = iota(shape, 0) * plan.chunk + plan.chunk - 2
    return [dot(one_hot(iota(shape, 1) == at + e), data) for e in range(2)]


def target_row(info_ref, plan, named):
    lane = info_ref[0]
    ranks, total = plan.ranks, plan.ranks * plan.chunk
    rank = iota((8, ranks), 1)
    fulls = jnp.zeros((8, ranks), I32)
    for i in range(plan.prefill):
        fulls += jnp.where(rank == info_ref[2 + i], 1, 0)
    ones = jnp.full((8, plan.rows), 1.0, BF16)
    counts = lax.dot_general(
        ones, named.astype(BF16), (((1,), (1,)), ((), ())), preferred_element_type=F32
    )
    decode = jnp.where(fulls > 0, 0.0, counts).astype(BF16)
    full = jnp.where(fulls > 0, 1.0, 0.0).astype(BF16)
    spread = (ranks, total)
    source = iota(spread, 1) // plan.chunk
    below = one_hot(iota(spread, 0) < source)
    here = one_hot(iota(spread, 0) == source)
    base = dot(decode, below).astype(I32)
    held = dot(decode, here).astype(I32)
    index = dot(full, below).astype(I32)
    full = dot(full, here) > 0.5
    needed = jnp.sum(decode.astype(F32), axis=1, keepdims=True)
    j = iota((8, total), 1) % plan.chunk
    block, slot = chunk_index(j, plan, lane % 2, full)
    half_rows = plan.decode // 2
    place = base + slot
    second = jnp.where(jnp.where(full, slot - plan.half_pre, place - half_rows) >= 0, 1, 0)
    row = jnp.where(
        full,
        index * plan.half_pre + slot - second * plan.half_pre,
        plan.prefill * plan.half_pre + place - second * half_rows,
    )
    kept = full | ((slot < held) & (place < plan.decode) & ((block < 2) | (second == lane % 2)))
    piece = jnp.where(block == 2, 4, 2 * block + second)
    return jnp.where(kept & (block < 3), piece * plan.half + row, -1), needed


def compact_kernel(plan, info_ref, in_ref, a_ref, b_ref, target_ref, needed_ref):
    total = plan.ranks * plan.chunk
    data = in_ref[...].reshape(total, LANE)
    first = weight_rows(plan, data)[0]
    named = jnp.where(first > 0.0, 1.0, 0.0)
    target, needed = target_row(info_ref, plan, named)
    target_ref[...] = target
    needed_ref[...] = jnp.broadcast_to(needed, (8, LANE))
    side = plan.side
    for ref, begin in ((a_ref, 0), (b_ref, side)):
        for at in range(0, side, plan.step):
            shape = (plan.step, total)
            take = one_hot(iota(shape, 0) + (begin + at) == target[0:1, :])
            ref[at : at + plan.step, :] = dot(take, data).astype(BF16)


def weights_kernel(plan, in_ref, target_ref, weight_ref):
    total = plan.ranks * plan.chunk
    data = in_ref[...].reshape(total, LANE)
    first, second = weight_rows(plan, data)
    place = places(plan, jnp.where(first > 0.0, 1.0, 0.0)).astype(I32)
    full_shape = (plan.ranks, plan.chunk, LANE)
    j = iota(full_shape, 1)
    match = (place[:, None, :] == j) & (j < plan.cap)
    target = target_ref[0:1, :]
    wide = []
    for value in (first, second):
        kept = jnp.where(match, value[:, None, :], 0.0)
        column = jnp.sum(kept, axis=2, keepdims=True)
        wide.append(jnp.broadcast_to(column, full_shape).reshape(total, LANE).astype(BF16))
    for piece in range(2):
        at = piece * plan.half
        take = one_hot(iota((plan.half, total), 0) + at == target)
        for e in range(2):
            weight_ref[at : at + plan.half, e * LANE : (e + 1) * LANE] = dot(take, wide[e])


def spread_table_kernel(plan, target_ref, spread_ref):
    total = plan.ranks * plan.chunk
    col = iota((LANE, LANE), 1)
    for g in range(0, total, LANE):
        wide = jnp.broadcast_to(target_ref[0:1, g : g + LANE], (LANE, LANE))
        column = wide.astype(F32).T.astype(I32)
        for at in range(0, plan.packed_up, LANE):
            spread_ref[g : g + LANE, at : at + LANE] = one_hot(col + at == column)


def combine_table_kernel(plan, info_ref, routes_ref, combine_ref):
    lane, own = info_ref[0], info_ref[1]
    ranks, rows = plan.ranks, plan.rows
    total = ranks * plan.chunk
    full = is_prefill(info_ref, plan, own)
    _, _, place = named_ranks(plan, full, routes_ref)
    square = jnp.concatenate([place, jnp.zeros((rows - ranks, rows), F32)], axis=0)
    turned = square.T[:, :ranks].astype(BF16)
    spread = (ranks, total)
    expand = one_hot(iota(spread, 1) // plan.chunk == iota(spread, 0))
    spots = dot(turned, expand).astype(I32)
    j = iota((1, total), 1) % plan.chunk
    block, slot = chunk_index(j, plan, lane % 2, full)
    match = spots == slot
    for b in range(3):
        combine_ref[:, b * total : (b + 1) * total] = one_hot(match & (block == b))


def lane_at(plan, me, sign, steps):
    return lax.rem(me + sign * steps + plan.lanes, plan.lanes)


def expert_kernel(plan, info_ref, *refs):
    n = len(GATHERED)
    a_refs, b_refs = refs[:n], refs[n : 2 * n]
    weight_ref, wg, wu, wd = refs[2 * n : 2 * n + 4]
    outs = refs[2 * n + 4 : -2]
    x_ref, h_ref = refs[-2:]
    me = info_ref[0]
    sign = 1 - 2 * lax.rem(me, 2)
    lanes, half, slots, side = plan.lanes, plan.half, plan.slots, plan.side
    over = side - slots

    def columns(lane):
        first = pl.multiple_of(lane * (2 * LANE), LANE)
        tail = pl.multiple_of((2 * lanes + lane // 2) * LANE, LANE)
        start = pl.multiple_of(lax.rem(lane, 2) * half, 8)
        return (
            pl.ds(first, LANE),
            pl.ds(pl.multiple_of(first + LANE, LANE), LANE),
            pl.ds(tail, LANE),
            pl.ds(start, half),
        )

    for refs_of, turn in ((a_refs, sign), (b_refs, -sign)):
        for ref, steps in zip(refs_of, GATHERED):
            for i, step in enumerate(steps):
                first, second, tail, rows = columns(lane_at(plan, me, turn, step))
                at = i * side
                if refs_of is a_refs:
                    x_ref[:, first] = ref[at : at + slots, :]
                    x_ref[0:over, second] = ref[at + slots : at + side, :]
                else:
                    x_ref[over:slots, second] = ref[at : at + slots - over, :]
                    x_ref[rows, tail] = ref[at + slots - over : at + side, :]
    turned = (((1,), (1,)), ((), ()))
    x = x_ref[...]
    gate = lax.dot_general(x, wg[...], turned, preferred_element_type=F32)
    up = lax.dot_general(x, wu[...], turned, preferred_element_type=F32)
    hidden = gate / (1.0 + jnp.exp(-gate)) * up * weight_ref[...]
    h_ref[...] = hidden.astype(BF16)
    out = 0
    for steps in SCATTERED:
        for turn in (sign, -sign):
            for i, step in enumerate(steps):
                first, second, tail, rows = columns(lane_at(plan, me, turn, step))
                ref, at = outs[out], i * side
                if turn is sign:
                    ref[at : at + slots, :] = dot(h_ref[...], wd[:, first]).astype(BF16)
                    ref[at + slots : at + side, :] = dot(h_ref[0:over, :], wd[:, second]).astype(BF16)
                else:
                    ref[at : at + slots - over, :] = dot(h_ref[over:slots, :], wd[:, second]).astype(BF16)
                    ref[at + slots - over : at + side, :] = dot(h_ref[rows, :], wd[:, tail]).astype(BF16)
            out += 1


def spread_kernel(plan, take_ref, needed_ref, own_a, got_a, own_b, got_b, out_ref, sum_ref):
    side = plan.side
    sum_ref[0:side, :] = (own_a[...].astype(F32) + got_a[...].astype(F32)).astype(BF16)
    sum_ref[side : 2 * side, :] = (own_b[...].astype(F32) + got_b[...].astype(F32)).astype(BF16)
    sum_ref[2 * side :, :] = jnp.zeros((plan.packed_up - 2 * side, LANE), BF16)
    shape = (plan.ranks, plan.chunk, LANE)
    spread = dot(take_ref[...], sum_ref[...]).reshape(shape)
    over = jnp.where(needed_ref[0:1, :] > float(plan.decode), 1.0, 0.0)
    spread = jnp.where(iota(shape, 1) == plan.chunk - 1, over[None], spread)
    out_ref[...] = spread.astype(BF16)


def combine_kernel(plan, take_ref, in_ref, out_ref, over_ref):
    total = plan.ranks * plan.chunk
    data = in_ref[...].reshape(total, LANE)
    own_rows = plan.own_rows
    for b in range(3):
        mine = dot(take_ref[:, b * total : (b + 1) * total], data).astype(BF16)
        for to in range(plan.lanes):
            out_ref[to, b * own_rows : (b + 1) * own_rows, :] = mine[
                to * own_rows : (to + 1) * own_rows
            ]
    shape = (8, total)
    flags = one_hot(iota(shape, 1) % plan.chunk == plan.chunk - 1)
    over_ref[...] = dot(flags, data)


def finish_kernel(plan, in_ref, out_ref):
    n = plan.own_rows
    for lane in range(plan.lanes):
        at = lane * 2 * LANE
        out_ref[:, at : at + LANE] = in_ref[lane, 0:n, :]
        out_ref[:, at + LANE : at + 2 * LANE] = in_ref[lane, n : 2 * n, :]
    for pair in range(plan.lanes // 2):
        at = (2 * plan.lanes + pair) * LANE
        first = in_ref[2 * pair, 2 * n : 3 * n, :].astype(F32)
        second = in_ref[2 * pair + 1, 2 * n : 3 * n, :].astype(F32)
        out_ref[:, at : at + LANE] = (first + second).astype(BF16)


SMEM = pl.BlockSpec(memory_space=pltpu.SMEM)
VMEM = pl.BlockSpec(memory_space=pltpu.VMEM)
HBM = pl.BlockSpec(memory_space=pltpu.HBM)
GATHERED = ((0,), (1,), (-1, -2), (2, 3), (-3, -4))
SCATTERED = ((-3, -4), (2, 3), (-1, -2), (0,), (1,))


def call(kernel, name, out, specs, *args, scratch=(), limit=24 << 20, flops=0):
    cost = None
    if flops:
        cost = pl.CostEstimate(flops=flops, bytes_accessed=1 << 20, transcendentals=0)
    return pl.pallas_call(
        kernel,
        out_shape=out,
        in_specs=specs,
        out_specs=jax.tree.map(lambda _: VMEM, out),
        scratch_shapes=scratch,
        compiler_params=pltpu.CompilerParams(vmem_limit_bytes=limit),
        cost_estimate=cost,
        interpret=INTERPRET,
        name=name,
    )(*args)


def pack(plan, info, routes, tokens):
    return call(
        lambda *refs: pack_kernel(plan, *refs),
        "pack",
        jax.ShapeDtypeStruct((plan.ranks, plan.chunk, LANE), BF16),
        [SMEM, VMEM, HBM],
        info,
        routes,
        tokens,
        scratch=[pltpu.VMEM((plan.rows, 3 * LANE), BF16), pltpu.SemaphoreType.DMA((2,))],
    )


def compact(plan, info, received):
    share = jax.ShapeDtypeStruct((plan.side, LANE), BF16)
    return call(
        lambda *refs: compact_kernel(plan, *refs),
        "compact",
        (
            share,
            share,
            jax.ShapeDtypeStruct((8, plan.ranks * plan.chunk), I32),
            jax.ShapeDtypeStruct((8, LANE), F32),
        ),
        [SMEM, VMEM],
        info,
        received,
    )


def weights_table(plan, received, target):
    return call(
        lambda *refs: weights_kernel(plan, *refs),
        "weights",
        jax.ShapeDtypeStruct((plan.slots, 2 * LANE), F32),
        [VMEM, VMEM],
        received,
        target,
        flops=1 << 29,
    )


def spread_table(plan, target):
    return call(
        lambda *refs: spread_table_kernel(plan, *refs),
        "spread_table",
        jax.ShapeDtypeStruct((plan.ranks * plan.chunk, plan.packed_up), BF16),
        [VMEM],
        target,
        flops=1 << 29,
    )


def combine_table(plan, info, routes):
    return call(
        lambda *refs: combine_table_kernel(plan, *refs),
        "combine_table",
        jax.ShapeDtypeStruct((plan.rows, 3 * plan.ranks * plan.chunk), BF16),
        [SMEM, VMEM],
        info,
        routes,
        flops=1 << 29,
    )


def experts(plan, info, a_parts, b_parts, weights, w_gate, w_up, w_down):
    hidden = w_gate.shape[0] * w_gate.shape[1]
    flat = [w.reshape(hidden, plan.width) for w in (w_gate, w_up, w_down)]
    out = []
    for steps in SCATTERED:
        out += [jax.ShapeDtypeStruct((len(steps) * plan.side, LANE), BF16)] * 2
    outs = call(
        lambda *refs: expert_kernel(plan, *refs),
        "experts",
        tuple(out),
        [SMEM] + [VMEM] * (2 * len(a_parts) + 4),
        info,
        *a_parts,
        *b_parts,
        weights,
        *flat,
        scratch=[
            pltpu.VMEM((plan.slots, plan.width), BF16),
            pltpu.VMEM((plan.slots, hidden), BF16),
        ],
        limit=32 << 20,
    )
    return outs[0::2], outs[1::2]


def spread(plan, take, needed, own_a, got_a, own_b, got_b):
    return call(
        lambda *refs: spread_kernel(plan, *refs),
        "spread",
        jax.ShapeDtypeStruct((plan.ranks, plan.chunk, LANE), BF16),
        [VMEM] * 6,
        take,
        needed,
        own_a,
        got_a,
        own_b,
        got_b,
        scratch=[pltpu.VMEM((plan.packed_up, LANE), BF16)],
    )


def combine(plan, take, back):
    return call(
        lambda *refs: combine_kernel(plan, *refs),
        "combine",
        (
            jax.ShapeDtypeStruct((plan.lanes, 3 * plan.own_rows, LANE), BF16),
            jax.ShapeDtypeStruct((8, LANE), F32),
        ),
        [VMEM, VMEM],
        take,
        back,
    )


def finish(plan, shares):
    return call(
        lambda *refs: finish_kernel(plan, *refs),
        "finish",
        jax.ShapeDtypeStruct((plan.own_rows, plan.width), BF16),
        [VMEM],
        shares,
    )


def neighbours(lanes):
    near = [(i, i ^ 1) for i in range(lanes)]
    far = [(i, (i - 1 + 2 * (i % 2)) % lanes) for i in range(lanes)]
    return near, far


def swap(arrays, pairs):
    return [lax.ppermute(x, "tp", p) for x, p in zip(arrays, pairs)]


def gather_lanes(shares, lanes, beside):
    near, far = neighbours(lanes)
    own = list(shares)
    first = swap(own, (near, far))
    held = [jnp.concatenate([x, y]) for x, y in zip(own, first)]
    parts, values = [own, first], []
    for hop in range(lanes // 2 - 1):
        if hop < len(beside):
            held, value = lax.optimization_barrier((held, beside[hop]))
            values.append(value)
        held = swap(held, (far, near) if hop % 2 == 0 else (near, far))
        parts.append(held)
    return [p[0] for p in parts], [p[1] for p in parts], values


def plus(x, y):
    return (x.astype(F32) + y.astype(F32)).astype(BF16)


def reduce_lanes(a_outs, b_outs, side, lanes):
    near, far = neighbours(lanes)
    stages = list(zip(a_outs, b_outs))
    held = list(stages[0])
    for hop in range(lanes // 2 - 2):
        got = swap(held, (far, near) if hop % 2 == 0 else (near, far))
        held = [plus(x, y) for x, y in zip(stages[hop + 1], got)]
    got = swap(held, (far, near))
    away = [plus(x, y[side:]) for x, y in zip(stages[-1], got)]
    home = [plus(x, y[:side]) for x, y in zip(stages[-2], got)]
    last = swap(away, (near, far))
    return home[0], last[0], home[1], last[1]


def through_experts(plan, info, received, take_in, matrices):
    a_share, b_share, target, needed = compact(plan, info, received)
    beside = [weights_table(plan, received, target), spread_table(plan, target), take_in]
    a_parts, b_parts, beside = gather_lanes((a_share, b_share), plan.lanes, beside)
    weights, take_out, take_in = beside
    a_outs, b_outs = experts(plan, info, a_parts, b_parts, weights, *matrices)
    sums = reduce_lanes(a_outs, b_outs, plan.side, plan.lanes)
    back = lax.all_to_all(spread(plan, take_out, needed, *sums), "ep", 0, 0, tiled=True)
    return combine(plan, take_in, back)


def on_device(
    tokens, device_choice, local_expert, route_weight, prefill_ranks, w_gate, w_up, w_down
):
    ranks, prefill = lax.axis_size("ep"), prefill_ranks.shape[0]
    sizes = (ranks, lax.axis_size("tp"), *tokens.shape, prefill)
    most = (ranks - prefill) * DEC_RANK
    plan, whole = Plan(*sizes, min(USUAL_DECODE, most)), Plan(*sizes, most)
    places = jnp.stack([lax.axis_index("tp"), lax.axis_index("ep")]).astype(I32)
    info = jnp.concatenate([places, prefill_ranks])
    routes = jnp.concatenate(
        [device_choice.T.astype(F32), local_expert.T.astype(F32), route_weight.T]
    )
    outgoing = pack(plan, info, routes, tokens)
    received = lax.all_to_all(outgoing, "ep", 0, 0, tiled=True)
    take_in = combine_table(plan, info, routes)
    rest = (info, received, take_in, (w_gate, w_up, w_down))
    shares, over = through_experts(plan, *rest)
    rest, over = lax.optimization_barrier((rest, over))
    shares = lax.cond(
        over[0, 0] > 0.0, lambda: through_experts(whole, *rest)[0], lambda: shares
    )
    shares = lax.all_to_all(shares, "tp", 0, 0, tiled=True)
    return finish(plan, shares)


def solution(mesh):
    in_specs = (
        P(("groups", "ep"), None),
        P(("groups", "ep"), None),
        P(("groups", "ep"), None),
        P(("groups", "ep"), None),
        P("groups"),
        P("ep", "tp", None),
        P("ep", "tp", None),
        P("ep", "tp", None),
    )
    out_specs = P(("groups", "ep", "tp"), None)
    return jax.shard_map(
        on_device, mesh=mesh, in_specs=in_specs, out_specs=out_specs, check_vma=False
    )
```

time: 197 us -> 195 us (0.990)
  waiting for transfers between devices: 16.8 us -> 26.2 us
  starting transfers between devices: 54.7 us -> 48.2 us
  Pallas kernels: 12.9 us -> 8.84 us
  blocking collectives: 108 us -> 105 us
  other arithmetic: 0.46 us -> 3.08 us
  local copies, waits for them, and re-layouts: 3.81 us -> 1.63 us
    ppermute x16, waiting for transfers between devices: 16.8 us -> 26.2 us  [swap(): return [lax.ppermute(x, 'tp', p) for x, p in zip(arrays, pairs)]]
    ppermute x16, starting transfers between devices: 54.7 us -> 48.2 us  [swap(): return [lax.ppermute(x, 'tp', p) for x, p in zip(arrays, pairs)]]
    pallas_call x7 -> x9, Pallas kernels: 12.9 us -> 8.84 us  [call(): pl.pallas_call(kernel, out_shape=out, in_specs=specs, out_specs=jax.tree....]
    unnamed x16 -> x10, local copies, waits for them, and re-layouts: 3.81 us -> 1.11 us
    all_to_all x2, blocking collectives: 41.4 us -> 39.2 us  [the longest x1 25.9 us: through_experts(): lax.all_to_all(spread(plan, take_out, needed, *sums), 'ep', 0, 0, tiled=T...]
  transfers between devices with their start and end apart: 16 -> 16, of which waited for: 9 -> 12; matrix products, arithmetic and copies ran while one was open for 0% -> 0% of each run, Pallas kernels for 2% -> 1%
where the time goes in v3:
time: 195 us
  blocking collectives  105 us (54%)
  starting transfers between devices  48.2 us (25%)
  waiting for transfers between devices  26.2 us (13%)
  Pallas kernels  8.84 us (5%)
  other arithmetic  3.08 us (2%)
    all_to_all x1, blocking collectives, on_device(): received = lax.all_to_all(outgoing, 'ep', 0, 0, tiled=True)  66.2 us
    ppermute x16, starting transfers between devices, swap(): return [lax.ppermute(x, 'tp', p) for x, p in zip(arrays, pairs)]  48.2 us
    ppermute x16, waiting for transfers between devices, swap(): return [lax.ppermute(x, 'tp', p) for x, p in zip(arrays, pairs)]  26.2 us
    all_to_all x1, blocking collectives, through_experts(): lax.all_to_all(spread(plan, take_out, needed, *sums), 'ep', 0, 0, tiled=T...  25.9 us
    all_to_all x1, blocking collectives, on_device(): shares = lax.all_to_all(shares, 'tp', 0, 0, tiled=True)  13.4 us
    pallas_call x9, Pallas kernels, call(): pl.pallas_call(kernel, out_shape=out, in_specs=specs, out_specs=jax.tree....  8.84 us
  transfers between devices with their start and end apart: 16, of which 12 were waited for; matrix products, arithmetic and copies ran while one was open for 0% of the time, Pallas kernels for 1%

profile of v3, /device:TPU:80, one launch (start us, length us, event | category | flops | bytes accessed | tf_op | source)
XLA Modules:
  0.0 194.6 jit_solution(143472831908094826)
XLA Ops:
  5.0 66.2 %all_to_all.20.refs_1_.refs_0_ = bf16[32,32,128]{2,1,0:T(8,128)(2,1)S(1)} all-to-all(bf16[32,32,128]{2,1,0:T(8,128)(2,1)S(1)} %pack.1), channel_id=1, replica_groups=mesh['groups'=2,'ep'=32,'tp'=8] {'ep'}, dimensions={0} | all-to-all | bytes 524288 | tf_op jit(solution)/shard_map/all_to_all | solution.py:555
  72.8 5.8 %collective-permute-start.17 = (bf16[280,128]{1,0:T(8,128)(2,1)S(1)}, bf16[280,128]{1,0:T(8,128)(2,1)S(1)}, u32[]{:S(2)}, u32[]{:S(2)}) collective-permute-start(bf16[280,128]{1,0:T(8,128)(2,1)S(1)} %get-tuple-element.84.refs_6_), channel_id=1, source_target_pairs={{0,7},{1,2},{2,1},{3,4},{4,3},{5,6},{6,5},{7,0},{8,15},{9,10},{10,... | collective-permute-start | bytes 215048 | tf_op jit(solution)/shard_map/ppermute | solution.py:495
  81.4 3.4 %collective-permute-done.16.refs_2_ = bf16[280,128]{1,0:T(8,128)(2,1)S(1)} collective-permute-done((bf16[280,128]{1,0:T(8,128)(2,1)S(1)}, bf16[280,128]{1,0:T(8,128)(2,1)S(1)}, u32[]{:S(2)}, u32[]{:S(2)}) %collective-permute-start.16) | collective-permute-done | bytes 71712 | tf_op jit(solution)/shard_map/ppermute | solution.py:495
  84.8 2.5 %collective-permute-start.18 = (bf16[560,128]{1,0:T(8,128)(2,1)S(1)}, bf16[560,128]{1,0:T(8,128)(2,1)S(1)}, u32[]{:S(2)}, u32[]{:S(2)}) collective-permute-start(bf16[560,128]{1,0:T(8,128)(2,1)S(1)} %pad_maximum_fusion.2), channel_id=1, source_target_pairs={{0,7},{1,2},{2,1},{3,4},{4,3},{5,6},{6,5},{7,0},{8,15},{9,10},{10,... | collective-permute-start | bytes 430088 | tf_op jit(solution)/shard_map/ppermute | solution.py:495
  87.3 3.2 %collective-permute-start.19 = (bf16[560,128]{1,0:T(8,128)(2,1)S(1)}, bf16[560,128]{1,0:T(8,128)(2,1)S(1)}, u32[]{:S(2)}, u32[]{:S(2)}) collective-permute-start(bf16[560,128]{1,0:T(8,128)(2,1)S(1)} %pad_maximum_fusion.3), channel_id=1, source_target_pairs={{0,1},{1,0},{2,3},{3,2},{4,5},{5,4},{6,7},{7,6},{8,9},{9,8},{10,11... | collective-permute-start | bytes 430088 | tf_op jit(solution)/shard_map/ppermute | solution.py:495
  91.0 2.1 %collective-permute-done.18.refs_3_ = bf16[560,128]{1,0:T(8,128)(2,1)S(1)} collective-permute-done((bf16[560,128]{1,0:T(8,128)(2,1)S(1)}, bf16[560,128]{1,0:T(8,128)(2,1)S(1)}, u32[]{:S(2)}, u32[]{:S(2)}) %collective-permute-start.18) | collective-permute-done | bytes 143392 | tf_op jit(solution)/shard_map/ppermute | solution.py:495
  94.4 3.2 %collective-permute-start.20 = (bf16[560,128]{1,0:T(8,128)(2,1)S(1)}, bf16[560,128]{1,0:T(8,128)(2,1)S(1)}, u32[]{:S(2)}, u32[]{:S(2)}) collective-permute-start(bf16[560,128]{1,0:T(8,128)(2,1)S(1)} %collective-permute-done.18.refs_3_), channel_id=1, source_target_pairs={{0,1},{1,0},{2,3},{3,2},{4,5},{5,4},{6,7},{7,6},{8,9},{9,8},{10,11... | collective-permute-start | bytes 430088 | tf_op jit(solution)/shard_map/ppermute | solution.py:495
  97.6 3.4 %collective-permute-start.21 = (bf16[560,128]{1,0:T(8,128)(2,1)S(1)}, bf16[560,128]{1,0:T(8,128)(2,1)S(1)}, u32[]{:S(2)}, u32[]{:S(2)}) collective-permute-start(bf16[560,128]{1,0:T(8,128)(2,1)S(1)} %collective-permute-done.19.refs_8_), channel_id=1, source_target_pairs={{0,7},{1,2},{2,1},{3,4},{4,3},{5,6},{6,5},{7,0},{8,15},{9,10},{10,... | collective-permute-start | bytes 430088 | tf_op jit(solution)/shard_map/ppermute | solution.py:495
  102.0 3.8 %collective-permute-done.21.refs_9_ = bf16[560,128]{1,0:T(8,128)(2,1)S(1)} collective-permute-done((bf16[560,128]{1,0:T(8,128)(2,1)S(1)}, bf16[560,128]{1,0:T(8,128)(2,1)S(1)}, u32[]{:S(2)}, u32[]{:S(2)}) %collective-permute-start.21) | collective-permute-done | bytes 143392 | tf_op jit(solution)/shard_map/ppermute | solution.py:495
  105.8 3.4 %collective-permute-start.22 = (bf16[560,128]{1,0:T(8,128)(2,1)S(1)}, bf16[560,128]{1,0:T(8,128)(2,1)S(1)}, u32[]{:S(2)}, u32[]{:S(2)}) collective-permute-start(bf16[560,128]{1,0:T(8,128)(2,1)S(1)} %collective-permute-done.20.refs_4_), channel_id=1, source_target_pairs={{0,7},{1,2},{2,1},{3,4},{4,3},{5,6},{6,5},{7,0},{8,15},{9,10},{10,... | collective-permute-start | bytes 430088 | tf_op jit(solution)/shard_map/ppermute | solution.py:495
  111.2 2.9 %collective-permute-done.22.refs_5_ = bf16[560,128]{1,0:T(8,128)(2,1)S(1)} collective-permute-done((bf16[560,128]{1,0:T(8,128)(2,1)S(1)}, bf16[560,128]{1,0:T(8,128)(2,1)S(1)}, u32[]{:S(2)}, u32[]{:S(2)}) %collective-permute-start.22) | collective-permute-done | bytes 143392 | tf_op jit(solution)/shard_map/ppermute | solution.py:495
  114.1 2.2 %collective-permute-done.23.refs_10_ = bf16[560,128]{1,0:T(8,128)(2,1)S(1)} collective-permute-done((bf16[560,128]{1,0:T(8,128)(2,1)S(1)}, bf16[560,128]{1,0:T(8,128)(2,1)S(1)}, u32[]{:S(2)}, u32[]{:S(2)}) %collective-permute-start.23) | collective-permute-done | bytes 143392 | tf_op jit(solution)/shard_map/ppermute | solution.py:495
  116.3 2.4 %experts.3 = (bf16[560,128]{1,0:T(8,128)(2,1)S(1)}, bf16[560,128]{1,0:T(8,128)(2,1)S(1)}, bf16[560,128]{1,0:T(8,128)(2,1)S(1)}, bf16[560,128]{1,0:T(8,128)(2,1)S...) custom-call(s32[18]{0:T(128)S(1)} %pad_add_fusion.refs_0_, ...), custom_call_target="tpu_custom_call" | custom-call | tf_op jit(solution)/shard_map/experts/pallas_call | solution.py:345
  118.7 3.7 %collective-permute-start.24 = (bf16[560,128]{1,0:T(8,128)(2,1)S(1)}, bf16[560,128]{1,0:T(8,128)(2,1)S(1)}, u32[]{:S(2)}, u32[]{:S(2)}) collective-permute-start(bf16[560,128]{1,0:T(8,128)(2,1)S(1)} %get-tuple-element.99), channel_id=1, source_target_pairs={{0,7},{1,2},{2,1},{3,4},{4,3},{5,6},{6,5},{7,0},{8,15},{9,10},{10,... | collective-permute-start | bytes 430088 | tf_op jit(solution)/shard_map/ppermute | solution.py:495
  122.4 2.0 %collective-permute-start.28 = (bf16[560,128]{1,0:T(8,128)(2,1)S(1)}, bf16[560,128]{1,0:T(8,128)(2,1)S(1)}, u32[]{:S(2)}, u32[]{:S(2)}) collective-permute-start(bf16[560,128]{1,0:T(8,128)(2,1)S(1)} %get-tuple-element.104), channel_id=1, source_target_pairs={{0,1},{1,0},{2,3},{3,2},{4,5},{5,4},{6,7},{7,6},{8,9},{9,8},{10,11... | collective-permute-start | bytes 430088 | tf_op jit(solution)/shard_map/ppermute | solution.py:495
  124.4 2.5 %collective-permute-done.24 = bf16[560,128]{1,0:T(8,128)(2,1)S(1)} collective-permute-done((bf16[560,128]{1,0:T(8,128)(2,1)S(1)}, bf16[560,128]{1,0:T(8,128)(2,1)S(1)}, u32[]{:S(2)}, u32[]{:S(2)}) %collective-permute-start.24) | collective-permute-done | bytes 143392 | tf_op jit(solution)/shard_map/ppermute | solution.py:495
  129.5 3.4 %collective-permute-start.29 = (bf16[560,128]{1,0:T(8,128)(2,1)S(1)}, bf16[560,128]{1,0:T(8,128)(2,1)S(1)}, u32[]{:S(2)}, u32[]{:S(2)}) collective-permute-start(bf16[560,128]{1,0:T(8,128)(2,1)S(1)} %add_convert_fusion.9), channel_id=1, source_target_pairs={{0,7},{1,2},{2,1},{3,4},{4,3},{5,6},{6,5},{7,0},{8,15},{9,10},{10,... | collective-permute-start | bytes 430088 | tf_op jit(solution)/shard_map/ppermute | solution.py:495
  134.1 3.7 %collective-permute-start.26 = (bf16[560,128]{1,0:T(8,128)(2,1)S(1)}, bf16[560,128]{1,0:T(8,128)(2,1)S(1)}, u32[]{:S(2)}, u32[]{:S(2)}) collective-permute-start(bf16[560,128]{1,0:T(8,128)(2,1)S(1)} %add_convert_fusion.10), channel_id=1, source_target_pairs={{0,7},{1,2},{2,1},{3,4},{4,3},{5,6},{6,5},{7,0},{8,15},{9,10},{10,... | collective-permute-start | bytes 430088 | tf_op jit(solution)/shard_map/ppermute | solution.py:495
  137.9 2.2 %collective-permute-start.30 = (bf16[560,128]{1,0:T(8,128)(2,1)S(1)}, bf16[560,128]{1,0:T(8,128)(2,1)S(1)}, u32[]{:S(2)}, u32[]{:S(2)}) collective-permute-start(bf16[560,128]{1,0:T(8,128)(2,1)S(1)} %add_convert_fusion.8), channel_id=1, source_target_pairs={{0,1},{1,0},{2,3},{3,2},{4,5},{5,4},{6,7},{7,6},{8,9},{9,8},{10,11... | collective-permute-start | bytes 430088 | tf_op jit(solution)/shard_map/ppermute | solution.py:495
  140.0 2.8 %collective-permute-done.26 = bf16[560,128]{1,0:T(8,128)(2,1)S(1)} collective-permute-done((bf16[560,128]{1,0:T(8,128)(2,1)S(1)}, bf16[560,128]{1,0:T(8,128)(2,1)S(1)}, u32[]{:S(2)}, u32[]{:S(2)}) %collective-permute-start.26) | collective-permute-done | bytes 143392 | tf_op jit(solution)/shard_map/ppermute | solution.py:495
  144.9 3.9 %collective-permute-start.31 = (bf16[280,128]{1,0:T(8,128)(2,1)S(1)}, bf16[280,128]{1,0:T(8,128)(2,1)S(1)}, u32[]{:S(2)}, u32[]{:S(2)}) collective-permute-start(bf16[280,128]{1,0:T(8,128)(2,1)S(1)} %get-tuple-element.119), channel_id=1, source_target_pairs={{0,7},{1,2},{2,1},{3,4},{4,3},{5,6},{6,5},{7,0},{8,15},{9,10},{10,... | collective-permute-start | bytes 215048 | tf_op jit(solution)/shard_map/ppermute | solution.py:495
  149.2 3.2 %collective-permute-done.31.refs_5_ = bf16[280,128]{1,0:T(8,128)(2,1)S(1)} collective-permute-done((bf16[280,128]{1,0:T(8,128)(2,1)S(1)}, bf16[280,128]{1,0:T(8,128)(2,1)S(1)}, u32[]{:S(2)}, u32[]{:S(2)}) %collective-permute-start.31) | collective-permute-done | bytes 71712 | tf_op jit(solution)/shard_map/ppermute | solution.py:495
  152.9 25.9 %all_to_all.21.refs_1_ = bf16[32,32,128]{2,1,0:T(8,128)(2,1)S(1)} all-to-all(bf16[32,32,128]{2,1,0:T(8,128)(2,1)S(1)} %spread.3), channel_id=1, replica_groups=mesh['groups'=2,'ep'=32,'tp'=8] {'ep'}, dimensions={0} | all-to-all | bytes 524288 | tf_op jit(solution)/shard_map/all_to_all | solution.py:538
  180.6 13.4 %all_to_all.22.refs_0_ = bf16[8,48,128]{2,1,0:T(8,128)(2,1)S(1)} all-to-all(bf16[8,48,128]{2,1,0:T(8,128)(2,1)S(1)} %get-tuple-element.123), channel_id=1, replica_groups=mesh['groups'=2,'ep'=32,'tp'=8] {'tp'}, dimensions={0} | all-to-all | bytes 196608 | tf_op jit(solution)/shard_map/all_to_all | solution.py:563
  (44 shorter events, 22.4 us)
Async XLA Ops:
  2.8 1.1 copy-start
  71.3 13.6 %copy-start.6 = (bf16[32,32,128]{2,1,0:T(8,128)(2,1)}, bf16[32,32,128]{2,1,0:T(8,128)(2,1)S(1)}, u32[]{:S(2)}) copy-start(bf16[32,32,128]{2,1,0:T(8,128)(2,1)S(1)} %all_to_all.20.refs_1_.refs_0_) | copy-start | bytes 786436
  72.8 8.6 %collective-permute-start.17 = (bf16[280,128]{1,0:T(8,128)(2,1)S(1)}, bf16[280,128]{1,0:T(8,128)(2,1)S(1)}, u32[]{:S(2)}, u32[]{:S(2)}) collective-permute-start(bf16[280,128]{1,0:T(8,128)(2,1)S(1)} %get-tuple-element.84.refs_6_), channel_id=1, source_target_pairs={{0,7},{1,2},{2,1},{3,4},{4,3},{5,6},{6,5},{7,0},{8,15},{9,10},{10,... | collective-permute-start | bytes 215048 | tf_op jit(solution)/shard_map/ppermute | solution.py:495
  78.5 6.3 %collective-permute-start.16 = (bf16[280,128]{1,0:T(8,128)(2,1)S(1)}, bf16[280,128]{1,0:T(8,128)(2,1)S(1)}, u32[]{:S(2)}, u32[]{:S(2)}) collective-permute-start(bf16[280,128]{1,0:T(8,128)(2,1)S(1)} %get-tuple-element.83.refs_1_), channel_id=1, source_target_pairs={{0,1},{1,0},{2,3},{3,2},{4,5},{5,4},{6,7},{7,6},{8,9},{9,8},{10,11... | collective-permute-start | bytes 215048 | tf_op jit(solution)/shard_map/ppermute | solution.py:495
  84.8 8.2 %collective-permute-start.18 = (bf16[560,128]{1,0:T(8,128)(2,1)S(1)}, bf16[560,128]{1,0:T(8,128)(2,1)S(1)}, u32[]{:S(2)}, u32[]{:S(2)}) collective-permute-start(bf16[560,128]{1,0:T(8,128)(2,1)S(1)} %pad_maximum_fusion.2), channel_id=1, source_target_pairs={{0,7},{1,2},{2,1},{3,4},{4,3},{5,6},{6,5},{7,0},{8,15},{9,10},{10,... | collective-permute-start | bytes 430088 | tf_op jit(solution)/shard_map/ppermute | solution.py:495
  87.3 7.0 %collective-permute-start.19 = (bf16[560,128]{1,0:T(8,128)(2,1)S(1)}, bf16[560,128]{1,0:T(8,128)(2,1)S(1)}, u32[]{:S(2)}, u32[]{:S(2)}) collective-permute-start(bf16[560,128]{1,0:T(8,128)(2,1)S(1)} %pad_maximum_fusion.3), channel_id=1, source_target_pairs={{0,1},{1,0},{2,3},{3,2},{4,5},{5,4},{6,7},{7,6},{8,9},{9,8},{10,11... | collective-permute-start | bytes 430088 | tf_op jit(solution)/shard_map/ppermute | solution.py:495
  90.6 25.6 %copy-start.2 = (bf16[2,128,2560]{2,1,0:T(8,128)(2,1)S(1)}, bf16[2,128,2560]{2,1,0:T(8,128)(2,1)}, u32[]{:S(2)}) copy-start(bf16[2,128,2560]{2,1,0:T(8,128)(2,1)} %param.16) | copy-start | bytes 3932164
  90.6 25.6 %copy-start.3 = (bf16[2,128,2560]{2,1,0:T(8,128)(2,1)S(1)}, bf16[2,128,2560]{2,1,0:T(8,128)(2,1)}, u32[]{:S(2)}) copy-start(bf16[2,128,2560]{2,1,0:T(8,128)(2,1)} %param.17) | copy-start | bytes 3932164
  91.0 25.3 %copy-start.1 = (bf16[2,128,2560]{2,1,0:T(8,128)(2,1)S(1)}, bf16[2,128,2560]{2,1,0:T(8,128)(2,1)}, u32[]{:S(2)}) copy-start(bf16[2,128,2560]{2,1,0:T(8,128)(2,1)} %param.15) | copy-start | bytes 3932164
  94.4 7.7 %collective-permute-start.20 = (bf16[560,128]{1,0:T(8,128)(2,1)S(1)}, bf16[560,128]{1,0:T(8,128)(2,1)S(1)}, u32[]{:S(2)}, u32[]{:S(2)}) collective-permute-start(bf16[560,128]{1,0:T(8,128)(2,1)S(1)} %collective-permute-done.18.refs_3_), channel_id=1, source_target_pairs={{0,1},{1,0},{2,3},{3,2},{4,5},{5,4},{6,7},{7,6},{8,9},{9,8},{10,11... | collective-permute-start | bytes 430088 | tf_op jit(solution)/shard_map/ppermute | solution.py:495
  97.6 8.2 %collective-permute-start.21 = (bf16[560,128]{1,0:T(8,128)(2,1)S(1)}, bf16[560,128]{1,0:T(8,128)(2,1)S(1)}, u32[]{:S(2)}, u32[]{:S(2)}) collective-permute-start(bf16[560,128]{1,0:T(8,128)(2,1)S(1)} %collective-permute-done.19.refs_8_), channel_id=1, source_target_pairs={{0,7},{1,2},{2,1},{3,4},{4,3},{5,6},{6,5},{7,0},{8,15},{9,10},{10,... | collective-permute-start | bytes 430088 | tf_op jit(solution)/shard_map/ppermute | solution.py:495
  105.8 8.2 %collective-permute-start.22 = (bf16[560,128]{1,0:T(8,128)(2,1)S(1)}, bf16[560,128]{1,0:T(8,128)(2,1)S(1)}, u32[]{:S(2)}, u32[]{:S(2)}) collective-permute-start(bf16[560,128]{1,0:T(8,128)(2,1)S(1)} %collective-permute-done.20.refs_4_), channel_id=1, source_target_pairs={{0,7},{1,2},{2,1},{3,4},{4,3},{5,6},{6,5},{7,0},{8,15},{9,10},{10,... | collective-permute-start | bytes 430088 | tf_op jit(solution)/shard_map/ppermute | solution.py:495
  109.2 7.0 %collective-permute-start.23 = (bf16[560,128]{1,0:T(8,128)(2,1)S(1)}, bf16[560,128]{1,0:T(8,128)(2,1)S(1)}, u32[]{:S(2)}, u32[]{:S(2)}) collective-permute-start(bf16[560,128]{1,0:T(8,128)(2,1)S(1)} %collective-permute-done.21.refs_9_), channel_id=1, source_target_pairs={{0,1},{1,0},{2,3},{3,2},{4,5},{5,4},{6,7},{7,6},{8,9},{9,8},{10,11... | collective-permute-start | bytes 430088 | tf_op jit(solution)/shard_map/ppermute | solution.py:495
  118.7 8.2 %collective-permute-start.24 = (bf16[560,128]{1,0:T(8,128)(2,1)S(1)}, bf16[560,128]{1,0:T(8,128)(2,1)S(1)}, u32[]{:S(2)}, u32[]{:S(2)}) collective-permute-start(bf16[560,128]{1,0:T(8,128)(2,1)S(1)} %get-tuple-element.99), channel_id=1, source_target_pairs={{0,7},{1,2},{2,1},{3,4},{4,3},{5,6},{6,5},{7,0},{8,15},{9,10},{10,... | collective-permute-start | bytes 430088 | tf_op jit(solution)/shard_map/ppermute | solution.py:495
  122.4 7.0 %collective-permute-start.28 = (bf16[560,128]{1,0:T(8,128)(2,1)S(1)}, bf16[560,128]{1,0:T(8,128)(2,1)S(1)}, u32[]{:S(2)}, u32[]{:S(2)}) collective-permute-start(bf16[560,128]{1,0:T(8,128)(2,1)S(1)} %get-tuple-element.104), channel_id=1, source_target_pairs={{0,1},{1,0},{2,3},{3,2},{4,5},{5,4},{6,7},{7,6},{8,9},{9,8},{10,11... | collective-permute-start | bytes 430088 | tf_op jit(solution)/shard_map/ppermute | solution.py:495
  127.0 7.0 %collective-permute-start.25 = (bf16[560,128]{1,0:T(8,128)(2,1)S(1)}, bf16[560,128]{1,0:T(8,128)(2,1)S(1)}, u32[]{:S(2)}, u32[]{:S(2)}) collective-permute-start(bf16[560,128]{1,0:T(8,128)(2,1)S(1)} %add_convert_fusion.11), channel_id=1, source_target_pairs={{0,1},{1,0},{2,3},{3,2},{4,5},{5,4},{6,7},{7,6},{8,9},{9,8},{10,11... | collective-permute-start | bytes 430088 | tf_op jit(solution)/shard_map/ppermute | solution.py:495
  129.5 8.3 %collective-permute-start.29 = (bf16[560,128]{1,0:T(8,128)(2,1)S(1)}, bf16[560,128]{1,0:T(8,128)(2,1)S(1)}, u32[]{:S(2)}, u32[]{:S(2)}) collective-permute-start(bf16[560,128]{1,0:T(8,128)(2,1)S(1)} %add_convert_fusion.9), channel_id=1, source_target_pairs={{0,7},{1,2},{2,1},{3,4},{4,3},{5,6},{6,5},{7,0},{8,15},{9,10},{10,... | collective-permute-start | bytes 430088 | tf_op jit(solution)/shard_map/ppermute | solution.py:495
  134.1 8.8 %collective-permute-start.26 = (bf16[560,128]{1,0:T(8,128)(2,1)S(1)}, bf16[560,128]{1,0:T(8,128)(2,1)S(1)}, u32[]{:S(2)}, u32[]{:S(2)}) collective-permute-start(bf16[560,128]{1,0:T(8,128)(2,1)S(1)} %add_convert_fusion.10), channel_id=1, source_target_pairs={{0,7},{1,2},{2,1},{3,4},{4,3},{5,6},{6,5},{7,0},{8,15},{9,10},{10,... | collective-permute-start | bytes 430088 | tf_op jit(solution)/shard_map/ppermute | solution.py:495
  137.9 7.0 %collective-permute-start.30 = (bf16[560,128]{1,0:T(8,128)(2,1)S(1)}, bf16[560,128]{1,0:T(8,128)(2,1)S(1)}, u32[]{:S(2)}, u32[]{:S(2)}) collective-permute-start(bf16[560,128]{1,0:T(8,128)(2,1)S(1)} %add_convert_fusion.8), channel_id=1, source_target_pairs={{0,1},{1,0},{2,3},{3,2},{4,5},{5,4},{6,7},{7,6},{8,9},{9,8},{10,11... | collective-permute-start | bytes 430088 | tf_op jit(solution)/shard_map/ppermute | solution.py:495
  142.9 6.3 %collective-permute-start.27 = (bf16[280,128]{1,0:T(8,128)(2,1)S(1)}, bf16[280,128]{1,0:T(8,128)(2,1)S(1)}, u32[]{:S(2)}, u32[]{:S(2)}) collective-permute-start(bf16[280,128]{1,0:T(8,128)(2,1)S(1)} %get-tuple-element.121), channel_id=1, source_target_pairs={{0,1},{1,0},{2,3},{3,2},{4,5},{5,4},{6,7},{7,6},{8,9},{9,8},{10,11... | collective-permute-start | bytes 215048 | tf_op jit(solution)/shard_map/ppermute | solution.py:495
  144.9 7.5 %collective-permute-start.31 = (bf16[280,128]{1,0:T(8,128)(2,1)S(1)}, bf16[280,128]{1,0:T(8,128)(2,1)S(1)}, u32[]{:S(2)}, u32[]{:S(2)}) collective-permute-start(bf16[280,128]{1,0:T(8,128)(2,1)S(1)} %get-tuple-element.119), channel_id=1, source_target_pairs={{0,7},{1,2},{2,1},{3,4},{4,3},{5,6},{6,5},{7,0},{8,15},{9,10},{10,... | collective-permute-start | bytes 215048 | tf_op jit(solution)/shard_map/ppermute | solution.py:495

commit v4 on v3

--- a/solution.py
+++ b/solution.py
@@ -25,8 +25,6 @@
         self.slots = 2 * self.half
         self.packed = 5 * self.half
         self.packed_up = -(-self.packed // LANE) * LANE
-        self.side = self.packed // 2
-        self.step = next(n for n in range(200, 0, -8) if self.side % n == 0)
         self.chunk = 2 * self.cap + self.half_pre + 2
         self.own_rows = rows // lanes
         assert width == (2 * lanes + lanes // 2) * LANE and self.chunk % 8 == 0
@@ -168,7 +166,7 @@
     return jnp.where(kept & (block < 3), piece * plan.half + row, -1), needed
 
 
-def compact_kernel(plan, info_ref, in_ref, a_ref, b_ref, target_ref, needed_ref):
+def compact_kernel(plan, info_ref, in_ref, out_ref, target_ref, needed_ref):
     total = plan.ranks * plan.chunk
     data = in_ref[...].reshape(total, LANE)
     first = weight_rows(plan, data)[0]
@@ -176,12 +174,9 @@
     target, needed = target_row(info_ref, plan, named)
     target_ref[...] = target
     needed_ref[...] = jnp.broadcast_to(needed, (8, LANE))
-    side = plan.side
-    for ref, begin in ((a_ref, 0), (b_ref, side)):
-        for at in range(0, side, plan.step):
-            shape = (plan.step, total)
-            take = one_hot(iota(shape, 0) + (begin + at) == target[0:1, :])
-            ref[at : at + plan.step, :] = dot(take, data).astype(BF16)
+    for at in range(0, plan.packed, plan.half):
+        take = one_hot(iota((plan.half, total), 0) + at == target[0:1, :])
+        out_ref[at : at + plan.half, :] = dot(take, data).astype(BF16)
 
 
 def weights_kernel(plan, in_ref, target_ref, weight_ref):
@@ -233,69 +228,45 @@
         combine_ref[:, b * total : (b + 1) * total] = one_hot(match & (block == b))
 
 
-def lane_at(plan, me, sign, steps):
-    return lax.rem(me + sign * steps + plan.lanes, plan.lanes)
-
-
-def expert_kernel(plan, info_ref, *refs):
-    n = len(GATHERED)
-    a_refs, b_refs = refs[:n], refs[n : 2 * n]
-    weight_ref, wg, wu, wd = refs[2 * n : 2 * n + 4]
-    outs = refs[2 * n + 4 : -2]
-    x_ref, h_ref = refs[-2:]
+def expert_kernel(plan, offsets, info_ref, *refs):
+    n = len(offsets)
+    weight_ref, wg, wu, wd, out_ref, x_ref, h_ref = refs[n:]
     me = info_ref[0]
-    sign = 1 - 2 * lax.rem(me, 2)
-    lanes, half, slots, side = plan.lanes, plan.half, plan.slots, plan.side
-    over = side - slots
-
-    def columns(lane):
+    lanes, half, slots = plan.lanes, plan.half, plan.slots
+    for offset, part in zip(offsets, refs):
+        lane = lax.rem(me + offset + lanes, lanes)
         first = pl.multiple_of(lane * (2 * LANE), LANE)
         tail = pl.multiple_of((2 * lanes + lane // 2) * LANE, LANE)
         start = pl.multiple_of(lax.rem(lane, 2) * half, 8)
-        return (
-            pl.ds(first, LANE),
-            pl.ds(pl.multiple_of(first + LANE, LANE), LANE),
-            pl.ds(tail, LANE),
-            pl.ds(start, half),
-        )
-
-    for refs_of, turn in ((a_refs, sign), (b_refs, -sign)):
-        for ref, steps in zip(refs_of, GATHERED):
-            for i, step in enumerate(steps):
-                first, second, tail, rows = columns(lane_at(plan, me, turn, step))
-                at = i * side
-                if refs_of is a_refs:
-                    x_ref[:, first] = ref[at : at + slots, :]
-                    x_ref[0:over, second] = ref[at + slots : at + side, :]
-                else:
-                    x_ref[over:slots, second] = ref[at : at + slots - over, :]
-                    x_ref[rows, tail] = ref[at + slots - over : at + side, :]
+        x_ref[:, pl.ds(first, LANE)] = part[0:slots, :]
+        x_ref[:, pl.ds(pl.multiple_of(first + LANE, LANE), LANE)] = part[slots : 2 * slots, :]
+        x_ref[pl.ds(start, half), pl.ds(tail, LANE)] = part[2 * slots : 2 * slots + half, :]
     turned = (((1,), (1,)), ((), ()))
     x = x_ref[...]
     gate = lax.dot_general(x, wg[...], turned, preferred_element_type=F32)
     up = lax.dot_general(x, wu[...], turned, preferred_element_type=F32)
     hidden = gate / (1.0 + jnp.exp(-gate)) * up * weight_ref[...]
     h_ref[...] = hidden.astype(BF16)
-    out = 0
-    for steps in SCATTERED:
-        for turn in (sign, -sign):
-            for i, step in enumerate(steps):
-                first, second, tail, rows = columns(lane_at(plan, me, turn, step))
-                ref, at = outs[out], i * side
-                if turn is sign:
-                    ref[at : at + slots, :] = dot(h_ref[...], wd[:, first]).astype(BF16)
-                    ref[at + slots : at + side, :] = dot(h_ref[0:over, :], wd[:, second]).astype(BF16)
-                else:
-                    ref[at : at + slots - over, :] = dot(h_ref[over:slots, :], wd[:, second]).astype(BF16)
-                    ref[at + slots - over : at + side, :] = dot(h_ref[rows, :], wd[:, tail]).astype(BF16)
-            out += 1
-
-
-def spread_kernel(plan, take_ref, needed_ref, own_a, got_a, own_b, got_b, out_ref, sum_ref):
-    side = plan.side
-    sum_ref[0:side, :] = (own_a[...].astype(F32) + got_a[...].astype(F32)).astype(BF16)
-    sum_ref[side : 2 * side, :] = (own_b[...].astype(F32) + got_b[...].astype(F32)).astype(BF16)
-    sum_ref[2 * side :, :] = jnp.zeros((plan.packed_up - 2 * side, LANE), BF16)
+    for lane in range(lanes):
+        at = lane * 2 * LANE
+        y = dot(h_ref[...], wd[:, at : at + 2 * LANE]).astype(BF16)
+        out_ref[lane, 0:slots, :] = y[:, :LANE]
+        out_ref[lane, slots : 2 * slots, :] = y[:, LANE:]
+    for pair in range(0, lanes // 2, 2):
+        at = (2 * lanes + pair) * LANE
+        y = dot(h_ref[...], wd[:, at : at + 2 * LANE]).astype(BF16)
+        for k in range(2):
+            for p in range(2):
+                piece = y[p * half : (p + 1) * half, k * LANE : (k + 1) * LANE]
+                out_ref[2 * (pair + k) + p, 2 * slots : 2 * slots + half, :] = piece
+
+
+def spread_kernel(plan, take_ref, needed_ref, in_ref, out_ref, sum_ref):
+    total = in_ref[0].astype(F32)
+    for lane in range(1, plan.lanes):
+        total += in_ref[lane].astype(F32)
+    sum_ref[0 : plan.packed, :] = total.astype(BF16)
+    sum_ref[plan.packed :, :] = jnp.zeros((plan.packed_up - plan.packed, LANE), BF16)
     shape = (plan.ranks, plan.chunk, LANE)
     spread = dot(take_ref[...], sum_ref[...]).reshape(shape)
     over = jnp.where(needed_ref[0:1, :] > float(plan.decode), 1.0, 0.0)
@@ -334,9 +305,6 @@
 SMEM = pl.BlockSpec(memory_space=pltpu.SMEM)
 VMEM = pl.BlockSpec(memory_space=pltpu.VMEM)
 HBM = pl.BlockSpec(memory_space=pltpu.HBM)
-GATHERED = ((0,), (1,), (-1, -2), (2, 3), (-3, -4))
-SCATTERED = ((-3, -4), (2, 3), (-1, -2), (0,), (1,))
-
 
 def call(kernel, name, out, specs, *args, scratch=(), limit=24 << 20, flops=0):
     cost = None
@@ -369,13 +337,11 @@
 
 
 def compact(plan, info, received):
-    share = jax.ShapeDtypeStruct((plan.side, LANE), BF16)
     return call(
         lambda *refs: compact_kernel(plan, *refs),
         "compact",
         (
-            share,
-            share,
+            jax.ShapeDtypeStruct((plan.packed, LANE), BF16),
             jax.ShapeDtypeStruct((8, plan.ranks * plan.chunk), I32),
             jax.ShapeDtypeStruct((8, LANE), F32),
         ),
@@ -420,20 +386,16 @@
     )
 
 
-def experts(plan, info, a_parts, b_parts, weights, w_gate, w_up, w_down):
+def experts(plan, offsets, info, parts, weights, w_gate, w_up, w_down):
     hidden = w_gate.shape[0] * w_gate.shape[1]
     flat = [w.reshape(hidden, plan.width) for w in (w_gate, w_up, w_down)]
-    out = []
-    for steps in SCATTERED:
-        out += [jax.ShapeDtypeStruct((len(steps) * plan.side, LANE), BF16)] * 2
-    outs = call(
-        lambda *refs: expert_kernel(plan, *refs),
+    return call(
+        lambda *refs: expert_kernel(plan, offsets, *refs),
         "experts",
-        tuple(out),
-        [SMEM] + [VMEM] * (2 * len(a_parts) + 4),
+        jax.ShapeDtypeStruct((plan.lanes, plan.packed, LANE), BF16),
+        [SMEM] + [VMEM] * (len(parts) + 4),
         info,
-        *a_parts,
-        *b_parts,
+        *parts,
         weights,
         *flat,
         scratch=[
@@ -442,21 +404,17 @@
         ],
         limit=32 << 20,
     )
-    return outs[0::2], outs[1::2]
-
-
-def spread(plan, take, needed, own_a, got_a, own_b, got_b):
+
+
+def spread(plan, take, needed, returned):
     return call(
         lambda *refs: spread_kernel(plan, *refs),
         "spread",
         jax.ShapeDtypeStruct((plan.ranks, plan.chunk, LANE), BF16),
-        [VMEM] * 6,
+        [VMEM] * 3,
         take,
         needed,
-        own_a,
-        got_a,
-        own_b,
-        got_b,
+        returned,
         scratch=[pltpu.VMEM((plan.packed_up, LANE), BF16)],
     )
 
@@ -485,57 +443,33 @@
     )
 
 
-def neighbours(lanes):
-    near = [(i, i ^ 1) for i in range(lanes)]
-    far = [(i, (i - 1 + 2 * (i % 2)) % lanes) for i in range(lanes)]
-    return near, far
-
-
-def swap(arrays, pairs):
-    return [lax.ppermute(x, "tp", p) for x, p in zip(arrays, pairs)]
-
-
-def gather_lanes(shares, lanes, beside):
-    near, far = neighbours(lanes)
-    own = list(shares)
-    first = swap(own, (near, far))
-    held = [jnp.concatenate([x, y]) for x, y in zip(own, first)]
-    parts, values = [own, first], []
-    for hop in range(lanes // 2 - 1):
-        if hop < len(beside):
-            held, value = lax.optimization_barrier((held, beside[hop]))
+def gather_lanes(packed, lanes, beside):
+    right = [(i, (i + 1) % lanes) for i in range(lanes)]
+    left = [(i, (i - 1) % lanes) for i in range(lanes)]
+    parts, offsets, values = [packed], [0], []
+    held = [packed, packed]
+    for hop in range(1, lanes // 2 + 1):
+        if hop > 1 and hop - 2 < len(beside):
+            held, value = lax.optimization_barrier((held, beside[hop - 2]))
             values.append(value)
-        held = swap(held, (far, near) if hop % 2 == 0 else (near, far))
-        parts.append(held)
-    return [p[0] for p in parts], [p[1] for p in parts], values
-
-
-def plus(x, y):
-    return (x.astype(F32) + y.astype(F32)).astype(BF16)
-
-
-def reduce_lanes(a_outs, b_outs, side, lanes):
-    near, far = neighbours(lanes)
-    stages = list(zip(a_outs, b_outs))
-    held = list(stages[0])
-    for hop in range(lanes // 2 - 2):
-        got = swap(held, (far, near) if hop % 2 == 0 else (near, far))
-        held = [plus(x, y) for x, y in zip(stages[hop + 1], got)]
-    got = swap(held, (far, near))
-    away = [plus(x, y[side:]) for x, y in zip(stages[-1], got)]
-    home = [plus(x, y[:side]) for x, y in zip(stages[-2], got)]
-    last = swap(away, (near, far))
-    return home[0], last[0], home[1], last[1]
+        got = [lax.ppermute(held[0], "tp", right)]
+        offsets.append(-hop)
+        if hop < lanes // 2:
+            got.append(lax.ppermute(held[1], "tp", left))
+            offsets.append(hop)
+        parts += got
+        held = got
+    return parts, offsets, values
 
 
 def through_experts(plan, info, received, take_in, matrices):
-    a_share, b_share, target, needed = compact(plan, info, received)
+    packed, target, needed = compact(plan, info, received)
     beside = [weights_table(plan, received, target), spread_table(plan, target), take_in]
-    a_parts, b_parts, beside = gather_lanes((a_share, b_share), plan.lanes, beside)
+    parts, offsets, beside = gather_lanes(packed, plan.lanes, beside)
     weights, take_out, take_in = beside
-    a_outs, b_outs = experts(plan, info, a_parts, b_parts, weights, *matrices)
-    sums = reduce_lanes(a_outs, b_outs, plan.side, plan.lanes)
-    back = lax.all_to_all(spread(plan, take_out, needed, *sums), "ep", 0, 0, tiled=True)
+    partial = experts(plan, offsets, info, parts, weights, *matrices)
+    returned = lax.all_to_all(partial, "tp", 0, 0, tiled=True)
+    back = lax.all_to_all(spread(plan, take_out, needed, returned), "ep", 0, 0, tiled=True)
     return combine(plan, take_in, back)
 
 
@@ -548,9 +482,13 @@
     plan, whole = Plan(*sizes, min(USUAL_DECODE, most)), Plan(*sizes, most)
     places = jnp.stack([lax.axis_index("tp"), lax.axis_index("ep")]).astype(I32)
     info = jnp.concatenate([places, prefill_ranks])
-    routes = jnp.concatenate(
-        [device_choice.T.astype(F32), local_expert.T.astype(F32), route_weight.T]
-    )
+    tables = (device_choice, local_expert, route_weight)
+    wide = sum(x.shape[1] for x in tables)
+    routes, at = 0.0, 0
+    for x in tables:
+        routes += jnp.pad(x.astype(F32), ((0, 0), (at, wide - at - x.shape[1])))
+        at += x.shape[1]
+    routes = routes.T
     outgoing = pack(plan, info, routes, tokens)
     received = lax.all_to_all(outgoing, "ep", 0, 0, tiled=True)
     take_in = combine_table(plan, info, routes)

time: 195 us -> 189 us (0.969)
  blocking collectives: 105 us -> 134 us
  starting transfers between devices: 48.2 us -> 25.8 us
  waiting for transfers between devices: 26.2 us -> 14.7 us
    all_to_all x1 -> x2, blocking collectives: 25.9 us -> 56.4 us  [the longest x1 30 us: through_experts(): returned = lax.all_to_all(partial, 'tp', 0, 0, tiled=True)]
    ppermute x16 -> x7, starting transfers between devices: 48.2 us -> 25.8 us  [the longest x3 16.5 us: gather_lanes(): got.append(lax.ppermute(held[1], 'tp', left))]
    ppermute x16 -> x7, waiting for transfers between devices: 26.2 us -> 14.7 us  [the longest x4 11.4 us: gather_lanes(): got = [lax.ppermute(held[0], 'tp', right)]]
    all_to_all x1, blocking collectives: 13.4 us -> 11.2 us  [on_device(): shares = lax.all_to_all(shares, 'tp', 0, 0, tiled=True)]
  transfers between devices with their start and end apart: 16 -> 7, of which waited for: 12 -> 7; matrix products, arithmetic and copies ran while one was open for 0% -> 0% of each run, Pallas kernels for 1% -> 1%
where the time goes in v4:
time: 189 us; the launch traced here: 188 us
  blocking collectives  134 us (71%)
  starting transfers between devices  25.8 us (14%)
  waiting for transfers between devices  14.7 us (8%)
  Pallas kernels  8.52 us (5%)
  other arithmetic  2.8 us (1%)
    all_to_all x1, blocking collectives, on_device(): received = lax.all_to_all(outgoing, 'ep', 0, 0, tiled=True)  66.2 us
    all_to_all x1, blocking collectives, through_experts(): returned = lax.all_to_all(partial, 'tp', 0, 0, tiled=True)  30 us
    all_to_all x1, blocking collectives, through_experts(): lax.all_to_all(spread(plan, take_out, needed, returned), 'ep', 0, 0, tile...  26.4 us
    ppermute x3, starting transfers between devices, gather_lanes(): got.append(lax.ppermute(held[1], 'tp', left))  16.5 us
    ppermute x4, waiting for transfers between devices, gather_lanes(): got = [lax.ppermute(held[0], 'tp', right)]  11.4 us
    all_to_all x1, blocking collectives, on_device(): shares = lax.all_to_all(shares, 'tp', 0, 0, tiled=True)  11.2 us
    ppermute x4, starting transfers between devices, gather_lanes(): got = [lax.ppermute(held[0], 'tp', right)]  9.25 us
    pallas_call x9, Pallas kernels, call(): pl.pallas_call(kernel, out_shape=out, in_specs=specs, out_specs=jax.tree....  8.52 us
  transfers between devices with their start and end apart: 7, of which 7 were waited for; matrix products, arithmetic and copies ran while one was open for 0% of the time, Pallas kernels for 1%

profile of v4, /device:TPU:80, one launch (start us, length us, event | category | flops | bytes accessed | tf_op | source)
XLA Modules:
  0.0 188.1 jit_solution(8652040952510262789)
XLA Ops:
  1.4 0.7 pad_add_fusion.refs_0_
  2.1 0.7 add_bitcast_fusion.refs_1_
  2.8 1.1 copy-done
  3.9 1.1 pack.1
  5.0 66.2 %all_to_all.30.refs_1_.refs_0_ = bf16[32,32,128]{2,1,0:T(8,128)(2,1)S(1)} all-to-all(bf16[32,32,128]{2,1,0:T(8,128)(2,1)S(1)} %pack.1), channel_id=1, replica_groups=mesh['groups'=2,'ep'=32,'tp'=8] {'ep'}, dimensions={0} | all-to-all | bytes 524288 | tf_op jit(solution)/shard_map/all_to_all | solution.py:493
  71.3 1.5 compact.3
  72.7 5.8 %collective-permute-start.8 = (bf16[560,128]{1,0:T(8,128)(2,1)S(1)}, bf16[560,128]{1,0:T(8,128)(2,1)S(1)}, u32[]{:S(2)}, u32[]{:S(2)}) collective-permute-start(bf16[560,128]{1,0:T(8,128)(2,1)S(1)} %get-tuple-element.59.refs_1_), channel_id=1, source_target_pairs={{0,7},{1,0},{2,1},{3,2},{4,3},{5,4},{6,5},{7,6},{8,15},{9,8},{10,9... | collective-permute-start | bytes 430088 | tf_op jit(solution)/shard_map/ppermute | solution.py:458
  78.5 2.0 %collective-permute-start.7 = (bf16[560,128]{1,0:T(8,128)(2,1)S(1)}, bf16[560,128]{1,0:T(8,128)(2,1)S(1)}, u32[]{:S(2)}, u32[]{:S(2)}) collective-permute-start(bf16[560,128]{1,0:T(8,128)(2,1)S(1)} %get-tuple-element.59.refs_1_), channel_id=1, source_target_pairs={{0,1},{1,2},{2,3},{3,4},{4,5},{5,6},{6,7},{7,0},{8,9},{9,10},{10,1... | collective-permute-start | bytes 430088 | tf_op jit(solution)/shard_map/ppermute | solution.py:455
  80.5 0.9 weights.3.refs_9_
  81.6 5.4 %collective-permute-done.7.refs_2_ = bf16[560,128]{1,0:T(8,128)(2,1)S(1)} collective-permute-done((bf16[560,128]{1,0:T(8,128)(2,1)S(1)}, bf16[560,128]{1,0:T(8,128)(2,1)S(1)}, u32[]{:S(2)}, u32[]{:S(2)}) %collective-permute-start.7) | collective-permute-done | bytes 143392 | tf_op jit(solution)/shard_map/ppermute | solution.py:455
  86.9 1.9 %collective-permute-start.9 = (bf16[560,128]{1,0:T(8,128)(2,1)S(1)}, bf16[560,128]{1,0:T(8,128)(2,1)S(1)}, u32[]{:S(2)}, u32[]{:S(2)}) collective-permute-start(bf16[560,128]{1,0:T(8,128)(2,1)S(1)} %collective-permute-done.7.refs_2_), channel_id=1, source_target_pairs={{0,1},{1,2},{2,3},{3,4},{4,5},{5,6},{6,7},{7,0},{8,9},{9,10},{10,1... | collective-permute-start | bytes 430088 | tf_op jit(solution)/shard_map/ppermute | solution.py:455
  88.9 5.2 %collective-permute-start.10 = (bf16[560,128]{1,0:T(8,128)(2,1)S(1)}, bf16[560,128]{1,0:T(8,128)(2,1)S(1)}, u32[]{:S(2)}, u32[]{:S(2)}) collective-permute-start(bf16[560,128]{1,0:T(8,128)(2,1)S(1)} %collective-permute-done.8.refs_3_), channel_id=1, source_target_pairs={{0,7},{1,0},{2,1},{3,2},{4,3},{5,4},{6,5},{7,6},{8,15},{9,8},{10,9... | collective-permute-start | bytes 430088 | tf_op jit(solution)/shard_map/ppermute | solution.py:458
  94.5 0.7 collective-permute-done.9.refs_4_
  95.2 1.5 collective-permute-done.10.refs_5_
  96.7 1.9 %collective-permute-start.11 = (bf16[560,128]{1,0:T(8,128)(2,1)S(1)}, bf16[560,128]{1,0:T(8,128)(2,1)S(1)}, u32[]{:S(2)}, u32[]{:S(2)}) collective-permute-start(bf16[560,128]{1,0:T(8,128)(2,1)S(1)} %collective-permute-done.9.refs_4_), channel_id=1, source_target_pairs={{0,1},{1,2},{2,3},{3,4},{4,5},{5,6},{6,7},{7,0},{8,9},{9,10},{10,1... | collective-permute-start | bytes 430088 | tf_op jit(solution)/shard_map/ppermute | solution.py:455
  98.6 5.6 %collective-permute-start.12 = (bf16[560,128]{1,0:T(8,128)(2,1)S(1)}, bf16[560,128]{1,0:T(8,128)(2,1)S(1)}, u32[]{:S(2)}, u32[]{:S(2)}) collective-permute-start(bf16[560,128]{1,0:T(8,128)(2,1)S(1)} %collective-permute-done.10.refs_5_), channel_id=1, source_target_pairs={{0,7},{1,0},{2,1},{3,2},{4,3},{5,4},{6,5},{7,6},{8,15},{9,8},{10,9... | collective-permute-start | bytes 430088 | tf_op jit(solution)/shard_map/ppermute | solution.py:458
  104.2 1.0 combine_table.1.refs_0_
  105.3 1.5 collective-permute-done.12.refs_7_
  106.9 3.4 %collective-permute-start.13 = (bf16[560,128]{1,0:T(8,128)(2,1)S(1)}, bf16[560,128]{1,0:T(8,128)(2,1)S(1)}, u32[]{:S(2)}, u32[]{:S(2)}) collective-permute-start(bf16[560,128]{1,0:T(8,128)(2,1)S(1)} %collective-permute-done.11.refs_6_), channel_id=1, source_target_pairs={{0,1},{1,2},{2,3},{3,4},{4,5},{5,6},{6,7},{7,0},{8,9},{9,10},{10,1... | collective-permute-start | bytes 430088 | tf_op jit(solution)/shard_map/ppermute | solution.py:455
  110.3 5.2 %collective-permute-done.13.refs_8_ = bf16[560,128]{1,0:T(8,128)(2,1)S(1)} collective-permute-done((bf16[560,128]{1,0:T(8,128)(2,1)S(1)}, bf16[560,128]{1,0:T(8,128)(2,1)S(1)}, u32[]{:S(2)}, u32[]{:S(2)}) %collective-permute-start.13) | collective-permute-done | bytes 143392 | tf_op jit(solution)/shard_map/ppermute | solution.py:455
  115.5 2.1 %experts.3 = bf16[8,560,128]{2,1,0:T(8,128)(2,1)S(1)} custom-call(s32[18]{0:T(128)S(1)} %pad_add_fusion.refs_0_, bf16[560,128]{1,0:T(8,128)(2,1)S(1)} %get-tuple-element.59.refs_1_, bf16[560,128]{1,0:T(8,128)(2,1)S(1)} %collective-permute-done.7.refs_2_, bf16[560,128]{1,0:T(8,128)(2,1)S(1)} %collective-permute-done.8.refs_3_, ...), custom_call_target="tpu_custom_call" | custom-call | tf_op jit(solution)/shard_map/experts/pallas_call | solution.py:313
  117.6 30.0 %all_to_all.31.refs_2_ = bf16[8,560,128]{2,1,0:T(8,128)(2,1)S(1)} all-to-all(bf16[8,560,128]{2,1,0:T(8,128)(2,1)S(1)} %experts.3), channel_id=1, replica_groups=mesh['groups'=2,'ep'=32,'tp'=8] {'tp'}, dimensions={0} | all-to-all | bytes 2293760 | tf_op jit(solution)/shard_map/all_to_all | solution.py:471
  148.3 26.4 %all_to_all.32.refs_1_ = bf16[32,32,128]{2,1,0:T(8,128)(2,1)S(1)} all-to-all(bf16[32,32,128]{2,1,0:T(8,128)(2,1)S(1)} %spread.3), channel_id=1, replica_groups=mesh['groups'=2,'ep'=32,'tp'=8] {'ep'}, dimensions={0} | all-to-all | bytes 524288 | tf_op jit(solution)/shard_map/all_to_all | solution.py:472
  176.2 11.2 %all_to_all.33.refs_0_ = bf16[8,48,128]{2,1,0:T(8,128)(2,1)S(1)} all-to-all(bf16[8,48,128]{2,1,0:T(8,128)(2,1)S(1)} %get-tuple-element.79), channel_id=1, replica_groups=mesh['groups'=2,'ep'=32,'tp'=8] {'tp'}, dimensions={0} | all-to-all | bytes 196608 | tf_op jit(solution)/shard_map/all_to_all | solution.py:501
  (19 shorter events, 4.3 us)
Async XLA Ops:
  2.8 1.1 copy-start
  71.3 17.6 %copy-start.6 = (bf16[32,32,128]{2,1,0:T(8,128)(2,1)}, bf16[32,32,128]{2,1,0:T(8,128)(2,1)S(1)}, u32[]{:S(2)}) copy-start(bf16[32,32,128]{2,1,0:T(8,128)(2,1)S(1)} %all_to_all.30.refs_1_.refs_0_) | copy-start | bytes 786436
  72.7 8.9 %collective-permute-start.8 = (bf16[560,128]{1,0:T(8,128)(2,1)S(1)}, bf16[560,128]{1,0:T(8,128)(2,1)S(1)}, u32[]{:S(2)}, u32[]{:S(2)}) collective-permute-start(bf16[560,128]{1,0:T(8,128)(2,1)S(1)} %get-tuple-element.59.refs_1_), channel_id=1, source_target_pairs={{0,7},{1,0},{2,1},{3,2},{4,3},{5,4},{6,5},{7,6},{8,15},{9,8},{10,9... | collective-permute-start | bytes 430088 | tf_op jit(solution)/shard_map/ppermute | solution.py:458
  78.5 8.4 %collective-permute-start.7 = (bf16[560,128]{1,0:T(8,128)(2,1)S(1)}, bf16[560,128]{1,0:T(8,128)(2,1)S(1)}, u32[]{:S(2)}, u32[]{:S(2)}) collective-permute-start(bf16[560,128]{1,0:T(8,128)(2,1)S(1)} %get-tuple-element.59.refs_1_), channel_id=1, source_target_pairs={{0,1},{1,2},{2,3},{3,4},{4,5},{5,6},{6,7},{7,0},{8,9},{9,10},{10,1... | collective-permute-start | bytes 430088 | tf_op jit(solution)/shard_map/ppermute | solution.py:455
  86.9 8.2 %collective-permute-start.9 = (bf16[560,128]{1,0:T(8,128)(2,1)S(1)}, bf16[560,128]{1,0:T(8,128)(2,1)S(1)}, u32[]{:S(2)}, u32[]{:S(2)}) collective-permute-start(bf16[560,128]{1,0:T(8,128)(2,1)S(1)} %collective-permute-done.7.refs_2_), channel_id=1, source_target_pairs={{0,1},{1,2},{2,3},{3,4},{4,5},{5,6},{6,7},{7,0},{8,9},{9,10},{10,1... | collective-permute-start | bytes 430088 | tf_op jit(solution)/shard_map/ppermute | solution.py:455
  88.9 7.8 %collective-permute-start.10 = (bf16[560,128]{1,0:T(8,128)(2,1)S(1)}, bf16[560,128]{1,0:T(8,128)(2,1)S(1)}, u32[]{:S(2)}, u32[]{:S(2)}) collective-permute-start(bf16[560,128]{1,0:T(8,128)(2,1)S(1)} %collective-permute-done.8.refs_3_), channel_id=1, source_target_pairs={{0,7},{1,0},{2,1},{3,2},{4,3},{5,4},{6,5},{7,6},{8,15},{9,8},{10,9... | collective-permute-start | bytes 430088 | tf_op jit(solution)/shard_map/ppermute | solution.py:458
  94.1 21.5 %copy-start.2 = (bf16[2,128,2560]{2,1,0:T(8,128)(2,1)S(1)}, bf16[2,128,2560]{2,1,0:T(8,128)(2,1)}, u32[]{:S(2)}) copy-start(bf16[2,128,2560]{2,1,0:T(8,128)(2,1)} %param.16) | copy-start | bytes 3932164
  94.1 21.5 %copy-start.3 = (bf16[2,128,2560]{2,1,0:T(8,128)(2,1)S(1)}, bf16[2,128,2560]{2,1,0:T(8,128)(2,1)}, u32[]{:S(2)}) copy-start(bf16[2,128,2560]{2,1,0:T(8,128)(2,1)} %param.17) | copy-start | bytes 3932164
  94.5 21.1 %copy-start.1 = (bf16[2,128,2560]{2,1,0:T(8,128)(2,1)S(1)}, bf16[2,128,2560]{2,1,0:T(8,128)(2,1)}, u32[]{:S(2)}) copy-start(bf16[2,128,2560]{2,1,0:T(8,128)(2,1)} %param.15) | copy-start | bytes 3932164
  96.7 8.7 %collective-permute-start.11 = (bf16[560,128]{1,0:T(8,128)(2,1)S(1)}, bf16[560,128]{1,0:T(8,128)(2,1)S(1)}, u32[]{:S(2)}, u32[]{:S(2)}) collective-permute-start(bf16[560,128]{1,0:T(8,128)(2,1)S(1)} %collective-permute-done.9.refs_4_), channel_id=1, source_target_pairs={{0,1},{1,2},{2,3},{3,4},{4,5},{5,6},{6,7},{7,0},{8,9},{9,10},{10,1... | collective-permute-start | bytes 430088 | tf_op jit(solution)/shard_map/ppermute | solution.py:455
  98.6 8.2 %collective-permute-start.12 = (bf16[560,128]{1,0:T(8,128)(2,1)S(1)}, bf16[560,128]{1,0:T(8,128)(2,1)S(1)}, u32[]{:S(2)}, u32[]{:S(2)}) collective-permute-start(bf16[560,128]{1,0:T(8,128)(2,1)S(1)} %collective-permute-done.10.refs_5_), channel_id=1, source_target_pairs={{0,7},{1,0},{2,1},{3,2},{4,3},{5,4},{6,5},{7,6},{8,15},{9,8},{10,9... | collective-permute-start | bytes 430088 | tf_op jit(solution)/shard_map/ppermute | solution.py:458
  106.9 8.7 %collective-permute-start.13 = (bf16[560,128]{1,0:T(8,128)(2,1)S(1)}, bf16[560,128]{1,0:T(8,128)(2,1)S(1)}, u32[]{:S(2)}, u32[]{:S(2)}) collective-permute-start(bf16[560,128]{1,0:T(8,128)(2,1)S(1)} %collective-permute-done.11.refs_6_), channel_id=1, source_target_pairs={{0,1},{1,2},{2,3},{3,4},{4,5},{5,6},{6,7},{7,0},{8,9},{9,10},{10,1... | collective-permute-start | bytes 430088 | tf_op jit(solution)/shard_map/ppermute | solution.py:455

commit v5 on v4

--- a/solution.py
+++ b/solution.py
@@ -31,6 +31,14 @@
         assert rows == LANE and self.half_dec <= self.cap - DEC_RANK and ranks <= LANE
 
 
+class Info:
+    def __init__(self, pre_ref):
+        self.places, self.pre_ref = (lax.axis_index("tp"), lax.axis_index("ep")), pre_ref
+
+    def __getitem__(self, i):
+        return self.places[i] if i < 2 else self.pre_ref[i - 2]
+
+
 def iota(shape, dim):
     return lax.broadcasted_iota(I32, shape, dim)
 
@@ -68,11 +76,11 @@
     return jnp.where(kept, block, 3), slot
 
 
-def named_ranks(plan, full, routes_ref):
+def named_ranks(plan, full, choice_ref):
     shape = (plan.ranks, plan.rows)
     live = iota(shape, 1) < jnp.where(full, plan.rows, DEC_RANK)
     rank = iota(shape, 0)
-    hits = [(routes_ref[k : k + 1, :].astype(I32) == rank) & live for k in range(DEV_TOP)]
+    hits = [(choice_ref[k : k + 1, :] == rank) & live for k in range(DEV_TOP)]
     named = sum(jnp.where(hit, 1.0, 0.0) for hit in hits)
     return hits, named, places(plan, named)
 
@@ -82,31 +90,34 @@
     return jnp.where(named > 0.5, before, -1.0)
 
 
-def pack_kernel(plan, info_ref, routes_ref, tok_ref, out_ref, x_ref, sems):
+def pack_kernel(plan, pre_hbm, choice_hbm, le_hbm, rw_hbm, tok_ref, out_ref, *scratch):
+    pre_ref, choice_ref, le_ref, rw_ref, x_ref, sems = scratch
+    info_ref = Info(pre_ref)
     lane, own = info_ref[0], info_ref[1]
     first_at = pl.multiple_of(lane * (2 * LANE), LANE)
     tail_at = pl.multiple_of((2 * plan.lanes + lane // 2) * LANE, LANE)
-    copies = [
-        pltpu.make_async_copy(
-            tok_ref.at[:, pl.ds(first_at, 2 * LANE)], x_ref.at[:, 0 : 2 * LANE], sems.at[0]
-        ),
-        pltpu.make_async_copy(
-            tok_ref.at[:, pl.ds(tail_at, LANE)], x_ref.at[:, 2 * LANE : 3 * LANE], sems.at[1]
-        ),
+    ends = [
+        (pre_hbm, pre_ref),
+        (choice_hbm, choice_ref),
+        (le_hbm, le_ref),
+        (rw_hbm, rw_ref),
+        (tok_ref.at[:, pl.ds(first_at, 2 * LANE)], x_ref.at[:, 0 : 2 * LANE]),
+        (tok_ref.at[:, pl.ds(tail_at, LANE)], x_ref.at[:, 2 * LANE : 3 * LANE]),
     ]
+    copies = [pltpu.make_async_copy(a, b, sems.at[i]) for i, (a, b) in enumerate(ends)]
     for copy in copies:
         copy.start()
+    for copy in copies[:4]:
+        copy.wait()
     full = is_prefill(info_ref, plan, own)
-    hits, named, place = named_ranks(plan, full, routes_ref)
+    hits, named, place = named_ranks(plan, full, choice_ref)
     weights = []
     for e in range(2):
         total = jnp.zeros(named.shape, F32)
         for k, hit in enumerate(hits):
             for j in (2 * k, 2 * k + 1):
-                at = DEV_TOP + j
-                chosen = hit & (routes_ref[at : at + 1, :] == float(e))
-                at += TOPK
-                total += jnp.where(chosen, routes_ref[at : at + 1, :], 0.0)
+                chosen = hit & (le_ref[j : j + 1, :] == e)
+                total += jnp.where(chosen, rw_ref[j : j + 1, :], 0.0)
         weights.append(total)
     full_shape = (plan.ranks, plan.chunk, LANE)
     flat = plan.ranks * plan.chunk
@@ -114,7 +125,7 @@
     block, slot = chunk_index(j, plan, lane % 2, full)
     match = place.astype(I32)[:, None, :] == slot
     picks = [one_hot(match & (block == b)).reshape(flat, LANE) for b in range(3)]
-    for copy in copies:
+    for copy in copies[4:]:
         copy.wait()
     total = sum(dot(picks[b], x_ref[:, b * LANE : (b + 1) * LANE]) for b in range(3))
     total = total.reshape(full_shape)
@@ -210,12 +221,12 @@
             spread_ref[g : g + LANE, at : at + LANE] = one_hot(col + at == column)
 
 
-def combine_table_kernel(plan, info_ref, routes_ref, combine_ref):
+def combine_table_kernel(plan, info_ref, choice_ref, combine_ref):
     lane, own = info_ref[0], info_ref[1]
     ranks, rows = plan.ranks, plan.rows
     total = ranks * plan.chunk
     full = is_prefill(info_ref, plan, own)
-    _, _, place = named_ranks(plan, full, routes_ref)
+    _, _, place = named_ranks(plan, full, choice_ref)
     square = jnp.concatenate([place, jnp.zeros((rows - ranks, rows), F32)], axis=0)
     turned = square.T[:, :ranks].astype(BF16)
     spread = (ranks, total)
@@ -286,7 +297,7 @@
             ]
     shape = (8, total)
     flags = one_hot(iota(shape, 1) % plan.chunk == plan.chunk - 1)
-    over_ref[...] = dot(flags, data)
+    over_ref[0] = jnp.where(jnp.max(dot(flags, data)) > 0.0, 1, 0)
 
 
 def finish_kernel(plan, in_ref, out_ref):
@@ -314,7 +325,7 @@
         kernel,
         out_shape=out,
         in_specs=specs,
-        out_specs=jax.tree.map(lambda _: VMEM, out),
+        out_specs=jax.tree.map(lambda o: SMEM if o.shape == (1,) else VMEM, out),
         scratch_shapes=scratch,
         compiler_params=pltpu.CompilerParams(vmem_limit_bytes=limit),
         cost_estimate=cost,
@@ -323,22 +334,31 @@
     )(*args)
 
 
-def pack(plan, info, routes, tokens):
+def pack(plan, prefill_ranks, choice, local, weights, tokens):
     return call(
         lambda *refs: pack_kernel(plan, *refs),
         "pack",
         jax.ShapeDtypeStruct((plan.ranks, plan.chunk, LANE), BF16),
-        [SMEM, VMEM, HBM],
-        info,
-        routes,
+        [HBM] * 5,
+        prefill_ranks,
+        choice,
+        local,
+        weights,
         tokens,
-        scratch=[pltpu.VMEM((plan.rows, 3 * LANE), BF16), pltpu.SemaphoreType.DMA((2,))],
+        scratch=[
+            pltpu.SMEM(prefill_ranks.shape, I32),
+            pltpu.VMEM(choice.shape, I32),
+            pltpu.VMEM(local.shape, I32),
+            pltpu.VMEM(weights.shape, F32),
+            pltpu.VMEM((plan.rows, 3 * LANE), BF16),
+            pltpu.SemaphoreType.DMA((6,)),
+        ],
     )
 
 
 def compact(plan, info, received):
     return call(
-        lambda *refs: compact_kernel(plan, *refs),
+        lambda *refs: compact_kernel(plan, Info(refs[0]), *refs[1:]),
         "compact",
         (
             jax.ShapeDtypeStruct((plan.packed, LANE), BF16),
@@ -374,14 +394,14 @@
     )
 
 
-def combine_table(plan, info, routes):
-    return call(
-        lambda *refs: combine_table_kernel(plan, *refs),
+def combine_table(plan, info, choice):
+    return call(
+        lambda *refs: combine_table_kernel(plan, Info(refs[0]), *refs[1:]),
         "combine_table",
         jax.ShapeDtypeStruct((plan.rows, 3 * plan.ranks * plan.chunk), BF16),
         [SMEM, VMEM],
         info,
-        routes,
+        choice,
         flops=1 << 29,
     )
 
@@ -390,7 +410,7 @@
     hidden = w_gate.shape[0] * w_gate.shape[1]
     flat = [w.reshape(hidden, plan.width) for w in (w_gate, w_up, w_down)]
     return call(
-        lambda *refs: expert_kernel(plan, offsets, *refs),
+        lambda *refs: expert_kernel(plan, offsets, Info(refs[0]), *refs[1:]),
         "experts",
         jax.ShapeDtypeStruct((plan.lanes, plan.packed, LANE), BF16),
         [SMEM] + [VMEM] * (len(parts) + 4),
@@ -425,7 +445,7 @@
         "combine",
         (
             jax.ShapeDtypeStruct((plan.lanes, 3 * plan.own_rows, LANE), BF16),
-            jax.ShapeDtypeStruct((8, LANE), F32),
+            jax.ShapeDtypeStruct((1,), I32),
         ),
         [VMEM, VMEM],
         take,
@@ -450,7 +470,8 @@
     held = [packed, packed]
     for hop in range(1, lanes // 2 + 1):
         if hop > 1 and hop - 2 < len(beside):
-            held, value = lax.optimization_barrier((held, beside[hop - 2]))
+            first, value = lax.optimization_barrier((held[0], beside[hop - 2]))
+            held = [first, held[1]]
             values.append(value)
         got = [lax.ppermute(held[0], "tp", right)]
         offsets.append(-hop)
@@ -480,23 +501,17 @@
     sizes = (ranks, lax.axis_size("tp"), *tokens.shape, prefill)
     most = (ranks - prefill) * DEC_RANK
     plan, whole = Plan(*sizes, min(USUAL_DECODE, most)), Plan(*sizes, most)
-    places = jnp.stack([lax.axis_index("tp"), lax.axis_index("ep")]).astype(I32)
-    info = jnp.concatenate([places, prefill_ranks])
-    tables = (device_choice, local_expert, route_weight)
-    wide = sum(x.shape[1] for x in tables)
-    routes, at = 0.0, 0
-    for x in tables:
-        routes += jnp.pad(x.astype(F32), ((0, 0), (at, wide - at - x.shape[1])))
-        at += x.shape[1]
-    routes = routes.T
-    outgoing = pack(plan, info, routes, tokens)
+    stay = [prefill_ranks, device_choice.T, local_expert.T, route_weight.T, tokens]
+    stay = [pltpu.with_memory_space_constraint(x, pltpu.HBM) for x in stay]
+    outgoing = pack(plan, *stay)
     received = lax.all_to_all(outgoing, "ep", 0, 0, tiled=True)
-    take_in = combine_table(plan, info, routes)
+    received, info, choice = lax.optimization_barrier((received, stay[0], stay[1]))
+    take_in = combine_table(plan, info, choice)
     rest = (info, received, take_in, (w_gate, w_up, w_down))
     shares, over = through_experts(plan, *rest)
     rest, over = lax.optimization_barrier((rest, over))
     shares = lax.cond(
-        over[0, 0] > 0.0, lambda: through_experts(whole, *rest)[0], lambda: shares
+        over[0] > 0, lambda: through_experts(whole, *rest)[0], lambda: shares
     )
     shares = lax.all_to_all(shares, "tp", 0, 0, tiled=True)
     return finish(plan, shares)

time: 189 us -> 181 us (0.958)
  waiting for transfers between devices: 14.7 us -> 7.85 us
  blocking collectives: 134 us -> 138 us
  other arithmetic: 2.8 us -> 0 us
    ppermute x4, waiting for transfers between devices: 11.4 us -> 7.2 us  [gather_lanes(): got = [lax.ppermute(held[0], 'tp', right)]]
    all_to_all x1, blocking collectives: 30 us -> 33.5 us  [through_experts(): returned = lax.all_to_all(partial, 'tp', 0, 0, tiled=True)]
    ppermute x3, waiting for transfers between devices: 3.29 us -> 0.65 us  [gather_lanes(): got.append(lax.ppermute(held[1], 'tp', left))]
    ppermute x3, starting transfers between devices: 16.5 us -> 14.6 us  [gather_lanes(): got.append(lax.ppermute(held[1], 'tp', left))]
  transfers between devices with their start and end apart: 7 -> 7, of which waited for: 7 -> 4; matrix products, arithmetic and copies ran while one was open for 0% -> 0% of each run, Pallas kernels for 1% -> 1%
where the time goes in v5:
time: 181 us; the launch traced here: 180 us
  blocking collectives  138 us (76%)
  starting transfers between devices  24 us (13%)
  Pallas kernels  9.73 us (5%)
  waiting for transfers between devices  7.85 us (4%)
    all_to_all x1, blocking collectives, on_device(): received = lax.all_to_all(outgoing, 'ep', 0, 0, tiled=True)  66.2 us
    all_to_all x1, blocking collectives, through_experts(): returned = lax.all_to_all(partial, 'tp', 0, 0, tiled=True)  33.5 us
    all_to_all x1, blocking collectives, through_experts(): lax.all_to_all(spread(plan, take_out, needed, returned), 'ep', 0, 0, tile...  26.6 us
    ppermute x3, starting transfers between devices, gather_lanes(): got.append(lax.ppermute(held[1], 'tp', left))  14.6 us
    all_to_all x1, blocking collectives, on_device(): shares = lax.all_to_all(shares, 'tp', 0, 0, tiled=True)  11.2 us
    pallas_call x9, Pallas kernels, call(): pl.pallas_call(kernel, out_shape=out, in_specs=specs, out_specs=jax.tree....  9.73 us
    ppermute x4, starting transfers between devices, gather_lanes(): got = [lax.ppermute(held[0], 'tp', right)]  9.39 us
    ppermute x4, waiting for transfers between devices, gather_lanes(): got = [lax.ppermute(held[0], 'tp', right)]  7.2 us
  transfers between devices with their start and end apart: 7, of which 4 were waited for; matrix products, arithmetic and copies ran while one was open for 0% of the time, Pallas kernels for 1%

profile of v5, /device:TPU:80, one launch (start us, length us, event | category | flops | bytes accessed | tf_op | source)
XLA Modules:
  0.0 180.0 jit_solution(11445408541358826579)
XLA Ops:
  0.0 1.3 pack.1
  1.3 66.2 %all_to_all.30.refs_1_.refs_0_ = bf16[32,32,128]{2,1,0:T(8,128)(2,1)S(1)} all-to-all(bf16[32,32,128]{2,1,0:T(8,128)(2,1)S(1)} %pack.1), channel_id=1, replica_groups=mesh['groups'=2,'ep'=32,'tp'=8] {'ep'}, dimensions={0} | all-to-all | bytes 524288 | tf_op jit(solution)/shard_map/all_to_all | solution.py:507
  67.6 1.6 compact.3
  69.2 3.6 %collective-permute-start.7 = (bf16[560,128]{1,0:T(8,128)(2,1)S(1)}, bf16[560,128]{1,0:T(8,128)(2,1)S(1)}, u32[]{:S(2)}, u32[]{:S(2)}) collective-permute-start(bf16[560,128]{1,0:T(8,128)(2,1)S(1)} %get-tuple-element.61.refs_1_), channel_id=1, source_target_pairs={{0,1},{1,2},{2,3},{3,4},{4,5},{5,6},{6,7},{7,0},{8,9},{9,10},{10,1... | collective-permute-start | bytes 430088 | tf_op jit(solution)/shard_map/ppermute | solution.py:476
  72.7 4.2 %collective-permute-start.10 = (bf16[560,128]{1,0:T(8,128)(2,1)S(1)}, bf16[560,128]{1,0:T(8,128)(2,1)S(1)}, u32[]{:S(2)}, u32[]{:S(2)}) collective-permute-start(bf16[560,128]{1,0:T(8,128)(2,1)S(1)} %get-tuple-element.61.refs_1_), channel_id=1, source_target_pairs={{0,7},{1,0},{2,1},{3,2},{4,3},{5,4},{6,5},{7,6},{8,15},{9,8},{10,9... | collective-permute-start | bytes 430088 | tf_op jit(solution)/shard_map/ppermute | solution.py:479
  76.9 0.9 weights.3.refs_9_
  77.7 1.0 collective-permute-done.7.refs_2_
  78.8 1.9 %collective-permute-start.8 = (bf16[560,128]{1,0:T(8,128)(2,1)S(1)}, bf16[560,128]{1,0:T(8,128)(2,1)S(1)}, u32[]{:S(2)}, u32[]{:S(2)}) collective-permute-start(bf16[560,128]{1,0:T(8,128)(2,1)S(1)} %collective-permute-done.7.refs_2_), channel_id=1, source_target_pairs={{0,1},{1,2},{2,3},{3,4},{4,5},{5,6},{6,7},{7,0},{8,9},{9,10},{10,1... | collective-permute-start | bytes 430088 | tf_op jit(solution)/shard_map/ppermute | solution.py:476
  80.7 0.4 spread_table.3.refs_0_
  81.1 5.3 %collective-permute-start.11 = (bf16[560,128]{1,0:T(8,128)(2,1)S(1)}, bf16[560,128]{1,0:T(8,128)(2,1)S(1)}, u32[]{:S(2)}, u32[]{:S(2)}) collective-permute-start(bf16[560,128]{1,0:T(8,128)(2,1)S(1)} %collective-permute-done.10.refs_3_), channel_id=1, source_target_pairs={{0,7},{1,0},{2,1},{3,2},{4,3},{5,4},{6,5},{7,6},{8,15},{9,8},{10,9... | collective-permute-start | bytes 430088 | tf_op jit(solution)/shard_map/ppermute | solution.py:479
  86.4 0.6 collective-permute-done.8.refs_4_
  87.0 1.9 %collective-permute-start.9 = (bf16[560,128]{1,0:T(8,128)(2,1)S(1)}, bf16[560,128]{1,0:T(8,128)(2,1)S(1)}, u32[]{:S(2)}, u32[]{:S(2)}) collective-permute-start(bf16[560,128]{1,0:T(8,128)(2,1)S(1)} %collective-permute-done.8.refs_4_), channel_id=1, source_target_pairs={{0,1},{1,2},{2,3},{3,4},{4,5},{5,6},{6,7},{7,0},{8,9},{9,10},{10,1... | collective-permute-start | bytes 430088 | tf_op jit(solution)/shard_map/ppermute | solution.py:476
  88.9 1.2 combine_table.1.refs_0_
  90.1 5.2 %collective-permute-start.12 = (bf16[560,128]{1,0:T(8,128)(2,1)S(1)}, bf16[560,128]{1,0:T(8,128)(2,1)S(1)}, u32[]{:S(2)}, u32[]{:S(2)}) collective-permute-start(bf16[560,128]{1,0:T(8,128)(2,1)S(1)} %collective-permute-done.11.refs_5_), channel_id=1, source_target_pairs={{0,7},{1,0},{2,1},{3,2},{4,3},{5,4},{6,5},{7,6},{8,15},{9,8},{10,9... | collective-permute-start | bytes 430088 | tf_op jit(solution)/shard_map/ppermute | solution.py:479
  95.3 2.0 %collective-permute-start.13 = (bf16[560,128]{1,0:T(8,128)(2,1)S(1)}, bf16[560,128]{1,0:T(8,128)(2,1)S(1)}, u32[]{:S(2)}, u32[]{:S(2)}) collective-permute-start(bf16[560,128]{1,0:T(8,128)(2,1)S(1)} %collective-permute-done.9.refs_6_), channel_id=1, source_target_pairs={{0,1},{1,2},{2,3},{3,4},{4,5},{5,6},{6,7},{7,0},{8,9},{9,10},{10,1... | collective-permute-start | bytes 430088 | tf_op jit(solution)/shard_map/ppermute | solution.py:476
  97.3 0.6 collective-permute-done.12.refs_7_
  97.9 5.6 %collective-permute-done.13.refs_8_ = bf16[560,128]{1,0:T(8,128)(2,1)S(1)} collective-permute-done((bf16[560,128]{1,0:T(8,128)(2,1)S(1)}, bf16[560,128]{1,0:T(8,128)(2,1)S(1)}, u32[]{:S(2)}, u32[]{:S(2)}) %collective-permute-start.13) | collective-permute-done | bytes 143392 | tf_op jit(solution)/shard_map/ppermute | solution.py:476
  103.5 2.2 %experts.3 = bf16[8,560,128]{2,1,0:T(8,128)(2,1)S(1)} custom-call(s32[16]{0:T(128)} %refs_0_.4, bf16[560,128]{1,0:T(8,128)(2,1)S(1)} %get-tuple-element.61.refs_1_, bf16[560,128]{1,0:T(8,128)(2,1)S(1)} %collective-permute-done.7.refs_2_, bf16[560,128]{1,0:T(8,128)(2,1)S(1)} %collective-permute-done.10.refs_3_, ...), custom_call_target="tpu_custom_call" | custom-call | tf_op jit(solution)/shard_map/experts/pallas_call | solution.py:324
  105.7 33.5 %all_to_all.31.refs_2_ = bf16[8,560,128]{2,1,0:T(8,128)(2,1)S(1)} all-to-all(bf16[8,560,128]{2,1,0:T(8,128)(2,1)S(1)} %experts.3), channel_id=1, replica_groups=mesh['groups'=2,'ep'=32,'tp'=8] {'tp'}, dimensions={0} | all-to-all | bytes 2293760 | tf_op jit(solution)/shard_map/all_to_all | solution.py:492
  139.2 0.6 spread.3
  139.8 26.6 %all_to_all.32.refs_1_ = bf16[32,32,128]{2,1,0:T(8,128)(2,1)S(1)} all-to-all(bf16[32,32,128]{2,1,0:T(8,128)(2,1)S(1)} %spread.3), channel_id=1, replica_groups=mesh['groups'=2,'ep'=32,'tp'=8] {'ep'}, dimensions={0} | all-to-all | bytes 524288 | tf_op jit(solution)/shard_map/all_to_all | solution.py:493
  166.5 1.0 combine.3
  168.2 11.2 %all_to_all.33.refs_0_ = bf16[8,48,128]{2,1,0:T(8,128)(2,1)S(1)} all-to-all(bf16[8,48,128]{2,1,0:T(8,128)(2,1)S(1)} %get-tuple-element.79), channel_id=1, replica_groups=mesh['groups'=2,'ep'=32,'tp'=8] {'tp'}, dimensions={0} | all-to-all | bytes 196608 | tf_op jit(solution)/shard_map/all_to_all | solution.py:516
  179.3 0.7 finish.1
  (10 shorter events, 0.0 us)
Async XLA Ops:
  69.2 9.6 %collective-permute-start.7 = (bf16[560,128]{1,0:T(8,128)(2,1)S(1)}, bf16[560,128]{1,0:T(8,128)(2,1)S(1)}, u32[]{:S(2)}, u32[]{:S(2)}) collective-permute-start(bf16[560,128]{1,0:T(8,128)(2,1)S(1)} %get-tuple-element.61.refs_1_), channel_id=1, source_target_pairs={{0,1},{1,2},{2,3},{3,4},{4,5},{5,6},{6,7},{7,0},{8,9},{9,10},{10,1... | collective-permute-start | bytes 430088 | tf_op jit(solution)/shard_map/ppermute | solution.py:476
  72.7 8.4 %collective-permute-start.10 = (bf16[560,128]{1,0:T(8,128)(2,1)S(1)}, bf16[560,128]{1,0:T(8,128)(2,1)S(1)}, u32[]{:S(2)}, u32[]{:S(2)}) collective-permute-start(bf16[560,128]{1,0:T(8,128)(2,1)S(1)} %get-tuple-element.61.refs_1_), channel_id=1, source_target_pairs={{0,7},{1,0},{2,1},{3,2},{4,3},{5,4},{6,5},{7,6},{8,15},{9,8},{10,9... | collective-permute-start | bytes 430088 | tf_op jit(solution)/shard_map/ppermute | solution.py:479
  78.8 8.2 %collective-permute-start.8 = (bf16[560,128]{1,0:T(8,128)(2,1)S(1)}, bf16[560,128]{1,0:T(8,128)(2,1)S(1)}, u32[]{:S(2)}, u32[]{:S(2)}) collective-permute-start(bf16[560,128]{1,0:T(8,128)(2,1)S(1)} %collective-permute-done.7.refs_2_), channel_id=1, source_target_pairs={{0,1},{1,2},{2,3},{3,4},{4,5},{5,6},{6,7},{7,0},{8,9},{9,10},{10,1... | collective-permute-start | bytes 430088 | tf_op jit(solution)/shard_map/ppermute | solution.py:476
  80.7 22.8 %copy-start.1 = (bf16[2,128,2560]{2,1,0:T(8,128)(2,1)S(1)}, bf16[2,128,2560]{2,1,0:T(8,128)(2,1)}, u32[]{:S(2)}) copy-start(bf16[2,128,2560]{2,1,0:T(8,128)(2,1)} %param.16) | copy-start | bytes 3932164
  80.7 22.8 %copy-start.2 = (bf16[2,128,2560]{2,1,0:T(8,128)(2,1)S(1)}, bf16[2,128,2560]{2,1,0:T(8,128)(2,1)}, u32[]{:S(2)}) copy-start(bf16[2,128,2560]{2,1,0:T(8,128)(2,1)} %param.17) | copy-start | bytes 3932164
  81.1 22.4 %copy-start = (bf16[2,128,2560]{2,1,0:T(8,128)(2,1)S(1)}, bf16[2,128,2560]{2,1,0:T(8,128)(2,1)}, u32[]{:S(2)}) copy-start(bf16[2,128,2560]{2,1,0:T(8,128)(2,1)} %param.15) | copy-start | bytes 3932164
  81.1 9.0 %collective-permute-start.11 = (bf16[560,128]{1,0:T(8,128)(2,1)S(1)}, bf16[560,128]{1,0:T(8,128)(2,1)S(1)}, u32[]{:S(2)}, u32[]{:S(2)}) collective-permute-start(bf16[560,128]{1,0:T(8,128)(2,1)S(1)} %collective-permute-done.10.refs_3_), channel_id=1, source_target_pairs={{0,7},{1,0},{2,1},{3,2},{4,3},{5,4},{6,5},{7,6},{8,15},{9,8},{10,9... | collective-permute-start | bytes 430088 | tf_op jit(solution)/shard_map/ppermute | solution.py:479
  87.0 8.3 %collective-permute-start.9 = (bf16[560,128]{1,0:T(8,128)(2,1)S(1)}, bf16[560,128]{1,0:T(8,128)(2,1)S(1)}, u32[]{:S(2)}, u32[]{:S(2)}) collective-permute-start(bf16[560,128]{1,0:T(8,128)(2,1)S(1)} %collective-permute-done.8.refs_4_), channel_id=1, source_target_pairs={{0,1},{1,2},{2,3},{3,4},{4,5},{5,6},{6,7},{7,0},{8,9},{9,10},{10,1... | collective-permute-start | bytes 430088 | tf_op jit(solution)/shard_map/ppermute | solution.py:476
  90.1 7.8 %collective-permute-start.12 = (bf16[560,128]{1,0:T(8,128)(2,1)S(1)}, bf16[560,128]{1,0:T(8,128)(2,1)S(1)}, u32[]{:S(2)}, u32[]{:S(2)}) collective-permute-start(bf16[560,128]{1,0:T(8,128)(2,1)S(1)} %collective-permute-done.11.refs_5_), channel_id=1, source_target_pairs={{0,7},{1,0},{2,1},{3,2},{4,3},{5,4},{6,5},{7,6},{8,15},{9,8},{10,9... | collective-permute-start | bytes 430088 | tf_op jit(solution)/shard_map/ppermute | solution.py:479
  95.3 8.2 %collective-permute-start.13 = (bf16[560,128]{1,0:T(8,128)(2,1)S(1)}, bf16[560,128]{1,0:T(8,128)(2,1)S(1)}, u32[]{:S(2)}, u32[]{:S(2)}) collective-permute-start(bf16[560,128]{1,0:T(8,128)(2,1)S(1)} %collective-permute-done.9.refs_6_), channel_id=1, source_target_pairs={{0,1},{1,2},{2,3},{3,4},{4,5},{5,6},{6,7},{7,0},{8,9},{9,10},{10,1... | collective-permute-start | bytes 430088 | tf_op jit(solution)/shard_map/ppermute | solution.py:476

commit v6 on v5

--- a/solution.py
+++ b/solution.py
@@ -242,10 +242,10 @@
 def expert_kernel(plan, offsets, info_ref, *refs):
     n = len(offsets)
     weight_ref, wg, wu, wd, out_ref, x_ref, h_ref = refs[n:]
-    me = info_ref[0]
+    me, way = info_ref[0], 1 - 2 * lax.rem(info_ref[1], 2)
     lanes, half, slots = plan.lanes, plan.half, plan.slots
     for offset, part in zip(offsets, refs):
-        lane = lax.rem(me + offset + lanes, lanes)
+        lane = lax.rem(me + way * offset + lanes, lanes)
         first = pl.multiple_of(lane * (2 * LANE), LANE)
         tail = pl.multiple_of((2 * lanes + lane // 2) * LANE, LANE)
         start = pl.multiple_of(lax.rem(lane, 2) * half, 8)
@@ -464,8 +464,19 @@
 
 
 def gather_lanes(packed, lanes, beside):
-    right = [(i, (i + 1) % lanes) for i in range(lanes)]
-    left = [(i, (i - 1) % lanes) for i in range(lanes)]
+    ranks = lax.axis_size("ep")
+    ways = []
+    for way in (1, -1):
+        steps = [way if rank % 2 == 0 else -way for rank in range(ranks)]
+        ways.append(
+            [
+                (rank * lanes + i, rank * lanes + (i + steps[rank]) % lanes)
+                for rank in range(ranks)
+                for i in range(lanes)
+            ]
+        )
+    right, left = ways
+    axes = ("ep", "tp")
     parts, offsets, values = [packed], [0], []
     held = [packed, packed]
     for hop in range(1, lanes // 2 + 1):
@@ -473,10 +484,10 @@
             first, value = lax.optimization_barrier((held[0], beside[hop - 2]))
             held = [first, held[1]]
             values.append(value)
-        got = [lax.ppermute(held[0], "tp", right)]
+        got = [lax.ppermute(held[0], axes, right)]
         offsets.append(-hop)
         if hop < lanes // 2:
-            got.append(lax.ppermute(held[1], "tp", left))
+            got.append(lax.ppermute(held[1], axes, left))
             offsets.append(hop)
         parts += got
         held = got

time: 181 us -> 178 us (0.983)
  blocking collectives: 138 us -> 136 us
where the time goes in v6:
time: 178 us; the launch traced here: 177 us
  blocking collectives  136 us (76%)
  starting transfers between devices  24 us (13%)
  Pallas kernels  9.75 us (5%)
  waiting for transfers between devices  7.08 us (4%)
    all_to_all x1, blocking collectives, on_device(): received = lax.all_to_all(outgoing, 'ep', 0, 0, tiled=True)  66.2 us
    all_to_all x1, blocking collectives, through_experts(): returned = lax.all_to_all(partial, 'tp', 0, 0, tiled=True)  32.2 us
    all_to_all x1, blocking collectives, through_experts(): lax.all_to_all(spread(plan, take_out, needed, returned), 'ep', 0, 0, tile...  26.1 us
    ppermute x3, starting transfers between devices, gather_lanes(): got.append(lax.ppermute(held[1], axes, left))  14.6 us
    all_to_all x1, blocking collectives, on_device(): shares = lax.all_to_all(shares, 'tp', 0, 0, tiled=True)  11.2 us
    pallas_call x9, Pallas kernels, call(): pl.pallas_call(kernel, out_shape=out, in_specs=specs, out_specs=jax.tree....  9.75 us
    ppermute x4, starting transfers between devices, gather_lanes(): got = [lax.ppermute(held[0], axes, right)]  9.39 us
    ppermute x4, waiting for transfers between devices, gather_lanes(): got = [lax.ppermute(held[0], axes, right)]  6.43 us
  transfers between devices with their start and end apart: 7, of which 4 were waited for; matrix products, arithmetic and copies ran while one was open for 0% of the time, Pallas kernels for 1%

profile of v6, /device:TPU:80, one launch (start us, length us, event | category | flops | bytes accessed | tf_op | source)
XLA Modules:
  0.0 177.4 jit_solution(5632565377422693059)
XLA Ops:
  0.0 1.3 pack.1
  1.3 66.2 %all_to_all.30.refs_1_.refs_0_ = bf16[32,32,128]{2,1,0:T(8,128)(2,1)S(1)} all-to-all(bf16[32,32,128]{2,1,0:T(8,128)(2,1)S(1)} %pack.1), channel_id=1, replica_groups=mesh['groups'=2,'ep'=32,'tp'=8] {'ep'}, dimensions={0} | all-to-all | bytes 524288 | tf_op jit(solution)/shard_map/all_to_all | solution.py:518
  67.6 1.6 compact.3
  69.2 3.6 %collective-permute-start.7 = (bf16[560,128]{1,0:T(8,128)(2,1)S(1)}, bf16[560,128]{1,0:T(8,128)(2,1)S(1)}, u32[]{:S(2)}, u32[]{:S(2)}) collective-permute-start(bf16[560,128]{1,0:T(8,128)(2,1)S(1)} %get-tuple-element.61.refs_1_), channel_id=1, source_target_pairs={{0,1},{1,2},{2,3},{3,4},{4,5},{5,6},{6,7},{7,0},{8,15},{9,8},{10,9... | collective-permute-start | bytes 430088 | tf_op jit(solution)/shard_map/ppermute | solution.py:487
  72.7 4.2 %collective-permute-start.10 = (bf16[560,128]{1,0:T(8,128)(2,1)S(1)}, bf16[560,128]{1,0:T(8,128)(2,1)S(1)}, u32[]{:S(2)}, u32[]{:S(2)}) collective-permute-start(bf16[560,128]{1,0:T(8,128)(2,1)S(1)} %get-tuple-element.61.refs_1_), channel_id=1, source_target_pairs={{0,7},{1,0},{2,1},{3,2},{4,3},{5,4},{6,5},{7,6},{8,9},{9,10},{10,1... | collective-permute-start | bytes 430088 | tf_op jit(solution)/shard_map/ppermute | solution.py:490
  76.9 0.9 weights.3.refs_9_
  77.7 0.2 collective-permute-done.7.refs_2_
  78.0 1.9 %collective-permute-start.8 = (bf16[560,128]{1,0:T(8,128)(2,1)S(1)}, bf16[560,128]{1,0:T(8,128)(2,1)S(1)}, u32[]{:S(2)}, u32[]{:S(2)}) collective-permute-start(bf16[560,128]{1,0:T(8,128)(2,1)S(1)} %collective-permute-done.7.refs_2_), channel_id=1, source_target_pairs={{0,1},{1,2},{2,3},{3,4},{4,5},{5,6},{6,7},{7,0},{8,15},{9,8},{10,9... | collective-permute-start | bytes 430088 | tf_op jit(solution)/shard_map/ppermute | solution.py:487
  80.0 0.4 spread_table.3.refs_0_
  80.3 5.3 %collective-permute-start.11 = (bf16[560,128]{1,0:T(8,128)(2,1)S(1)}, bf16[560,128]{1,0:T(8,128)(2,1)S(1)}, u32[]{:S(2)}, u32[]{:S(2)}) collective-permute-start(bf16[560,128]{1,0:T(8,128)(2,1)S(1)} %collective-permute-done.10.refs_3_), channel_id=1, source_target_pairs={{0,7},{1,0},{2,1},{3,2},{4,3},{5,4},{6,5},{7,6},{8,9},{9,10},{10,1... | collective-permute-start | bytes 430088 | tf_op jit(solution)/shard_map/ppermute | solution.py:490
  85.6 0.6 collective-permute-done.8.refs_4_
  86.2 1.9 %collective-permute-start.9 = (bf16[560,128]{1,0:T(8,128)(2,1)S(1)}, bf16[560,128]{1,0:T(8,128)(2,1)S(1)}, u32[]{:S(2)}, u32[]{:S(2)}) collective-permute-start(bf16[560,128]{1,0:T(8,128)(2,1)S(1)} %collective-permute-done.8.refs_4_), channel_id=1, source_target_pairs={{0,1},{1,2},{2,3},{3,4},{4,5},{5,6},{6,7},{7,0},{8,15},{9,8},{10,9... | collective-permute-start | bytes 430088 | tf_op jit(solution)/shard_map/ppermute | solution.py:487
  88.2 1.2 combine_table.1.refs_0_
  89.4 5.2 %collective-permute-start.12 = (bf16[560,128]{1,0:T(8,128)(2,1)S(1)}, bf16[560,128]{1,0:T(8,128)(2,1)S(1)}, u32[]{:S(2)}, u32[]{:S(2)}) collective-permute-start(bf16[560,128]{1,0:T(8,128)(2,1)S(1)} %collective-permute-done.11.refs_5_), channel_id=1, source_target_pairs={{0,7},{1,0},{2,1},{3,2},{4,3},{5,4},{6,5},{7,6},{8,9},{9,10},{10,1... | collective-permute-start | bytes 430088 | tf_op jit(solution)/shard_map/ppermute | solution.py:490
  94.5 2.0 %collective-permute-start.13 = (bf16[560,128]{1,0:T(8,128)(2,1)S(1)}, bf16[560,128]{1,0:T(8,128)(2,1)S(1)}, u32[]{:S(2)}, u32[]{:S(2)}) collective-permute-start(bf16[560,128]{1,0:T(8,128)(2,1)S(1)} %collective-permute-done.9.refs_6_), channel_id=1, source_target_pairs={{0,1},{1,2},{2,3},{3,4},{4,5},{5,6},{6,7},{7,0},{8,15},{9,8},{10,9... | collective-permute-start | bytes 430088 | tf_op jit(solution)/shard_map/ppermute | solution.py:487
  96.5 0.6 collective-permute-done.12.refs_7_
  97.1 5.6 %collective-permute-done.13.refs_8_ = bf16[560,128]{1,0:T(8,128)(2,1)S(1)} collective-permute-done((bf16[560,128]{1,0:T(8,128)(2,1)S(1)}, bf16[560,128]{1,0:T(8,128)(2,1)S(1)}, u32[]{:S(2)}, u32[]{:S(2)}) %collective-permute-start.13) | collective-permute-done | bytes 143392 | tf_op jit(solution)/shard_map/ppermute | solution.py:487
  102.8 2.2 %experts.3 = bf16[8,560,128]{2,1,0:T(8,128)(2,1)S(1)} custom-call(s32[16]{0:T(128)} %refs_0_.4, bf16[560,128]{1,0:T(8,128)(2,1)S(1)} %get-tuple-element.61.refs_1_, bf16[560,128]{1,0:T(8,128)(2,1)S(1)} %collective-permute-done.7.refs_2_, bf16[560,128]{1,0:T(8,128)(2,1)S(1)} %collective-permute-done.10.refs_3_, ...), custom_call_target="tpu_custom_call" | custom-call | tf_op jit(solution)/shard_map/experts/pallas_call | solution.py:324
  105.0 32.2 %all_to_all.31.refs_2_ = bf16[8,560,128]{2,1,0:T(8,128)(2,1)S(1)} all-to-all(bf16[8,560,128]{2,1,0:T(8,128)(2,1)S(1)} %experts.3), channel_id=1, replica_groups=mesh['groups'=2,'ep'=32,'tp'=8] {'tp'}, dimensions={0} | all-to-all | bytes 2293760 | tf_op jit(solution)/shard_map/all_to_all | solution.py:503
  137.1 0.6 spread.3
  137.8 26.1 %all_to_all.32.refs_1_ = bf16[32,32,128]{2,1,0:T(8,128)(2,1)S(1)} all-to-all(bf16[32,32,128]{2,1,0:T(8,128)(2,1)S(1)} %spread.3), channel_id=1, replica_groups=mesh['groups'=2,'ep'=32,'tp'=8] {'ep'}, dimensions={0} | all-to-all | bytes 524288 | tf_op jit(solution)/shard_map/all_to_all | solution.py:504
  163.8 1.0 combine.3
  165.5 11.2 %all_to_all.33.refs_0_ = bf16[8,48,128]{2,1,0:T(8,128)(2,1)S(1)} all-to-all(bf16[8,48,128]{2,1,0:T(8,128)(2,1)S(1)} %get-tuple-element.79), channel_id=1, replica_groups=mesh['groups'=2,'ep'=32,'tp'=8] {'tp'}, dimensions={0} | all-to-all | bytes 196608 | tf_op jit(solution)/shard_map/all_to_all | solution.py:527
  176.7 0.7 finish.1
  (10 shorter events, 0.0 us)
Async XLA Ops:
  69.2 8.8 %collective-permute-start.7 = (bf16[560,128]{1,0:T(8,128)(2,1)S(1)}, bf16[560,128]{1,0:T(8,128)(2,1)S(1)}, u32[]{:S(2)}, u32[]{:S(2)}) collective-permute-start(bf16[560,128]{1,0:T(8,128)(2,1)S(1)} %get-tuple-element.61.refs_1_), channel_id=1, source_target_pairs={{0,1},{1,2},{2,3},{3,4},{4,5},{5,6},{6,7},{7,0},{8,15},{9,8},{10,9... | collective-permute-start | bytes 430088 | tf_op jit(solution)/shard_map/ppermute | solution.py:487
  72.7 7.6 %collective-permute-start.10 = (bf16[560,128]{1,0:T(8,128)(2,1)S(1)}, bf16[560,128]{1,0:T(8,128)(2,1)S(1)}, u32[]{:S(2)}, u32[]{:S(2)}) collective-permute-start(bf16[560,128]{1,0:T(8,128)(2,1)S(1)} %get-tuple-element.61.refs_1_), channel_id=1, source_target_pairs={{0,7},{1,0},{2,1},{3,2},{4,3},{5,4},{6,5},{7,6},{8,9},{9,10},{10,1... | collective-permute-start | bytes 430088 | tf_op jit(solution)/shard_map/ppermute | solution.py:490
  78.0 8.2 %collective-permute-start.8 = (bf16[560,128]{1,0:T(8,128)(2,1)S(1)}, bf16[560,128]{1,0:T(8,128)(2,1)S(1)}, u32[]{:S(2)}, u32[]{:S(2)}) collective-permute-start(bf16[560,128]{1,0:T(8,128)(2,1)S(1)} %collective-permute-done.7.refs_2_), channel_id=1, source_target_pairs={{0,1},{1,2},{2,3},{3,4},{4,5},{5,6},{6,7},{7,0},{8,15},{9,8},{10,9... | collective-permute-start | bytes 430088 | tf_op jit(solution)/shard_map/ppermute | solution.py:487
  79.9 22.8 %copy-start.1 = (bf16[2,128,2560]{2,1,0:T(8,128)(2,1)S(1)}, bf16[2,128,2560]{2,1,0:T(8,128)(2,1)}, u32[]{:S(2)}) copy-start(bf16[2,128,2560]{2,1,0:T(8,128)(2,1)} %param.16) | copy-start | bytes 3932164
  79.9 22.8 %copy-start.2 = (bf16[2,128,2560]{2,1,0:T(8,128)(2,1)S(1)}, bf16[2,128,2560]{2,1,0:T(8,128)(2,1)}, u32[]{:S(2)}) copy-start(bf16[2,128,2560]{2,1,0:T(8,128)(2,1)} %param.17) | copy-start | bytes 3932164
  80.3 22.4 %copy-start = (bf16[2,128,2560]{2,1,0:T(8,128)(2,1)S(1)}, bf16[2,128,2560]{2,1,0:T(8,128)(2,1)}, u32[]{:S(2)}) copy-start(bf16[2,128,2560]{2,1,0:T(8,128)(2,1)} %param.15) | copy-start | bytes 3932164
  80.3 9.0 %collective-permute-start.11 = (bf16[560,128]{1,0:T(8,128)(2,1)S(1)}, bf16[560,128]{1,0:T(8,128)(2,1)S(1)}, u32[]{:S(2)}, u32[]{:S(2)}) collective-permute-start(bf16[560,128]{1,0:T(8,128)(2,1)S(1)} %collective-permute-done.10.refs_3_), channel_id=1, source_target_pairs={{0,7},{1,0},{2,1},{3,2},{4,3},{5,4},{6,5},{7,6},{8,9},{9,10},{10,1... | collective-permute-start | bytes 430088 | tf_op jit(solution)/shard_map/ppermute | solution.py:490
  86.2 8.3 %collective-permute-start.9 = (bf16[560,128]{1,0:T(8,128)(2,1)S(1)}, bf16[560,128]{1,0:T(8,128)(2,1)S(1)}, u32[]{:S(2)}, u32[]{:S(2)}) collective-permute-start(bf16[560,128]{1,0:T(8,128)(2,1)S(1)} %collective-permute-done.8.refs_4_), channel_id=1, source_target_pairs={{0,1},{1,2},{2,3},{3,4},{4,5},{5,6},{6,7},{7,0},{8,15},{9,8},{10,9... | collective-permute-start | bytes 430088 | tf_op jit(solution)/shard_map/ppermute | solution.py:487
  89.4 7.8 %collective-permute-start.12 = (bf16[560,128]{1,0:T(8,128)(2,1)S(1)}, bf16[560,128]{1,0:T(8,128)(2,1)S(1)}, u32[]{:S(2)}, u32[]{:S(2)}) collective-permute-start(bf16[560,128]{1,0:T(8,128)(2,1)S(1)} %collective-permute-done.11.refs_5_), channel_id=1, source_target_pairs={{0,7},{1,0},{2,1},{3,2},{4,3},{5,4},{6,5},{7,6},{8,9},{9,10},{10,1... | collective-permute-start | bytes 430088 | tf_op jit(solution)/shard_map/ppermute | solution.py:490
  94.5 8.2 %collective-permute-start.13 = (bf16[560,128]{1,0:T(8,128)(2,1)S(1)}, bf16[560,128]{1,0:T(8,128)(2,1)S(1)}, u32[]{:S(2)}, u32[]{:S(2)}) collective-permute-start(bf16[560,128]{1,0:T(8,128)(2,1)S(1)} %collective-permute-done.9.refs_6_), channel_id=1, source_target_pairs={{0,1},{1,2},{2,3},{3,4},{4,5},{5,6},{6,7},{7,0},{8,15},{9,8},{10,9... | collective-permute-start | bytes 430088 | tf_op jit(solution)/shard_map/ppermute | solution.py:487

commit v7 on v6

--- a/solution.py
+++ b/solution.py
@@ -239,23 +239,48 @@
         combine_ref[:, b * total : (b + 1) * total] = one_hot(match & (block == b))
 
 
-def expert_kernel(plan, offsets, info_ref, *refs):
+def share_columns(plan, info_ref, offset):
+    way = 1 - 2 * lax.rem(info_ref[1], 2)
+    lane = lax.rem(info_ref[0] + way * offset + plan.lanes, plan.lanes)
+    first = pl.multiple_of(lane * (2 * LANE), LANE)
+    tail = pl.multiple_of((2 * plan.lanes + lane // 2) * LANE, LANE)
+    start = pl.multiple_of(lax.rem(lane, 2) * plan.half, 8)
+    return first, tail, pl.ds(start, plan.half)
+
+
+TURNED = (((1,), (1,)), ((), ()))
+
+
+def early_kernel(plan, offsets, late, info_ref, *refs):
     n = len(offsets)
-    weight_ref, wg, wu, wd, out_ref, x_ref, h_ref = refs[n:]
-    me, way = info_ref[0], 1 - 2 * lax.rem(info_ref[1], 2)
+    wg, wu, gate_ref, up_ref, x_ref = refs[n:]
+    half, slots = plan.half, plan.slots
+    for offset, part in zip(offsets + [late], refs[:n] + (None,)):
+        first, tail, rows = share_columns(plan, info_ref, offset)
+        if part is None:
+            x_ref[:, pl.ds(first, 2 * LANE)] = jnp.zeros((slots, 2 * LANE), BF16)
+            x_ref[rows, pl.ds(tail, LANE)] = jnp.zeros((half, LANE), BF16)
+        else:
+            x_ref[:, pl.ds(first, LANE)] = part[0:slots, :]
+            x_ref[:, pl.ds(pl.multiple_of(first + LANE, LANE), LANE)] = part[slots : 2 * slots, :]
+            x_ref[rows, pl.ds(tail, LANE)] = part[2 * slots : 2 * slots + half, :]
+    x = x_ref[...]
+    gate_ref[...] = lax.dot_general(x, wg[...], TURNED, preferred_element_type=F32)
+    up_ref[...] = lax.dot_general(x, wu[...], TURNED, preferred_element_type=F32)
+
+
+def expert_kernel(plan, late, info_ref, part, gate_ref, up_ref, weight_ref, wg, wu, wd, out_ref, x_ref, h_ref):
     lanes, half, slots = plan.lanes, plan.half, plan.slots
-    for offset, part in zip(offsets, refs):
-        lane = lax.rem(me + way * offset + lanes, lanes)
-        first = pl.multiple_of(lane * (2 * LANE), LANE)
-        tail = pl.multiple_of((2 * lanes + lane // 2) * LANE, LANE)
-        start = pl.multiple_of(lax.rem(lane, 2) * half, 8)
-        x_ref[:, pl.ds(first, LANE)] = part[0:slots, :]
-        x_ref[:, pl.ds(pl.multiple_of(first + LANE, LANE), LANE)] = part[slots : 2 * slots, :]
-        x_ref[pl.ds(start, half), pl.ds(tail, LANE)] = part[2 * slots : 2 * slots + half, :]
-    turned = (((1,), (1,)), ((), ()))
-    x = x_ref[...]
-    gate = lax.dot_general(x, wg[...], turned, preferred_element_type=F32)
-    up = lax.dot_general(x, wu[...], turned, preferred_element_type=F32)
+    first, tail, rows = share_columns(plan, info_ref, late)
+    x_ref[:, 0:LANE] = part[0:slots, :]
+    x_ref[:, LANE : 2 * LANE] = part[slots : 2 * slots, :]
+    x_ref[:, 2 * LANE : 3 * LANE] = jnp.zeros((slots, LANE), BF16)
+    x_ref[rows, 2 * LANE : 3 * LANE] = part[2 * slots : 2 * slots + half, :]
+    gate, up = gate_ref[...], up_ref[...]
+    for at, columns in ((0, pl.ds(first, 2 * LANE)), (2 * LANE, pl.ds(tail, LANE))):
+        x = x_ref[:, at : at + columns.size]
+        gate += lax.dot_general(x, wg[:, columns], TURNED, preferred_element_type=F32)
+        up += lax.dot_general(x, wu[:, columns], TURNED, preferred_element_type=F32)
     hidden = gate / (1.0 + jnp.exp(-gate)) * up * weight_ref[...]
     h_ref[...] = hidden.astype(BF16)
     for lane in range(lanes):
@@ -408,21 +433,38 @@
 
 def experts(plan, offsets, info, parts, weights, w_gate, w_up, w_down):
     hidden = w_gate.shape[0] * w_gate.shape[1]
-    flat = [w.reshape(hidden, plan.width) for w in (w_gate, w_up, w_down)]
-    return call(
-        lambda *refs: expert_kernel(plan, offsets, Info(refs[0]), *refs[1:]),
+    w_gate, w_up, w_down = [w.reshape(hidden, plan.width) for w in (w_gate, w_up, w_down)]
+    late = offsets[-1]
+    product = jax.ShapeDtypeStruct((plan.slots, hidden), F32)
+    gate, up = call(
+        lambda *refs: early_kernel(plan, offsets[:-1], late, Info(refs[0]), *refs[1:]),
+        "early",
+        (product, product),
+        [SMEM] + [VMEM] * (len(parts) + 1),
+        info,
+        *parts[:-1],
+        w_gate,
+        w_up,
+        scratch=[pltpu.VMEM((plan.slots, plan.width), BF16)],
+        flops=1 << 29,
+    )
+    return call(
+        lambda *refs: expert_kernel(plan, late, Info(refs[0]), *refs[1:]),
         "experts",
         jax.ShapeDtypeStruct((plan.lanes, plan.packed, LANE), BF16),
-        [SMEM] + [VMEM] * (len(parts) + 4),
+        [SMEM] + [VMEM] * 7,
         info,
-        *parts,
+        parts[-1],
+        gate,
+        up,
         weights,
-        *flat,
+        w_gate,
+        w_up,
+        w_down,
         scratch=[
-            pltpu.VMEM((plan.slots, plan.width), BF16),
+            pltpu.VMEM((plan.slots, 3 * LANE), BF16),
             pltpu.VMEM((plan.slots, hidden), BF16),
         ],
-        limit=32 << 20,
     )
 
 

time: 178 us -> 180 us (1.011)
  blocking collectives: 136 us -> 138 us
    all_to_all x1, blocking collectives: 32.2 us -> 35.1 us  [through_experts(): returned = lax.all_to_all(partial, 'tp', 0, 0, tiled=True)]
    pallas_call x9 -> x10, Pallas kernels: 9.75 us -> 10.9 us  [call(): pl.pallas_call(kernel, out_shape=out, in_specs=specs, out_specs=jax.tree....]
  transfers between devices with their start and end apart: 7 -> 7, of which waited for: 4 -> 3; matrix products, arithmetic and copies ran while one was open for 0% -> 0% of each run, Pallas kernels for 1% -> 2%
where the time goes in v7:
time: 180 us; the launch traced here: 179 us
  blocking collectives  138 us (77%)
  starting transfers between devices  23.9 us (13%)
  Pallas kernels  10.9 us (6%)
  waiting for transfers between devices  5.29 us (3%)
    all_to_all x1, blocking collectives, on_device(): received = lax.all_to_all(outgoing, 'ep', 0, 0, tiled=True)  66.2 us
    all_to_all x1, blocking collectives, through_experts(): returned = lax.all_to_all(partial, 'tp', 0, 0, tiled=True)  35.1 us
    all_to_all x1, blocking collectives, through_experts(): lax.all_to_all(spread(plan, take_out, needed, returned), 'ep', 0, 0, tile...  25.9 us
    ppermute x3, starting transfers between devices, gather_lanes(): got.append(lax.ppermute(held[1], axes, left))  14.5 us
    all_to_all x1, blocking collectives, on_device(): shares = lax.all_to_all(shares, 'tp', 0, 0, tiled=True)  11.2 us
    pallas_call x10, Pallas kernels, call(): pl.pallas_call(kernel, out_shape=out, in_specs=specs, out_specs=jax.tree....  10.9 us
    ppermute x4, starting transfers between devices, gather_lanes(): got = [lax.ppermute(held[0], axes, right)]  9.39 us
    ppermute x4, waiting for transfers between devices, gather_lanes(): got = [lax.ppermute(held[0], axes, right)]  5.28 us
  transfers between devices with their start and end apart: 7, of which 3 were waited for; matrix products, arithmetic and copies ran while one was open for 0% of the time, Pallas kernels for 2%

profile of v7, /device:TPU:80, one launch (start us, length us, event | category | flops | bytes accessed | tf_op | source)
XLA Modules:
  0.0 179.3 jit_solution(12346756124666096772)
XLA Ops:
  0.0 1.3 pack.1
  1.3 66.2 %all_to_all.30.refs_1_.refs_0_ = bf16[32,32,128]{2,1,0:T(8,128)(2,1)S(1)} all-to-all(bf16[32,32,128]{2,1,0:T(8,128)(2,1)S(1)} %pack.1), channel_id=1, replica_groups=mesh['groups'=2,'ep'=32,'tp'=8] {'ep'}, dimensions={0} | all-to-all | bytes 524288 | tf_op jit(solution)/shard_map/all_to_all | solution.py:560
  67.6 1.6 compact.3
  69.2 3.6 %collective-permute-start.7 = (bf16[560,128]{1,0:T(8,128)(2,1)S(1)}, bf16[560,128]{1,0:T(8,128)(2,1)S(1)}, u32[]{:S(2)}, u32[]{:S(2)}) collective-permute-start(bf16[560,128]{1,0:T(8,128)(2,1)S(1)} %get-tuple-element.65.refs_1_), channel_id=1, source_target_pairs={{0,1},{1,2},{2,3},{3,4},{4,5},{5,6},{6,7},{7,0},{8,15},{9,8},{10,9... | collective-permute-start | bytes 430088 | tf_op jit(solution)/shard_map/ppermute | solution.py:529
  72.7 4.2 %collective-permute-start.11 = (bf16[560,128]{1,0:T(8,128)(2,1)S(1)}, bf16[560,128]{1,0:T(8,128)(2,1)S(1)}, u32[]{:S(2)}, u32[]{:S(2)}) collective-permute-start(bf16[560,128]{1,0:T(8,128)(2,1)S(1)} %get-tuple-element.65.refs_1_), channel_id=1, source_target_pairs={{0,7},{1,0},{2,1},{3,2},{4,3},{5,4},{6,5},{7,6},{8,9},{9,10},{10,1... | collective-permute-start | bytes 430088 | tf_op jit(solution)/shard_map/ppermute | solution.py:532
  76.9 0.9 weights.3.refs_4_
  77.7 0.2 collective-permute-done.7.refs_2_
  78.0 1.9 %collective-permute-start.8 = (bf16[560,128]{1,0:T(8,128)(2,1)S(1)}, bf16[560,128]{1,0:T(8,128)(2,1)S(1)}, u32[]{:S(2)}, u32[]{:S(2)}) collective-permute-start(bf16[560,128]{1,0:T(8,128)(2,1)S(1)} %collective-permute-done.7.refs_2_), channel_id=1, source_target_pairs={{0,1},{1,2},{2,3},{3,4},{4,5},{5,6},{6,7},{7,0},{8,15},{9,8},{10,9... | collective-permute-start | bytes 430088 | tf_op jit(solution)/shard_map/ppermute | solution.py:529
  79.9 5.2 %collective-permute-start.12 = (bf16[560,128]{1,0:T(8,128)(2,1)S(1)}, bf16[560,128]{1,0:T(8,128)(2,1)S(1)}, u32[]{:S(2)}, u32[]{:S(2)}) collective-permute-start(bf16[560,128]{1,0:T(8,128)(2,1)S(1)} %collective-permute-done.11.refs_3_), channel_id=1, source_target_pairs={{0,7},{1,0},{2,1},{3,2},{4,3},{5,4},{6,5},{7,6},{8,9},{9,10},{10,1... | collective-permute-start | bytes 430088 | tf_op jit(solution)/shard_map/ppermute | solution.py:532
  85.1 0.4 spread_table.3.refs_0_
  85.5 0.7 collective-permute-done.8.refs_4_
  86.2 1.9 %collective-permute-start.9 = (bf16[560,128]{1,0:T(8,128)(2,1)S(1)}, bf16[560,128]{1,0:T(8,128)(2,1)S(1)}, u32[]{:S(2)}, u32[]{:S(2)}) collective-permute-start(bf16[560,128]{1,0:T(8,128)(2,1)S(1)} %collective-permute-done.8.refs_4_), channel_id=1, source_target_pairs={{0,1},{1,2},{2,3},{3,4},{4,5},{5,6},{6,7},{7,0},{8,15},{9,8},{10,9... | collective-permute-start | bytes 430088 | tf_op jit(solution)/shard_map/ppermute | solution.py:529
  88.2 5.2 %collective-permute-start.13 = (bf16[560,128]{1,0:T(8,128)(2,1)S(1)}, bf16[560,128]{1,0:T(8,128)(2,1)S(1)}, u32[]{:S(2)}, u32[]{:S(2)}) collective-permute-start(bf16[560,128]{1,0:T(8,128)(2,1)S(1)} %collective-permute-done.12.refs_5_), channel_id=1, source_target_pairs={{0,7},{1,0},{2,1},{3,2},{4,3},{5,4},{6,5},{7,6},{8,9},{9,10},{10,1... | collective-permute-start | bytes 430088 | tf_op jit(solution)/shard_map/ppermute | solution.py:532
  93.3 1.2 combine_table.1.refs_0_
  94.5 2.0 %collective-permute-start.10 = (bf16[560,128]{1,0:T(8,128)(2,1)S(1)}, bf16[560,128]{1,0:T(8,128)(2,1)S(1)}, u32[]{:S(2)}, u32[]{:S(2)}) collective-permute-start(bf16[560,128]{1,0:T(8,128)(2,1)S(1)} %collective-permute-done.9.refs_6_), channel_id=1, source_target_pairs={{0,1},{1,2},{2,3},{3,4},{4,5},{5,6},{6,7},{7,0},{8,15},{9,8},{10,9... | collective-permute-start | bytes 430088 | tf_op jit(solution)/shard_map/ppermute | solution.py:529
  96.5 1.9 %early.3 = (f32[224,256]{1,0:T(8,128)S(1)}, f32[224,256]{1,0:T(8,128)S(1)}) custom-call(s32[16]{0:T(128)} %refs_0_.5, bf16[560,128]{1,0:T(8,128)(2,1)S(1)} %get-tuple-element.65.refs_1_, bf16[560,128]{1,0:T(8,128)(2,1)S(1)} %collective-permute-done.7.refs_2_, bf16[560,128]{1,0:T(8,128)(2,1)S(1)} %collective-permute-done.11.refs_3_, ...), custom_call_target="tpu_custom_call" | custom-call | flops 536870912 | bytes 1048576 | tf_op jit(solution)/shard_map/early/pallas_call | solution.py:349
  98.4 4.3 %collective-permute-done.10.refs_1_ = bf16[560,128]{1,0:T(8,128)(2,1)S(1)} collective-permute-done((bf16[560,128]{1,0:T(8,128)(2,1)S(1)}, bf16[560,128]{1,0:T(8,128)(2,1)S(1)}, u32[]{:S(2)}, u32[]{:S(2)}) %collective-permute-start.10) | collective-permute-done | bytes 143392 | tf_op jit(solution)/shard_map/ppermute | solution.py:529
  102.8 1.4 experts.3
  104.2 35.1 %all_to_all.31.refs_2_ = bf16[8,560,128]{2,1,0:T(8,128)(2,1)S(1)} all-to-all(bf16[8,560,128]{2,1,0:T(8,128)(2,1)S(1)} %experts.3), channel_id=1, replica_groups=mesh['groups'=2,'ep'=32,'tp'=8] {'tp'}, dimensions={0} | all-to-all | bytes 2293760 | tf_op jit(solution)/shard_map/all_to_all | solution.py:545
  139.3 0.6 spread.3
  139.9 25.9 %all_to_all.32.refs_1_ = bf16[32,32,128]{2,1,0:T(8,128)(2,1)S(1)} all-to-all(bf16[32,32,128]{2,1,0:T(8,128)(2,1)S(1)} %spread.3), channel_id=1, replica_groups=mesh['groups'=2,'ep'=32,'tp'=8] {'ep'}, dimensions={0} | all-to-all | bytes 524288 | tf_op jit(solution)/shard_map/all_to_all | solution.py:546
  165.8 1.0 combine.3
  167.4 11.2 %all_to_all.33.refs_0_ = bf16[8,48,128]{2,1,0:T(8,128)(2,1)S(1)} all-to-all(bf16[8,48,128]{2,1,0:T(8,128)(2,1)S(1)} %get-tuple-element.85), channel_id=1, replica_groups=mesh['groups'=2,'ep'=32,'tp'=8] {'tp'}, dimensions={0} | all-to-all | bytes 196608 | tf_op jit(solution)/shard_map/all_to_all | solution.py:569
  178.6 0.7 finish.1
  (11 shorter events, 0.0 us)
Async XLA Ops:
  69.2 8.8 %collective-permute-start.7 = (bf16[560,128]{1,0:T(8,128)(2,1)S(1)}, bf16[560,128]{1,0:T(8,128)(2,1)S(1)}, u32[]{:S(2)}, u32[]{:S(2)}) collective-permute-start(bf16[560,128]{1,0:T(8,128)(2,1)S(1)} %get-tuple-element.65.refs_1_), channel_id=1, source_target_pairs={{0,1},{1,2},{2,3},{3,4},{4,5},{5,6},{6,7},{7,0},{8,15},{9,8},{10,9... | collective-permute-start | bytes 430088 | tf_op jit(solution)/shard_map/ppermute | solution.py:529
  72.7 7.2 %collective-permute-start.11 = (bf16[560,128]{1,0:T(8,128)(2,1)S(1)}, bf16[560,128]{1,0:T(8,128)(2,1)S(1)}, u32[]{:S(2)}, u32[]{:S(2)}) collective-permute-start(bf16[560,128]{1,0:T(8,128)(2,1)S(1)} %get-tuple-element.65.refs_1_), channel_id=1, source_target_pairs={{0,7},{1,0},{2,1},{3,2},{4,3},{5,4},{6,5},{7,6},{8,9},{9,10},{10,1... | collective-permute-start | bytes 430088 | tf_op jit(solution)/shard_map/ppermute | solution.py:532
  78.0 8.2 %collective-permute-start.8 = (bf16[560,128]{1,0:T(8,128)(2,1)S(1)}, bf16[560,128]{1,0:T(8,128)(2,1)S(1)}, u32[]{:S(2)}, u32[]{:S(2)}) collective-permute-start(bf16[560,128]{1,0:T(8,128)(2,1)S(1)} %collective-permute-done.7.refs_2_), channel_id=1, source_target_pairs={{0,1},{1,2},{2,3},{3,4},{4,5},{5,6},{6,7},{7,0},{8,15},{9,8},{10,9... | collective-permute-start | bytes 430088 | tf_op jit(solution)/shard_map/ppermute | solution.py:529
  79.9 8.2 %collective-permute-start.12 = (bf16[560,128]{1,0:T(8,128)(2,1)S(1)}, bf16[560,128]{1,0:T(8,128)(2,1)S(1)}, u32[]{:S(2)}, u32[]{:S(2)}) collective-permute-start(bf16[560,128]{1,0:T(8,128)(2,1)S(1)} %collective-permute-done.11.refs_3_), channel_id=1, source_target_pairs={{0,7},{1,0},{2,1},{3,2},{4,3},{5,4},{6,5},{7,6},{8,9},{9,10},{10,1... | collective-permute-start | bytes 430088 | tf_op jit(solution)/shard_map/ppermute | solution.py:532
  85.1 11.4 %copy-start.1 = (bf16[2,128,2560]{2,1,0:T(8,128)(2,1)S(1)}, bf16[2,128,2560]{2,1,0:T(8,128)(2,1)}, u32[]{:S(2)}) copy-start(bf16[2,128,2560]{2,1,0:T(8,128)(2,1)} %param.16) | copy-start | bytes 3932164
  85.5 11.0 %copy-start = (bf16[2,128,2560]{2,1,0:T(8,128)(2,1)S(1)}, bf16[2,128,2560]{2,1,0:T(8,128)(2,1)}, u32[]{:S(2)}) copy-start(bf16[2,128,2560]{2,1,0:T(8,128)(2,1)} %param.15) | copy-start | bytes 3932164
  86.2 8.3 %collective-permute-start.9 = (bf16[560,128]{1,0:T(8,128)(2,1)S(1)}, bf16[560,128]{1,0:T(8,128)(2,1)S(1)}, u32[]{:S(2)}, u32[]{:S(2)}) collective-permute-start(bf16[560,128]{1,0:T(8,128)(2,1)S(1)} %collective-permute-done.8.refs_4_), channel_id=1, source_target_pairs={{0,1},{1,2},{2,3},{3,4},{4,5},{5,6},{6,7},{7,0},{8,15},{9,8},{10,9... | collective-permute-start | bytes 430088 | tf_op jit(solution)/shard_map/ppermute | solution.py:529
  88.2 8.3 %collective-permute-start.13 = (bf16[560,128]{1,0:T(8,128)(2,1)S(1)}, bf16[560,128]{1,0:T(8,128)(2,1)S(1)}, u32[]{:S(2)}, u32[]{:S(2)}) collective-permute-start(bf16[560,128]{1,0:T(8,128)(2,1)S(1)} %collective-permute-done.12.refs_5_), channel_id=1, source_target_pairs={{0,7},{1,0},{2,1},{3,2},{4,3},{5,4},{6,5},{7,6},{8,9},{9,10},{10,1... | collective-permute-start | bytes 430088 | tf_op jit(solution)/shard_map/ppermute | solution.py:532
  94.5 8.2 %collective-permute-start.10 = (bf16[560,128]{1,0:T(8,128)(2,1)S(1)}, bf16[560,128]{1,0:T(8,128)(2,1)S(1)}, u32[]{:S(2)}, u32[]{:S(2)}) collective-permute-start(bf16[560,128]{1,0:T(8,128)(2,1)S(1)} %collective-permute-done.9.refs_6_), channel_id=1, source_target_pairs={{0,1},{1,2},{2,3},{3,4},{4,5},{5,6},{6,7},{7,0},{8,15},{9,8},{10,9... | collective-permute-start | bytes 430088 | tf_op jit(solution)/shard_map/ppermute | solution.py:529
  96.5 6.2 %copy-start.2 = (bf16[2,128,2560]{2,1,0:T(8,128)(2,1)S(1)}, bf16[2,128,2560]{2,1,0:T(8,128)(2,1)}, u32[]{:S(2)}) copy-start(bf16[2,128,2560]{2,1,0:T(8,128)(2,1)} %param.17) | copy-start | bytes 3932164

commit v8 on v5

--- a/solution.py
+++ b/solution.py
@@ -242,10 +242,10 @@
 def expert_kernel(plan, offsets, info_ref, *refs):
     n = len(offsets)
     weight_ref, wg, wu, wd, out_ref, x_ref, h_ref = refs[n:]
-    me = info_ref[0]
+    me, way = info_ref[0], 1 - 2 * lax.rem(info_ref[1], 2)
     lanes, half, slots = plan.lanes, plan.half, plan.slots
     for offset, part in zip(offsets, refs):
-        lane = lax.rem(me + offset + lanes, lanes)
+        lane = lax.rem(me + way * offset + lanes, lanes)
         first = pl.multiple_of(lane * (2 * LANE), LANE)
         tail = pl.multiple_of((2 * lanes + lane // 2) * LANE, LANE)
         start = pl.multiple_of(lax.rem(lane, 2) * half, 8)
@@ -464,23 +464,20 @@
 
 
 def gather_lanes(packed, lanes, beside):
-    right = [(i, (i + 1) % lanes) for i in range(lanes)]
-    left = [(i, (i - 1) % lanes) for i in range(lanes)]
-    parts, offsets, values = [packed], [0], []
-    held = [packed, packed]
-    for hop in range(1, lanes // 2 + 1):
-        if hop > 1 and hop - 2 < len(beside):
-            first, value = lax.optimization_barrier((held[0], beside[hop - 2]))
-            held = [first, held[1]]
+    ranks = lax.axis_size("ep")
+    pairs = [
+        (rank * lanes + i, rank * lanes + (i + 1 - 2 * (rank % 2)) % lanes)
+        for rank in range(ranks)
+        for i in range(lanes)
+    ]
+    parts, values = [packed], []
+    for hop in range(lanes - 1):
+        held = parts[-1]
+        if 0 < hop <= len(beside):
+            held, value = lax.optimization_barrier((held, beside[hop - 1]))
             values.append(value)
-        got = [lax.ppermute(held[0], "tp", right)]
-        offsets.append(-hop)
-        if hop < lanes // 2:
-            got.append(lax.ppermute(held[1], "tp", left))
-            offsets.append(hop)
-        parts += got
-        held = got
-    return parts, offsets, values
+        parts.append(lax.ppermute(held, ("ep", "tp"), pairs))
+    return parts, [-hop for hop in range(lanes)], values
 
 
 def through_experts(plan, info, received, take_in, matrices):

time: 181 us -> 199 us (1.099)
  waiting for transfers between devices: 7.85 us -> 40.5 us
  starting transfers between devices: 24 us -> 15.2 us
  blocking collectives: 138 us -> 132 us
    ppermute x7, waiting for transfers between devices: 7.85 us -> 40.5 us  [gather_lanes(): parts.append(lax.ppermute(held, ('ep', 'tp'), pairs))]
    ppermute x7, starting transfers between devices: 24 us -> 15.2 us  [gather_lanes(): parts.append(lax.ppermute(held, ('ep', 'tp'), pairs))]
    all_to_all x1, blocking collectives: 33.5 us -> 27.2 us  [through_experts(): returned = lax.all_to_all(partial, 'tp', 0, 0, tiled=True)]
  transfers between devices with their start and end apart: 7 -> 7, of which waited for: 4 -> 7; matrix products, arithmetic and copies ran while one was open for 0% -> 0% of each run, Pallas kernels for 1% -> 1%
where the time goes in v8:
time: 199 us
  blocking collectives  132 us (66%)
  waiting for transfers between devices  40.5 us (20%)
  starting transfers between devices  15.2 us (8%)
  Pallas kernels  9.77 us (5%)
    all_to_all x1, blocking collectives, on_device(): received = lax.all_to_all(outgoing, 'ep', 0, 0, tiled=True)  66.2 us
    ppermute x7, waiting for transfers between devices, gather_lanes(): parts.append(lax.ppermute(held, ('ep', 'tp'), pairs))  40.5 us
    all_to_all x1, blocking collectives, through_experts(): lax.all_to_all(spread(plan, take_out, needed, returned), 'ep', 0, 0, tile...  27.8 us
    all_to_all x1, blocking collectives, through_experts(): returned = lax.all_to_all(partial, 'tp', 0, 0, tiled=True)  27.2 us
    ppermute x7, starting transfers between devices, gather_lanes(): parts.append(lax.ppermute(held, ('ep', 'tp'), pairs))  15.2 us
    all_to_all x1, blocking collectives, on_device(): shares = lax.all_to_all(shares, 'tp', 0, 0, tiled=True)  11.2 us
    pallas_call x9, Pallas kernels, call(): pl.pallas_call(kernel, out_shape=out, in_specs=specs, out_specs=jax.tree....  9.77 us
  transfers between devices with their start and end apart: 7, of which 7 were waited for; matrix products, arithmetic and copies ran while one was open for 0% of the time, Pallas kernels for 1%

profile of v8, /device:TPU:80, one launch (start us, length us, event | category | flops | bytes accessed | tf_op | source)
XLA Modules:
  0.0 198.7 jit_solution(3670134315265982333)
XLA Ops:
  0.0 1.3 pack.1
  1.3 66.2 %all_to_all.30.refs_1_.refs_0_ = bf16[32,32,128]{2,1,0:T(8,128)(2,1)S(1)} all-to-all(bf16[32,32,128]{2,1,0:T(8,128)(2,1)S(1)} %pack.1), channel_id=1, replica_groups=mesh['groups'=2,'ep'=32,'tp'=8] {'ep'}, dimensions={0} | all-to-all | bytes 524288 | tf_op jit(solution)/shard_map/all_to_all | solution.py:504
  67.6 1.6 compact.3
  69.2 3.6 %collective-permute-start.7 = (bf16[560,128]{1,0:T(8,128)(2,1)S(1)}, bf16[560,128]{1,0:T(8,128)(2,1)S(1)}, u32[]{:S(2)}, u32[]{:S(2)}) collective-permute-start(bf16[560,128]{1,0:T(8,128)(2,1)S(1)} %get-tuple-element.61.refs_1_), channel_id=1, source_target_pairs={{0,1},{1,2},{2,3},{3,4},{4,5},{5,6},{6,7},{7,0},{8,15},{9,8},{10,9... | collective-permute-start | bytes 430088 | tf_op jit(solution)/shard_map/ppermute | solution.py:479
  72.7 0.9 weights.3.refs_9_
  73.6 4.4 %collective-permute-done.7.refs_2_ = bf16[560,128]{1,0:T(8,128)(2,1)S(1)} collective-permute-done((bf16[560,128]{1,0:T(8,128)(2,1)S(1)}, bf16[560,128]{1,0:T(8,128)(2,1)S(1)}, u32[]{:S(2)}, u32[]{:S(2)}) %collective-permute-start.7) | collective-permute-done | bytes 143392 | tf_op jit(solution)/shard_map/ppermute | solution.py:479
  78.0 1.9 collective-permute-start.8
  80.3 5.9 %collective-permute-done.8.refs_3_ = bf16[560,128]{1,0:T(8,128)(2,1)S(1)} collective-permute-done((bf16[560,128]{1,0:T(8,128)(2,1)S(1)}, bf16[560,128]{1,0:T(8,128)(2,1)S(1)}, u32[]{:S(2)}, u32[]{:S(2)}) %collective-permute-start.8) | collective-permute-done | bytes 143392 | tf_op jit(solution)/shard_map/ppermute | solution.py:479
  86.2 1.9 collective-permute-start.9
  88.2 1.2 combine_table.1.refs_0_
  89.3 5.1 %collective-permute-done.9.refs_4_ = bf16[560,128]{1,0:T(8,128)(2,1)S(1)} collective-permute-done((bf16[560,128]{1,0:T(8,128)(2,1)S(1)}, bf16[560,128]{1,0:T(8,128)(2,1)S(1)}, u32[]{:S(2)}, u32[]{:S(2)}) %collective-permute-start.9) | collective-permute-done | bytes 143392 | tf_op jit(solution)/shard_map/ppermute | solution.py:479
  94.4 1.9 collective-permute-start.10
  96.4 6.3 %collective-permute-done.10.refs_5_ = bf16[560,128]{1,0:T(8,128)(2,1)S(1)} collective-permute-done((bf16[560,128]{1,0:T(8,128)(2,1)S(1)}, bf16[560,128]{1,0:T(8,128)(2,1)S(1)}, u32[]{:S(2)}, u32[]{:S(2)}) %collective-permute-start.10) | collective-permute-done | bytes 143392 | tf_op jit(solution)/shard_map/ppermute | solution.py:479
  102.7 1.9 collective-permute-start.11
  104.6 6.3 %collective-permute-done.11.refs_6_ = bf16[560,128]{1,0:T(8,128)(2,1)S(1)} collective-permute-done((bf16[560,128]{1,0:T(8,128)(2,1)S(1)}, bf16[560,128]{1,0:T(8,128)(2,1)S(1)}, u32[]{:S(2)}, u32[]{:S(2)}) %collective-permute-start.11) | collective-permute-done | bytes 143392 | tf_op jit(solution)/shard_map/ppermute | solution.py:479
  110.9 1.9 collective-permute-start.12
  112.8 6.3 %collective-permute-done.12.refs_7_ = bf16[560,128]{1,0:T(8,128)(2,1)S(1)} collective-permute-done((bf16[560,128]{1,0:T(8,128)(2,1)S(1)}, bf16[560,128]{1,0:T(8,128)(2,1)S(1)}, u32[]{:S(2)}, u32[]{:S(2)}) %collective-permute-start.12) | collective-permute-done | bytes 143392 | tf_op jit(solution)/shard_map/ppermute | solution.py:479
  119.1 1.9 collective-permute-start.13
  121.0 6.3 %collective-permute-done.13.refs_8_ = bf16[560,128]{1,0:T(8,128)(2,1)S(1)} collective-permute-done((bf16[560,128]{1,0:T(8,128)(2,1)S(1)}, bf16[560,128]{1,0:T(8,128)(2,1)S(1)}, u32[]{:S(2)}, u32[]{:S(2)}) %collective-permute-start.13) | collective-permute-done | bytes 143392 | tf_op jit(solution)/shard_map/ppermute | solution.py:479
  127.3 2.2 %experts.3 = bf16[8,560,128]{2,1,0:T(8,128)(2,1)S(1)} custom-call(s32[16]{0:T(128)} %refs_0_.4, bf16[560,128]{1,0:T(8,128)(2,1)S(1)} %get-tuple-element.61.refs_1_, bf16[560,128]{1,0:T(8,128)(2,1)S(1)} %collective-permute-done.7.refs_2_, bf16[560,128]{1,0:T(8,128)(2,1)S(1)} %collective-permute-done.8.refs_3_, ...), custom_call_target="tpu_custom_call" | custom-call | tf_op jit(solution)/shard_map/experts/pallas_call | solution.py:324
  129.5 27.2 %all_to_all.31.refs_2_ = bf16[8,560,128]{2,1,0:T(8,128)(2,1)S(1)} all-to-all(bf16[8,560,128]{2,1,0:T(8,128)(2,1)S(1)} %experts.3), channel_id=1, replica_groups=mesh['groups'=2,'ep'=32,'tp'=8] {'tp'}, dimensions={0} | all-to-all | bytes 2293760 | tf_op jit(solution)/shard_map/all_to_all | solution.py:489
  157.4 27.8 %all_to_all.32.refs_1_ = bf16[32,32,128]{2,1,0:T(8,128)(2,1)S(1)} all-to-all(bf16[32,32,128]{2,1,0:T(8,128)(2,1)S(1)} %spread.3), channel_id=1, replica_groups=mesh['groups'=2,'ep'=32,'tp'=8] {'ep'}, dimensions={0} | all-to-all | bytes 524288 | tf_op jit(solution)/shard_map/all_to_all | solution.py:490
  185.1 1.0 combine.3
  186.8 11.2 %all_to_all.33.refs_0_ = bf16[8,48,128]{2,1,0:T(8,128)(2,1)S(1)} all-to-all(bf16[8,48,128]{2,1,0:T(8,128)(2,1)S(1)} %get-tuple-element.79), channel_id=1, replica_groups=mesh['groups'=2,'ep'=32,'tp'=8] {'tp'}, dimensions={0} | all-to-all | bytes 196608 | tf_op jit(solution)/shard_map/all_to_all | solution.py:513
  (10 shorter events, 1.7 us)
Async XLA Ops:
  69.2 8.8 %collective-permute-start.7 = (bf16[560,128]{1,0:T(8,128)(2,1)S(1)}, bf16[560,128]{1,0:T(8,128)(2,1)S(1)}, u32[]{:S(2)}, u32[]{:S(2)}) collective-permute-start(bf16[560,128]{1,0:T(8,128)(2,1)S(1)} %get-tuple-element.61.refs_1_), channel_id=1, source_target_pairs={{0,1},{1,2},{2,3},{3,4},{4,5},{5,6},{6,7},{7,0},{8,15},{9,8},{10,9... | collective-permute-start | bytes 430088 | tf_op jit(solution)/shard_map/ppermute | solution.py:479
  78.0 8.2 %collective-permute-start.8 = (bf16[560,128]{1,0:T(8,128)(2,1)S(1)}, bf16[560,128]{1,0:T(8,128)(2,1)S(1)}, u32[]{:S(2)}, u32[]{:S(2)}) collective-permute-start(bf16[560,128]{1,0:T(8,128)(2,1)S(1)} %collective-permute-done.7.refs_2_), channel_id=1, source_target_pairs={{0,1},{1,2},{2,3},{3,4},{4,5},{5,6},{6,7},{7,0},{8,15},{9,8},{10,9... | collective-permute-start | bytes 430088 | tf_op jit(solution)/shard_map/ppermute | solution.py:479
  79.9 47.4 %copy-start.1 = (bf16[2,128,2560]{2,1,0:T(8,128)(2,1)S(1)}, bf16[2,128,2560]{2,1,0:T(8,128)(2,1)}, u32[]{:S(2)}) copy-start(bf16[2,128,2560]{2,1,0:T(8,128)(2,1)} %param.16) | copy-start | bytes 3932164
  79.9 47.4 %copy-start.2 = (bf16[2,128,2560]{2,1,0:T(8,128)(2,1)S(1)}, bf16[2,128,2560]{2,1,0:T(8,128)(2,1)}, u32[]{:S(2)}) copy-start(bf16[2,128,2560]{2,1,0:T(8,128)(2,1)} %param.17) | copy-start | bytes 3932164
  80.3 47.0 %copy-start = (bf16[2,128,2560]{2,1,0:T(8,128)(2,1)S(1)}, bf16[2,128,2560]{2,1,0:T(8,128)(2,1)}, u32[]{:S(2)}) copy-start(bf16[2,128,2560]{2,1,0:T(8,128)(2,1)} %param.15) | copy-start | bytes 3932164
  86.2 8.2 %collective-permute-start.9 = (bf16[560,128]{1,0:T(8,128)(2,1)S(1)}, bf16[560,128]{1,0:T(8,128)(2,1)S(1)}, u32[]{:S(2)}, u32[]{:S(2)}) collective-permute-start(bf16[560,128]{1,0:T(8,128)(2,1)S(1)} %collective-permute-done.8.refs_3_), channel_id=1, source_target_pairs={{0,1},{1,2},{2,3},{3,4},{4,5},{5,6},{6,7},{7,0},{8,15},{9,8},{10,9... | collective-permute-start | bytes 430088 | tf_op jit(solution)/shard_map/ppermute | solution.py:479
  94.4 8.2 %collective-permute-start.10 = (bf16[560,128]{1,0:T(8,128)(2,1)S(1)}, bf16[560,128]{1,0:T(8,128)(2,1)S(1)}, u32[]{:S(2)}, u32[]{:S(2)}) collective-permute-start(bf16[560,128]{1,0:T(8,128)(2,1)S(1)} %collective-permute-done.9.refs_4_), channel_id=1, source_target_pairs={{0,1},{1,2},{2,3},{3,4},{4,5},{5,6},{6,7},{7,0},{8,15},{9,8},{10,9... | collective-permute-start | bytes 430088 | tf_op jit(solution)/shard_map/ppermute | solution.py:479
  102.7 8.2 %collective-permute-start.11 = (bf16[560,128]{1,0:T(8,128)(2,1)S(1)}, bf16[560,128]{1,0:T(8,128)(2,1)S(1)}, u32[]{:S(2)}, u32[]{:S(2)}) collective-permute-start(bf16[560,128]{1,0:T(8,128)(2,1)S(1)} %collective-permute-done.10.refs_5_), channel_id=1, source_target_pairs={{0,1},{1,2},{2,3},{3,4},{4,5},{5,6},{6,7},{7,0},{8,15},{9,8},{10,9... | collective-permute-start | bytes 430088 | tf_op jit(solution)/shard_map/ppermute | solution.py:479
  110.9 8.2 %collective-permute-start.12 = (bf16[560,128]{1,0:T(8,128)(2,1)S(1)}, bf16[560,128]{1,0:T(8,128)(2,1)S(1)}, u32[]{:S(2)}, u32[]{:S(2)}) collective-permute-start(bf16[560,128]{1,0:T(8,128)(2,1)S(1)} %collective-permute-done.11.refs_6_), channel_id=1, source_target_pairs={{0,1},{1,2},{2,3},{3,4},{4,5},{5,6},{6,7},{7,0},{8,15},{9,8},{10,9... | collective-permute-start | bytes 430088 | tf_op jit(solution)/shard_map/ppermute | solution.py:479
  119.1 8.2 %collective-permute-start.13 = (bf16[560,128]{1,0:T(8,128)(2,1)S(1)}, bf16[560,128]{1,0:T(8,128)(2,1)S(1)}, u32[]{:S(2)}, u32[]{:S(2)}) collective-permute-start(bf16[560,128]{1,0:T(8,128)(2,1)S(1)} %collective-permute-done.12.refs_7_), channel_id=1, source_target_pairs={{0,1},{1,2},{2,3},{3,4},{4,5},{5,6},{6,7},{7,0},{8,15},{9,8},{10,9... | collective-permute-start | bytes 430088 | tf_op jit(solution)/shard_map/ppermute | solution.py:479

commit v9 on v6

--- a/solution.py
+++ b/solution.py
@@ -477,13 +477,9 @@
         )
     right, left = ways
     axes = ("ep", "tp")
-    parts, offsets, values = [packed], [0], []
+    parts, offsets = [packed], [0]
     held = [packed, packed]
     for hop in range(1, lanes // 2 + 1):
-        if hop > 1 and hop - 2 < len(beside):
-            first, value = lax.optimization_barrier((held[0], beside[hop - 2]))
-            held = [first, held[1]]
-            values.append(value)
         got = [lax.ppermute(held[0], axes, right)]
         offsets.append(-hop)
         if hop < lanes // 2:
@@ -491,7 +487,8 @@
             offsets.append(hop)
         parts += got
         held = got
-    return parts, offsets, values
+    last, beside = lax.optimization_barrier((parts[-1], beside))
+    return parts[:-1] + [last], offsets, beside
 
 
 def through_experts(plan, info, received, take_in, matrices):

time: 178 us -> 179 us (level)
  no operation moved by 1% of the time
where the time goes in v9:
time: 179 us; the launch traced here: 178 us
  blocking collectives  137 us (77%)
  starting transfers between devices  23.9 us (13%)
  Pallas kernels  9.95 us (6%)
  waiting for transfers between devices  6.93 us (4%)
    all_to_all x1, blocking collectives, on_device(): received = lax.all_to_all(outgoing, 'ep', 0, 0, tiled=True)  66.2 us
    all_to_all x1, blocking collectives, through_experts(): returned = lax.all_to_all(partial, 'tp', 0, 0, tiled=True)  33.4 us
    all_to_all x1, blocking collectives, through_experts(): lax.all_to_all(spread(plan, take_out, needed, returned), 'ep', 0, 0, tile...  25.9 us
    ppermute x3, starting transfers between devices, gather_lanes(): got.append(lax.ppermute(held[1], axes, left))  14.5 us
    all_to_all x1, blocking collectives, on_device(): shares = lax.all_to_all(shares, 'tp', 0, 0, tiled=True)  11.2 us
    pallas_call x9, Pallas kernels, call(): pl.pallas_call(kernel, out_shape=out, in_specs=specs, out_specs=jax.tree....  9.95 us
    ppermute x4, starting transfers between devices, gather_lanes(): got = [lax.ppermute(held[0], axes, right)]  9.38 us
    ppermute x4, waiting for transfers between devices, gather_lanes(): got = [lax.ppermute(held[0], axes, right)]  6.93 us
  transfers between devices with their start and end apart: 7, of which 4 were waited for; matrix products, arithmetic and copies ran while one was open for 0% of the time, Pallas kernels for 1%

profile of v9, /device:TPU:80, one launch (start us, length us, event | category | flops | bytes accessed | tf_op | source)
XLA Modules:
  0.0 178.2 jit_solution(5212862742731359132)
XLA Ops:
  0.0 1.3 pack.1
  1.3 66.2 %all_to_all.30.refs_1_.refs_0_ = bf16[32,32,128]{2,1,0:T(8,128)(2,1)S(1)} all-to-all(bf16[32,32,128]{2,1,0:T(8,128)(2,1)S(1)} %pack.1), channel_id=1, replica_groups=mesh['groups'=2,'ep'=32,'tp'=8] {'ep'}, dimensions={0} | all-to-all | bytes 524288 | tf_op jit(solution)/shard_map/all_to_all | solution.py:515
  67.6 1.6 compact.3
  69.2 3.6 %collective-permute-start.7 = (bf16[560,128]{1,0:T(8,128)(2,1)S(1)}, bf16[560,128]{1,0:T(8,128)(2,1)S(1)}, u32[]{:S(2)}, u32[]{:S(2)}) collective-permute-start(bf16[560,128]{1,0:T(8,128)(2,1)S(1)} %get-tuple-element.57.refs_1_), channel_id=1, source_target_pairs={{0,1},{1,2},{2,3},{3,4},{4,5},{5,6},{6,7},{7,0},{8,15},{9,8},{10,9... | collective-permute-start | bytes 430088 | tf_op jit(solution)/shard_map/ppermute | solution.py:483
  72.7 4.2 %collective-permute-start.11 = (bf16[560,128]{1,0:T(8,128)(2,1)S(1)}, bf16[560,128]{1,0:T(8,128)(2,1)S(1)}, u32[]{:S(2)}, u32[]{:S(2)}) collective-permute-start(bf16[560,128]{1,0:T(8,128)(2,1)S(1)} %get-tuple-element.57.refs_1_), channel_id=1, source_target_pairs={{0,7},{1,0},{2,1},{3,2},{4,3},{5,4},{6,5},{7,6},{8,9},{9,10},{10,1... | collective-permute-start | bytes 430088 | tf_op jit(solution)/shard_map/ppermute | solution.py:486
  76.9 1.1 collective-permute-done.7.refs_2_
  78.0 1.9 %collective-permute-start.8 = (bf16[560,128]{1,0:T(8,128)(2,1)S(1)}, bf16[560,128]{1,0:T(8,128)(2,1)S(1)}, u32[]{:S(2)}, u32[]{:S(2)}) collective-permute-start(bf16[560,128]{1,0:T(8,128)(2,1)S(1)} %collective-permute-done.7.refs_2_), channel_id=1, source_target_pairs={{0,1},{1,2},{2,3},{3,4},{4,5},{5,6},{6,7},{7,0},{8,15},{9,8},{10,9... | collective-permute-start | bytes 430088 | tf_op jit(solution)/shard_map/ppermute | solution.py:483
  79.9 5.2 %collective-permute-start.12 = (bf16[560,128]{1,0:T(8,128)(2,1)S(1)}, bf16[560,128]{1,0:T(8,128)(2,1)S(1)}, u32[]{:S(2)}, u32[]{:S(2)}) collective-permute-start(bf16[560,128]{1,0:T(8,128)(2,1)S(1)} %collective-permute-done.11.refs_3_), channel_id=1, source_target_pairs={{0,7},{1,0},{2,1},{3,2},{4,3},{5,4},{6,5},{7,6},{8,9},{9,10},{10,1... | collective-permute-start | bytes 430088 | tf_op jit(solution)/shard_map/ppermute | solution.py:486
  85.1 1.1 collective-permute-done.8.refs_4_
  86.2 1.9 %collective-permute-start.9 = (bf16[560,128]{1,0:T(8,128)(2,1)S(1)}, bf16[560,128]{1,0:T(8,128)(2,1)S(1)}, u32[]{:S(2)}, u32[]{:S(2)}) collective-permute-start(bf16[560,128]{1,0:T(8,128)(2,1)S(1)} %collective-permute-done.8.refs_4_), channel_id=1, source_target_pairs={{0,1},{1,2},{2,3},{3,4},{4,5},{5,6},{6,7},{7,0},{8,15},{9,8},{10,9... | collective-permute-start | bytes 430088 | tf_op jit(solution)/shard_map/ppermute | solution.py:483
  88.2 5.2 %collective-permute-start.13 = (bf16[560,128]{1,0:T(8,128)(2,1)S(1)}, bf16[560,128]{1,0:T(8,128)(2,1)S(1)}, u32[]{:S(2)}, u32[]{:S(2)}) collective-permute-start(bf16[560,128]{1,0:T(8,128)(2,1)S(1)} %collective-permute-done.12.refs_5_), channel_id=1, source_target_pairs={{0,7},{1,0},{2,1},{3,2},{4,3},{5,4},{6,5},{7,6},{8,9},{9,10},{10,1... | collective-permute-start | bytes 430088 | tf_op jit(solution)/shard_map/ppermute | solution.py:486
  93.3 1.1 collective-permute-done.9.refs_6_
  94.4 1.9 %collective-permute-start.10 = (bf16[560,128]{1,0:T(8,128)(2,1)S(1)}, bf16[560,128]{1,0:T(8,128)(2,1)S(1)}, u32[]{:S(2)}, u32[]{:S(2)}) collective-permute-start(bf16[560,128]{1,0:T(8,128)(2,1)S(1)} %collective-permute-done.9.refs_6_), channel_id=1, source_target_pairs={{0,1},{1,2},{2,3},{3,4},{4,5},{5,6},{6,7},{7,0},{8,15},{9,8},{10,9... | collective-permute-start | bytes 430088 | tf_op jit(solution)/shard_map/ppermute | solution.py:483
  96.4 0.9 weights.3.refs_9_
  97.3 0.4 spread_table.3.refs_0_
  97.6 1.4 combine_table.1.refs_0_
  99.0 3.6 %collective-permute-done.10.refs_8_ = bf16[560,128]{1,0:T(8,128)(2,1)S(1)} collective-permute-done((bf16[560,128]{1,0:T(8,128)(2,1)S(1)}, bf16[560,128]{1,0:T(8,128)(2,1)S(1)}, u32[]{:S(2)}, u32[]{:S(2)}) %collective-permute-start.10) | collective-permute-done | bytes 143392 | tf_op jit(solution)/shard_map/ppermute | solution.py:483
  102.7 2.2 %experts.3 = bf16[8,560,128]{2,1,0:T(8,128)(2,1)S(1)} custom-call(s32[16]{0:T(128)} %refs_0_.4, bf16[560,128]{1,0:T(8,128)(2,1)S(1)} %get-tuple-element.57.refs_1_, bf16[560,128]{1,0:T(8,128)(2,1)S(1)} %collective-permute-done.7.refs_2_, bf16[560,128]{1,0:T(8,128)(2,1)S(1)} %collective-permute-done.11.refs_3_, ...), custom_call_target="tpu_custom_call" | custom-call | tf_op jit(solution)/shard_map/experts/pallas_call | solution.py:324
  104.9 33.4 %all_to_all.31.refs_2_ = bf16[8,560,128]{2,1,0:T(8,128)(2,1)S(1)} all-to-all(bf16[8,560,128]{2,1,0:T(8,128)(2,1)S(1)} %experts.3), channel_id=1, replica_groups=mesh['groups'=2,'ep'=32,'tp'=8] {'tp'}, dimensions={0} | all-to-all | bytes 2293760 | tf_op jit(solution)/shard_map/all_to_all | solution.py:500
  138.3 0.6 spread.3
  138.9 25.9 %all_to_all.32.refs_1_ = bf16[32,32,128]{2,1,0:T(8,128)(2,1)S(1)} all-to-all(bf16[32,32,128]{2,1,0:T(8,128)(2,1)S(1)} %spread.3), channel_id=1, replica_groups=mesh['groups'=2,'ep'=32,'tp'=8] {'ep'}, dimensions={0} | all-to-all | bytes 524288 | tf_op jit(solution)/shard_map/all_to_all | solution.py:501
  164.7 1.0 combine.3
  166.4 11.2 %all_to_all.33.refs_0_ = bf16[8,48,128]{2,1,0:T(8,128)(2,1)S(1)} all-to-all(bf16[8,48,128]{2,1,0:T(8,128)(2,1)S(1)} %get-tuple-element.73), channel_id=1, replica_groups=mesh['groups'=2,'ep'=32,'tp'=8] {'tp'}, dimensions={0} | all-to-all | bytes 196608 | tf_op jit(solution)/shard_map/all_to_all | solution.py:524
  177.6 0.7 finish.1
  (10 shorter events, 0.0 us)
Async XLA Ops:
  69.2 8.8 %collective-permute-start.7 = (bf16[560,128]{1,0:T(8,128)(2,1)S(1)}, bf16[560,128]{1,0:T(8,128)(2,1)S(1)}, u32[]{:S(2)}, u32[]{:S(2)}) collective-permute-start(bf16[560,128]{1,0:T(8,128)(2,1)S(1)} %get-tuple-element.57.refs_1_), channel_id=1, source_target_pairs={{0,1},{1,2},{2,3},{3,4},{4,5},{5,6},{6,7},{7,0},{8,15},{9,8},{10,9... | collective-permute-start | bytes 430088 | tf_op jit(solution)/shard_map/ppermute | solution.py:483
  72.7 7.2 %collective-permute-start.11 = (bf16[560,128]{1,0:T(8,128)(2,1)S(1)}, bf16[560,128]{1,0:T(8,128)(2,1)S(1)}, u32[]{:S(2)}, u32[]{:S(2)}) collective-permute-start(bf16[560,128]{1,0:T(8,128)(2,1)S(1)} %get-tuple-element.57.refs_1_), channel_id=1, source_target_pairs={{0,7},{1,0},{2,1},{3,2},{4,3},{5,4},{6,5},{7,6},{8,9},{9,10},{10,1... | collective-permute-start | bytes 430088 | tf_op jit(solution)/shard_map/ppermute | solution.py:486
  78.0 8.2 %collective-permute-start.8 = (bf16[560,128]{1,0:T(8,128)(2,1)S(1)}, bf16[560,128]{1,0:T(8,128)(2,1)S(1)}, u32[]{:S(2)}, u32[]{:S(2)}) collective-permute-start(bf16[560,128]{1,0:T(8,128)(2,1)S(1)} %collective-permute-done.7.refs_2_), channel_id=1, source_target_pairs={{0,1},{1,2},{2,3},{3,4},{4,5},{5,6},{6,7},{7,0},{8,15},{9,8},{10,9... | collective-permute-start | bytes 430088 | tf_op jit(solution)/shard_map/ppermute | solution.py:483
  79.9 8.2 %collective-permute-start.12 = (bf16[560,128]{1,0:T(8,128)(2,1)S(1)}, bf16[560,128]{1,0:T(8,128)(2,1)S(1)}, u32[]{:S(2)}, u32[]{:S(2)}) collective-permute-start(bf16[560,128]{1,0:T(8,128)(2,1)S(1)} %collective-permute-done.11.refs_3_), channel_id=1, source_target_pairs={{0,7},{1,0},{2,1},{3,2},{4,3},{5,4},{6,5},{7,6},{8,9},{9,10},{10,1... | collective-permute-start | bytes 430088 | tf_op jit(solution)/shard_map/ppermute | solution.py:486
  86.2 8.2 %collective-permute-start.9 = (bf16[560,128]{1,0:T(8,128)(2,1)S(1)}, bf16[560,128]{1,0:T(8,128)(2,1)S(1)}, u32[]{:S(2)}, u32[]{:S(2)}) collective-permute-start(bf16[560,128]{1,0:T(8,128)(2,1)S(1)} %collective-permute-done.8.refs_4_), channel_id=1, source_target_pairs={{0,1},{1,2},{2,3},{3,4},{4,5},{5,6},{6,7},{7,0},{8,15},{9,8},{10,9... | collective-permute-start | bytes 430088 | tf_op jit(solution)/shard_map/ppermute | solution.py:483
  88.2 14.5 %collective-permute-start.13 = (bf16[560,128]{1,0:T(8,128)(2,1)S(1)}, bf16[560,128]{1,0:T(8,128)(2,1)S(1)}, u32[]{:S(2)}, u32[]{:S(2)}) collective-permute-start(bf16[560,128]{1,0:T(8,128)(2,1)S(1)} %collective-permute-done.12.refs_5_), channel_id=1, source_target_pairs={{0,7},{1,0},{2,1},{3,2},{4,3},{5,4},{6,5},{7,6},{8,9},{9,10},{10,1... | collective-permute-start | bytes 430088 | tf_op jit(solution)/shard_map/ppermute | solution.py:486
  94.4 8.2 %collective-permute-start.10 = (bf16[560,128]{1,0:T(8,128)(2,1)S(1)}, bf16[560,128]{1,0:T(8,128)(2,1)S(1)}, u32[]{:S(2)}, u32[]{:S(2)}) collective-permute-start(bf16[560,128]{1,0:T(8,128)(2,1)S(1)} %collective-permute-done.9.refs_6_), channel_id=1, source_target_pairs={{0,1},{1,2},{2,3},{3,4},{4,5},{5,6},{6,7},{7,0},{8,15},{9,8},{10,9... | collective-permute-start | bytes 430088 | tf_op jit(solution)/shard_map/ppermute | solution.py:483
  97.2 5.4 %copy-start.1 = (bf16[2,128,2560]{2,1,0:T(8,128)(2,1)S(1)}, bf16[2,128,2560]{2,1,0:T(8,128)(2,1)}, u32[]{:S(2)}) copy-start(bf16[2,128,2560]{2,1,0:T(8,128)(2,1)} %param.16) | copy-start | bytes 3932164
  97.3 5.4 %copy-start.2 = (bf16[2,128,2560]{2,1,0:T(8,128)(2,1)S(1)}, bf16[2,128,2560]{2,1,0:T(8,128)(2,1)}, u32[]{:S(2)}) copy-start(bf16[2,128,2560]{2,1,0:T(8,128)(2,1)} %param.17) | copy-start | bytes 3932164
  97.6 5.0 %copy-start = (bf16[2,128,2560]{2,1,0:T(8,128)(2,1)S(1)}, bf16[2,128,2560]{2,1,0:T(8,128)(2,1)}, u32[]{:S(2)}) copy-start(bf16[2,128,2560]{2,1,0:T(8,128)(2,1)} %param.15) | copy-start | bytes 3932164

commit v10 on v7

--- a/solution.py
+++ b/solution.py
@@ -134,10 +134,10 @@
     out_ref[...] = total.astype(BF16)
 
 
-def weight_rows(plan, data):
+def weight_rows(plan, data, expert):
     shape = (plan.ranks, plan.ranks * plan.chunk)
-    at = iota(shape, 0) * plan.chunk + plan.chunk - 2
-    return [dot(one_hot(iota(shape, 1) == at + e), data) for e in range(2)]
+    at = iota(shape, 0) * plan.chunk + plan.chunk - 2 + expert
+    return dot(one_hot(iota(shape, 1) == at), data)
 
 
 def target_row(info_ref, plan, named):
@@ -180,7 +180,7 @@
 def compact_kernel(plan, info_ref, in_ref, out_ref, target_ref, needed_ref):
     total = plan.ranks * plan.chunk
     data = in_ref[...].reshape(total, LANE)
-    first = weight_rows(plan, data)[0]
+    first = weight_rows(plan, data, 0)
     named = jnp.where(first > 0.0, 1.0, 0.0)
     target, needed = target_row(info_ref, plan, named)
     target_ref[...] = target
@@ -193,7 +193,7 @@
 def weights_kernel(plan, in_ref, target_ref, weight_ref):
     total = plan.ranks * plan.chunk
     data = in_ref[...].reshape(total, LANE)
-    first, second = weight_rows(plan, data)
+    first, second = weight_rows(plan, data, 0), weight_rows(plan, data, 1)
     place = places(plan, jnp.where(first > 0.0, 1.0, 0.0)).astype(I32)
     full_shape = (plan.ranks, plan.chunk, LANE)
     j = iota(full_shape, 1)
@@ -519,13 +519,9 @@
         )
     right, left = ways
     axes = ("ep", "tp")
-    parts, offsets, values = [packed], [0], []
+    parts, offsets = [packed], [0]
     held = [packed, packed]
     for hop in range(1, lanes // 2 + 1):
-        if hop > 1 and hop - 2 < len(beside):
-            first, value = lax.optimization_barrier((held[0], beside[hop - 2]))
-            held = [first, held[1]]
-            values.append(value)
         got = [lax.ppermute(held[0], axes, right)]
         offsets.append(-hop)
         if hop < lanes // 2:
@@ -533,7 +529,8 @@
             offsets.append(hop)
         parts += got
         held = got
-    return parts, offsets, values
+    last, beside = lax.optimization_barrier((parts[-1], beside))
+    return parts[:-1] + [last], offsets, beside
 
 
 def through_experts(plan, info, received, take_in, matrices):

time: 180 us -> 179 us (level)
  transfers between devices with their start and end apart: 7 -> 7, of which waited for: 3 -> 4; matrix products, arithmetic and copies ran while one was open for 0% -> 0% of each run, Pallas kernels for 2% -> 2%
where the time goes in v10:
time: 179 us
  blocking collectives  138 us (77%)
  starting transfers between devices  23.9 us (13%)
  Pallas kernels  11 us (6%)
  waiting for transfers between devices  5 us (3%)
    all_to_all x1, blocking collectives, on_device(): received = lax.all_to_all(outgoing, 'ep', 0, 0, tiled=True)  66.2 us
    all_to_all x1, blocking collectives, through_experts(): returned = lax.all_to_all(partial, 'tp', 0, 0, tiled=True)  34.6 us
    all_to_all x1, blocking collectives, through_experts(): lax.all_to_all(spread(plan, take_out, needed, returned), 'ep', 0, 0, tile...  25.9 us
    ppermute x3, starting transfers between devices, gather_lanes(): got.append(lax.ppermute(held[1], axes, left))  14.5 us
    all_to_all x1, blocking collectives, on_device(): shares = lax.all_to_all(shares, 'tp', 0, 0, tiled=True)  11.2 us
    pallas_call x10, Pallas kernels, call(): pl.pallas_call(kernel, out_shape=out, in_specs=specs, out_specs=jax.tree....  11 us
    ppermute x4, starting transfers between devices, gather_lanes(): got = [lax.ppermute(held[0], axes, right)]  9.38 us
    ppermute x4, waiting for transfers between devices, gather_lanes(): got = [lax.ppermute(held[0], axes, right)]  4.99 us
  transfers between devices with their start and end apart: 7, of which 4 were waited for; matrix products, arithmetic and copies ran while one was open for 0% of the time, Pallas kernels for 2%

profile of v10, /device:TPU:80, one launch (start us, length us, event | category | flops | bytes accessed | tf_op | source)
XLA Modules:
  0.0 178.6 jit_solution(609115880759312316)
XLA Ops:
  0.0 1.3 pack.1
  1.3 66.2 %all_to_all.30.refs_1_.refs_0_ = bf16[32,32,128]{2,1,0:T(8,128)(2,1)S(1)} all-to-all(bf16[32,32,128]{2,1,0:T(8,128)(2,1)S(1)} %pack.1), channel_id=1, replica_groups=mesh['groups'=2,'ep'=32,'tp'=8] {'ep'}, dimensions={0} | all-to-all | bytes 524288 | tf_op jit(solution)/shard_map/all_to_all | solution.py:557
  67.6 1.6 compact.3
  69.2 3.6 %collective-permute-start.7 = (bf16[560,128]{1,0:T(8,128)(2,1)S(1)}, bf16[560,128]{1,0:T(8,128)(2,1)S(1)}, u32[]{:S(2)}, u32[]{:S(2)}) collective-permute-start(bf16[560,128]{1,0:T(8,128)(2,1)S(1)} %get-tuple-element.61.refs_1_), channel_id=1, source_target_pairs={{0,1},{1,2},{2,3},{3,4},{4,5},{5,6},{6,7},{7,0},{8,15},{9,8},{10,9... | collective-permute-start | bytes 430088 | tf_op jit(solution)/shard_map/ppermute | solution.py:525
  72.7 4.2 %collective-permute-start.11 = (bf16[560,128]{1,0:T(8,128)(2,1)S(1)}, bf16[560,128]{1,0:T(8,128)(2,1)S(1)}, u32[]{:S(2)}, u32[]{:S(2)}) collective-permute-start(bf16[560,128]{1,0:T(8,128)(2,1)S(1)} %get-tuple-element.61.refs_1_), channel_id=1, source_target_pairs={{0,7},{1,0},{2,1},{3,2},{4,3},{5,4},{6,5},{7,6},{8,9},{9,10},{10,1... | collective-permute-start | bytes 430088 | tf_op jit(solution)/shard_map/ppermute | solution.py:528
  76.9 1.1 collective-permute-done.7.refs_2_
  78.0 1.9 %collective-permute-start.8 = (bf16[560,128]{1,0:T(8,128)(2,1)S(1)}, bf16[560,128]{1,0:T(8,128)(2,1)S(1)}, u32[]{:S(2)}, u32[]{:S(2)}) collective-permute-start(bf16[560,128]{1,0:T(8,128)(2,1)S(1)} %collective-permute-done.7.refs_2_), channel_id=1, source_target_pairs={{0,1},{1,2},{2,3},{3,4},{4,5},{5,6},{6,7},{7,0},{8,15},{9,8},{10,9... | collective-permute-start | bytes 430088 | tf_op jit(solution)/shard_map/ppermute | solution.py:525
  79.9 5.2 %collective-permute-start.12 = (bf16[560,128]{1,0:T(8,128)(2,1)S(1)}, bf16[560,128]{1,0:T(8,128)(2,1)S(1)}, u32[]{:S(2)}, u32[]{:S(2)}) collective-permute-start(bf16[560,128]{1,0:T(8,128)(2,1)S(1)} %collective-permute-done.11.refs_3_), channel_id=1, source_target_pairs={{0,7},{1,0},{2,1},{3,2},{4,3},{5,4},{6,5},{7,6},{8,9},{9,10},{10,1... | collective-permute-start | bytes 430088 | tf_op jit(solution)/shard_map/ppermute | solution.py:528
  85.1 1.1 collective-permute-done.8.refs_4_
  86.2 1.9 %collective-permute-start.9 = (bf16[560,128]{1,0:T(8,128)(2,1)S(1)}, bf16[560,128]{1,0:T(8,128)(2,1)S(1)}, u32[]{:S(2)}, u32[]{:S(2)}) collective-permute-start(bf16[560,128]{1,0:T(8,128)(2,1)S(1)} %collective-permute-done.8.refs_4_), channel_id=1, source_target_pairs={{0,1},{1,2},{2,3},{3,4},{4,5},{5,6},{6,7},{7,0},{8,15},{9,8},{10,9... | collective-permute-start | bytes 430088 | tf_op jit(solution)/shard_map/ppermute | solution.py:525
  88.2 5.2 %collective-permute-start.13 = (bf16[560,128]{1,0:T(8,128)(2,1)S(1)}, bf16[560,128]{1,0:T(8,128)(2,1)S(1)}, u32[]{:S(2)}, u32[]{:S(2)}) collective-permute-start(bf16[560,128]{1,0:T(8,128)(2,1)S(1)} %collective-permute-done.12.refs_5_), channel_id=1, source_target_pairs={{0,7},{1,0},{2,1},{3,2},{4,3},{5,4},{6,5},{7,6},{8,9},{9,10},{10,1... | collective-permute-start | bytes 430088 | tf_op jit(solution)/shard_map/ppermute | solution.py:528
  93.3 0.9 weights.3.refs_4_
  94.4 1.9 %collective-permute-start.10 = (bf16[560,128]{1,0:T(8,128)(2,1)S(1)}, bf16[560,128]{1,0:T(8,128)(2,1)S(1)}, u32[]{:S(2)}, u32[]{:S(2)}) collective-permute-start(bf16[560,128]{1,0:T(8,128)(2,1)S(1)} %collective-permute-done.9.refs_6_), channel_id=1, source_target_pairs={{0,1},{1,2},{2,3},{3,4},{4,5},{5,6},{6,7},{7,0},{8,15},{9,8},{10,9... | collective-permute-start | bytes 430088 | tf_op jit(solution)/shard_map/ppermute | solution.py:525
  96.4 0.4 spread_table.3.refs_0_
  96.8 1.3 combine_table.1.refs_0_
  98.2 1.9 %early.3 = (f32[224,256]{1,0:T(8,128)S(1)}, f32[224,256]{1,0:T(8,128)S(1)}) custom-call(s32[16]{0:T(128)} %refs_0_.5, bf16[560,128]{1,0:T(8,128)(2,1)S(1)} %get-tuple-element.61.refs_1_, bf16[560,128]{1,0:T(8,128)(2,1)S(1)} %collective-permute-done.7.refs_2_, bf16[560,128]{1,0:T(8,128)(2,1)S(1)} %collective-permute-done.11.refs_3_, ...), custom_call_target="tpu_custom_call" | custom-call | flops 536870912 | bytes 1048576 | tf_op jit(solution)/shard_map/early/pallas_call | solution.py:349
  100.1 2.6 %collective-permute-done.10.refs_1_ = bf16[560,128]{1,0:T(8,128)(2,1)S(1)} collective-permute-done((bf16[560,128]{1,0:T(8,128)(2,1)S(1)}, bf16[560,128]{1,0:T(8,128)(2,1)S(1)}, u32[]{:S(2)}, u32[]{:S(2)}) %collective-permute-start.10) | collective-permute-done | bytes 143392 | tf_op jit(solution)/shard_map/ppermute | solution.py:525
  102.7 1.4 experts.3
  104.1 34.6 %all_to_all.31.refs_2_ = bf16[8,560,128]{2,1,0:T(8,128)(2,1)S(1)} all-to-all(bf16[8,560,128]{2,1,0:T(8,128)(2,1)S(1)} %experts.3), channel_id=1, replica_groups=mesh['groups'=2,'ep'=32,'tp'=8] {'tp'}, dimensions={0} | all-to-all | bytes 2293760 | tf_op jit(solution)/shard_map/all_to_all | solution.py:542
  138.7 0.6 spread.3
  139.3 25.9 %all_to_all.32.refs_1_ = bf16[32,32,128]{2,1,0:T(8,128)(2,1)S(1)} all-to-all(bf16[32,32,128]{2,1,0:T(8,128)(2,1)S(1)} %spread.3), channel_id=1, replica_groups=mesh['groups'=2,'ep'=32,'tp'=8] {'ep'}, dimensions={0} | all-to-all | bytes 524288 | tf_op jit(solution)/shard_map/all_to_all | solution.py:543
  165.1 1.0 combine.3
  166.8 11.2 %all_to_all.33.refs_0_ = bf16[8,48,128]{2,1,0:T(8,128)(2,1)S(1)} all-to-all(bf16[8,48,128]{2,1,0:T(8,128)(2,1)S(1)} %get-tuple-element.79), channel_id=1, replica_groups=mesh['groups'=2,'ep'=32,'tp'=8] {'tp'}, dimensions={0} | all-to-all | bytes 196608 | tf_op jit(solution)/shard_map/all_to_all | solution.py:566
  178.0 0.7 finish.1
  (11 shorter events, 0.4 us)
Async XLA Ops:
  69.2 8.8 %collective-permute-start.7 = (bf16[560,128]{1,0:T(8,128)(2,1)S(1)}, bf16[560,128]{1,0:T(8,128)(2,1)S(1)}, u32[]{:S(2)}, u32[]{:S(2)}) collective-permute-start(bf16[560,128]{1,0:T(8,128)(2,1)S(1)} %get-tuple-element.61.refs_1_), channel_id=1, source_target_pairs={{0,1},{1,2},{2,3},{3,4},{4,5},{5,6},{6,7},{7,0},{8,15},{9,8},{10,9... | collective-permute-start | bytes 430088 | tf_op jit(solution)/shard_map/ppermute | solution.py:525
  72.7 7.2 %collective-permute-start.11 = (bf16[560,128]{1,0:T(8,128)(2,1)S(1)}, bf16[560,128]{1,0:T(8,128)(2,1)S(1)}, u32[]{:S(2)}, u32[]{:S(2)}) collective-permute-start(bf16[560,128]{1,0:T(8,128)(2,1)S(1)} %get-tuple-element.61.refs_1_), channel_id=1, source_target_pairs={{0,7},{1,0},{2,1},{3,2},{4,3},{5,4},{6,5},{7,6},{8,9},{9,10},{10,1... | collective-permute-start | bytes 430088 | tf_op jit(solution)/shard_map/ppermute | solution.py:528
  78.0 8.2 %collective-permute-start.8 = (bf16[560,128]{1,0:T(8,128)(2,1)S(1)}, bf16[560,128]{1,0:T(8,128)(2,1)S(1)}, u32[]{:S(2)}, u32[]{:S(2)}) collective-permute-start(bf16[560,128]{1,0:T(8,128)(2,1)S(1)} %collective-permute-done.7.refs_2_), channel_id=1, source_target_pairs={{0,1},{1,2},{2,3},{3,4},{4,5},{5,6},{6,7},{7,0},{8,15},{9,8},{10,9... | collective-permute-start | bytes 430088 | tf_op jit(solution)/shard_map/ppermute | solution.py:525
  79.9 8.2 %collective-permute-start.12 = (bf16[560,128]{1,0:T(8,128)(2,1)S(1)}, bf16[560,128]{1,0:T(8,128)(2,1)S(1)}, u32[]{:S(2)}, u32[]{:S(2)}) collective-permute-start(bf16[560,128]{1,0:T(8,128)(2,1)S(1)} %collective-permute-done.11.refs_3_), channel_id=1, source_target_pairs={{0,7},{1,0},{2,1},{3,2},{4,3},{5,4},{6,5},{7,6},{8,9},{9,10},{10,1... | collective-permute-start | bytes 430088 | tf_op jit(solution)/shard_map/ppermute | solution.py:528
  86.2 8.2 %collective-permute-start.9 = (bf16[560,128]{1,0:T(8,128)(2,1)S(1)}, bf16[560,128]{1,0:T(8,128)(2,1)S(1)}, u32[]{:S(2)}, u32[]{:S(2)}) collective-permute-start(bf16[560,128]{1,0:T(8,128)(2,1)S(1)} %collective-permute-done.8.refs_4_), channel_id=1, source_target_pairs={{0,1},{1,2},{2,3},{3,4},{4,5},{5,6},{6,7},{7,0},{8,15},{9,8},{10,9... | collective-permute-start | bytes 430088 | tf_op jit(solution)/shard_map/ppermute | solution.py:525
  88.2 9.9 %collective-permute-start.13 = (bf16[560,128]{1,0:T(8,128)(2,1)S(1)}, bf16[560,128]{1,0:T(8,128)(2,1)S(1)}, u32[]{:S(2)}, u32[]{:S(2)}) collective-permute-start(bf16[560,128]{1,0:T(8,128)(2,1)S(1)} %collective-permute-done.12.refs_5_), channel_id=1, source_target_pairs={{0,7},{1,0},{2,1},{3,2},{4,3},{5,4},{6,5},{7,6},{8,9},{9,10},{10,1... | collective-permute-start | bytes 430088 | tf_op jit(solution)/shard_map/ppermute | solution.py:528
  94.4 8.2 %collective-permute-start.10 = (bf16[560,128]{1,0:T(8,128)(2,1)S(1)}, bf16[560,128]{1,0:T(8,128)(2,1)S(1)}, u32[]{:S(2)}, u32[]{:S(2)}) collective-permute-start(bf16[560,128]{1,0:T(8,128)(2,1)S(1)} %collective-permute-done.9.refs_6_), channel_id=1, source_target_pairs={{0,1},{1,2},{2,3},{3,4},{4,5},{5,6},{6,7},{7,0},{8,15},{9,8},{10,9... | collective-permute-start | bytes 430088 | tf_op jit(solution)/shard_map/ppermute | solution.py:525
  96.4 1.7 copy-start.1
  96.8 1.4 copy-start
  98.2 4.5 %copy-start.2 = (bf16[2,128,2560]{2,1,0:T(8,128)(2,1)S(1)}, bf16[2,128,2560]{2,1,0:T(8,128)(2,1)}, u32[]{:S(2)}) copy-start(bf16[2,128,2560]{2,1,0:T(8,128)(2,1)} %param.17) | copy-start | bytes 3932164

commit v11 on v6

--- a/solution.py
+++ b/solution.py
@@ -134,10 +134,10 @@
     out_ref[...] = total.astype(BF16)
 
 
-def weight_rows(plan, data):
+def weight_rows(plan, data, expert):
     shape = (plan.ranks, plan.ranks * plan.chunk)
-    at = iota(shape, 0) * plan.chunk + plan.chunk - 2
-    return [dot(one_hot(iota(shape, 1) == at + e), data) for e in range(2)]
+    at = iota(shape, 0) * plan.chunk + plan.chunk - 2 + expert
+    return dot(one_hot(iota(shape, 1) == at), data)
 
 
 def target_row(info_ref, plan, named):
@@ -180,7 +180,7 @@
 def compact_kernel(plan, info_ref, in_ref, out_ref, target_ref, needed_ref):
     total = plan.ranks * plan.chunk
     data = in_ref[...].reshape(total, LANE)
-    first = weight_rows(plan, data)[0]
+    first = weight_rows(plan, data, 0)
     named = jnp.where(first > 0.0, 1.0, 0.0)
     target, needed = target_row(info_ref, plan, named)
     target_ref[...] = target
@@ -193,7 +193,7 @@
 def weights_kernel(plan, in_ref, target_ref, weight_ref):
     total = plan.ranks * plan.chunk
     data = in_ref[...].reshape(total, LANE)
-    first, second = weight_rows(plan, data)
+    first, second = weight_rows(plan, data, 0), weight_rows(plan, data, 1)
     place = places(plan, jnp.where(first > 0.0, 1.0, 0.0)).astype(I32)
     full_shape = (plan.ranks, plan.chunk, LANE)
     j = iota(full_shape, 1)
@@ -480,7 +480,7 @@
     parts, offsets, values = [packed], [0], []
     held = [packed, packed]
     for hop in range(1, lanes // 2 + 1):
-        if hop > 1 and hop - 2 < len(beside):
+        if hop > 1 and hop - 2 < len(beside) - 1 and hop < lanes // 2:
             first, value = lax.optimization_barrier((held[0], beside[hop - 2]))
             held = [first, held[1]]
             values.append(value)
@@ -491,7 +491,8 @@
             offsets.append(hop)
         parts += got
         held = got
-    return parts, offsets, values
+    last, rest = lax.optimization_barrier((parts[-1], beside[len(values) :]))
+    return parts[:-1] + [last], offsets, values + list(rest)
 
 
 def through_experts(plan, info, received, take_in, matrices):

time: 178 us -> 183 us (1.028)
  blocking collectives: 136 us -> 139 us
    all_to_all x1, blocking collectives: 32.2 us -> 35.5 us  [through_experts(): returned = lax.all_to_all(partial, 'tp', 0, 0, tiled=True)]
  transfers between devices with their start and end apart: 7 -> 7, of which waited for: 4 -> 5; matrix products, arithmetic and copies ran while one was open for 0% -> 0% of each run, Pallas kernels for 1% -> 1%
where the time goes in v11:
time: 183 us; the launch traced here: 182 us
  blocking collectives  139 us (76%)
  starting transfers between devices  25 us (14%)
  Pallas kernels  9.77 us (5%)
  waiting for transfers between devices  7.87 us (4%)
    all_to_all x1, blocking collectives, on_device(): received = lax.all_to_all(outgoing, 'ep', 0, 0, tiled=True)  66.2 us
    all_to_all x1, blocking collectives, through_experts(): returned = lax.all_to_all(partial, 'tp', 0, 0, tiled=True)  35.5 us
    all_to_all x1, blocking collectives, through_experts(): lax.all_to_all(spread(plan, take_out, needed, returned), 'ep', 0, 0, tile...  25.9 us
    ppermute x3, starting transfers between devices, gather_lanes(): got.append(lax.ppermute(held[1], axes, left))  15.5 us
    all_to_all x1, blocking collectives, on_device(): shares = lax.all_to_all(shares, 'tp', 0, 0, tiled=True)  11.2 us
    pallas_call x9, Pallas kernels, call(): pl.pallas_call(kernel, out_shape=out, in_specs=specs, out_specs=jax.tree....  9.77 us
    ppermute x4, starting transfers between devices, gather_lanes(): got = [lax.ppermute(held[0], axes, right)]  9.51 us
    ppermute x4, waiting for transfers between devices, gather_lanes(): got = [lax.ppermute(held[0], axes, right)]  7.24 us
  transfers between devices with their start and end apart: 7, of which 5 were waited for; matrix products, arithmetic and copies ran while one was open for 0% of the time, Pallas kernels for 1%

profile of v11, /device:TPU:80, one launch (start us, length us, event | category | flops | bytes accessed | tf_op | source)
XLA Modules:
  0.0 182.3 jit_solution(7005775432623369871)
XLA Ops:
  0.0 1.3 pack.1
  1.3 66.2 %all_to_all.30.refs_1_.refs_0_ = bf16[32,32,128]{2,1,0:T(8,128)(2,1)S(1)} all-to-all(bf16[32,32,128]{2,1,0:T(8,128)(2,1)S(1)} %pack.1), channel_id=1, replica_groups=mesh['groups'=2,'ep'=32,'tp'=8] {'ep'}, dimensions={0} | all-to-all | bytes 524288 | tf_op jit(solution)/shard_map/all_to_all | solution.py:519
  67.6 1.6 compact.3
  69.2 3.6 %collective-permute-start.7 = (bf16[560,128]{1,0:T(8,128)(2,1)S(1)}, bf16[560,128]{1,0:T(8,128)(2,1)S(1)}, u32[]{:S(2)}, u32[]{:S(2)}) collective-permute-start(bf16[560,128]{1,0:T(8,128)(2,1)S(1)} %get-tuple-element.61.refs_1_), channel_id=1, source_target_pairs={{0,1},{1,2},{2,3},{3,4},{4,5},{5,6},{6,7},{7,0},{8,15},{9,8},{10,9... | collective-permute-start | bytes 430088 | tf_op jit(solution)/shard_map/ppermute | solution.py:487
  72.7 0.9 weights.3.refs_9_
  73.6 4.4 %collective-permute-done.7.refs_2_ = bf16[560,128]{1,0:T(8,128)(2,1)S(1)} collective-permute-done((bf16[560,128]{1,0:T(8,128)(2,1)S(1)}, bf16[560,128]{1,0:T(8,128)(2,1)S(1)}, u32[]{:S(2)}, u32[]{:S(2)}) %collective-permute-start.7) | collective-permute-done | bytes 143392 | tf_op jit(solution)/shard_map/ppermute | solution.py:487
  78.0 1.9 %collective-permute-start.8 = (bf16[560,128]{1,0:T(8,128)(2,1)S(1)}, bf16[560,128]{1,0:T(8,128)(2,1)S(1)}, u32[]{:S(2)}, u32[]{:S(2)}) collective-permute-start(bf16[560,128]{1,0:T(8,128)(2,1)S(1)} %collective-permute-done.7.refs_2_), channel_id=1, source_target_pairs={{0,1},{1,2},{2,3},{3,4},{4,5},{5,6},{6,7},{7,0},{8,15},{9,8},{10,9... | collective-permute-start | bytes 430088 | tf_op jit(solution)/shard_map/ppermute | solution.py:487
  79.9 5.2 %collective-permute-start.11 = (bf16[560,128]{1,0:T(8,128)(2,1)S(1)}, bf16[560,128]{1,0:T(8,128)(2,1)S(1)}, u32[]{:S(2)}, u32[]{:S(2)}) collective-permute-start(bf16[560,128]{1,0:T(8,128)(2,1)S(1)} %get-tuple-element.61.refs_1_), channel_id=1, source_target_pairs={{0,7},{1,0},{2,1},{3,2},{4,3},{5,4},{6,5},{7,6},{8,9},{9,10},{10,1... | collective-permute-start | bytes 430088 | tf_op jit(solution)/shard_map/ppermute | solution.py:490
  85.5 0.7 collective-permute-done.8.refs_4_
  86.2 2.1 %collective-permute-start.9 = (bf16[560,128]{1,0:T(8,128)(2,1)S(1)}, bf16[560,128]{1,0:T(8,128)(2,1)S(1)}, u32[]{:S(2)}, u32[]{:S(2)}) collective-permute-start(bf16[560,128]{1,0:T(8,128)(2,1)S(1)} %collective-permute-done.8.refs_4_), channel_id=1, source_target_pairs={{0,1},{1,2},{2,3},{3,4},{4,5},{5,6},{6,7},{7,0},{8,15},{9,8},{10,9... | collective-permute-start | bytes 430088 | tf_op jit(solution)/shard_map/ppermute | solution.py:487
  88.3 5.2 %collective-permute-start.12 = (bf16[560,128]{1,0:T(8,128)(2,1)S(1)}, bf16[560,128]{1,0:T(8,128)(2,1)S(1)}, u32[]{:S(2)}, u32[]{:S(2)}) collective-permute-start(bf16[560,128]{1,0:T(8,128)(2,1)S(1)} %collective-permute-done.11.refs_3_), channel_id=1, source_target_pairs={{0,7},{1,0},{2,1},{3,2},{4,3},{5,4},{6,5},{7,6},{8,9},{9,10},{10,1... | collective-permute-start | bytes 430088 | tf_op jit(solution)/shard_map/ppermute | solution.py:490
  93.5 1.1 collective-permute-done.9.refs_6_
  94.6 1.9 %collective-permute-start.10 = (bf16[560,128]{1,0:T(8,128)(2,1)S(1)}, bf16[560,128]{1,0:T(8,128)(2,1)S(1)}, u32[]{:S(2)}, u32[]{:S(2)}) collective-permute-start(bf16[560,128]{1,0:T(8,128)(2,1)S(1)} %collective-permute-done.9.refs_6_), channel_id=1, source_target_pairs={{0,1},{1,2},{2,3},{3,4},{4,5},{5,6},{6,7},{7,0},{8,15},{9,8},{10,9... | collective-permute-start | bytes 430088 | tf_op jit(solution)/shard_map/ppermute | solution.py:487
  96.5 5.2 %collective-permute-start.13 = (bf16[560,128]{1,0:T(8,128)(2,1)S(1)}, bf16[560,128]{1,0:T(8,128)(2,1)S(1)}, u32[]{:S(2)}, u32[]{:S(2)}) collective-permute-start(bf16[560,128]{1,0:T(8,128)(2,1)S(1)} %collective-permute-done.12.refs_5_), channel_id=1, source_target_pairs={{0,7},{1,0},{2,1},{3,2},{4,3},{5,4},{6,5},{7,6},{8,9},{9,10},{10,1... | collective-permute-start | bytes 430088 | tf_op jit(solution)/shard_map/ppermute | solution.py:490
  101.7 1.2 combine_table.1.refs_0_
  102.9 1.0 collective-permute-done.10.refs_8_
  103.9 0.6 collective-permute-done.13.refs_7_
  104.6 2.2 %experts.3 = bf16[8,560,128]{2,1,0:T(8,128)(2,1)S(1)} custom-call(s32[16]{0:T(128)} %refs_0_.4, bf16[560,128]{1,0:T(8,128)(2,1)S(1)} %get-tuple-element.61.refs_1_, bf16[560,128]{1,0:T(8,128)(2,1)S(1)} %collective-permute-done.7.refs_2_, bf16[560,128]{1,0:T(8,128)(2,1)S(1)} %collective-permute-done.11.refs_3_, ...), custom_call_target="tpu_custom_call" | custom-call | tf_op jit(solution)/shard_map/experts/pallas_call | solution.py:324
  106.8 35.5 %all_to_all.31.refs_2_ = bf16[8,560,128]{2,1,0:T(8,128)(2,1)S(1)} all-to-all(bf16[8,560,128]{2,1,0:T(8,128)(2,1)S(1)} %experts.3), channel_id=1, replica_groups=mesh['groups'=2,'ep'=32,'tp'=8] {'tp'}, dimensions={0} | all-to-all | bytes 2293760 | tf_op jit(solution)/shard_map/all_to_all | solution.py:504
  142.3 0.6 spread.3
  142.9 25.9 %all_to_all.32.refs_1_ = bf16[32,32,128]{2,1,0:T(8,128)(2,1)S(1)} all-to-all(bf16[32,32,128]{2,1,0:T(8,128)(2,1)S(1)} %spread.3), channel_id=1, replica_groups=mesh['groups'=2,'ep'=32,'tp'=8] {'ep'}, dimensions={0} | all-to-all | bytes 524288 | tf_op jit(solution)/shard_map/all_to_all | solution.py:505
  168.8 1.0 combine.3
  170.5 11.2 %all_to_all.33.refs_0_ = bf16[8,48,128]{2,1,0:T(8,128)(2,1)S(1)} all-to-all(bf16[8,48,128]{2,1,0:T(8,128)(2,1)S(1)} %get-tuple-element.79), channel_id=1, replica_groups=mesh['groups'=2,'ep'=32,'tp'=8] {'tp'}, dimensions={0} | all-to-all | bytes 196608 | tf_op jit(solution)/shard_map/all_to_all | solution.py:528
  181.6 0.7 finish.1
  (10 shorter events, 0.4 us)
Async XLA Ops:
  69.2 8.8 %collective-permute-start.7 = (bf16[560,128]{1,0:T(8,128)(2,1)S(1)}, bf16[560,128]{1,0:T(8,128)(2,1)S(1)}, u32[]{:S(2)}, u32[]{:S(2)}) collective-permute-start(bf16[560,128]{1,0:T(8,128)(2,1)S(1)} %get-tuple-element.61.refs_1_), channel_id=1, source_target_pairs={{0,1},{1,2},{2,3},{3,4},{4,5},{5,6},{6,7},{7,0},{8,15},{9,8},{10,9... | collective-permute-start | bytes 430088 | tf_op jit(solution)/shard_map/ppermute | solution.py:487
  78.0 8.2 %collective-permute-start.8 = (bf16[560,128]{1,0:T(8,128)(2,1)S(1)}, bf16[560,128]{1,0:T(8,128)(2,1)S(1)}, u32[]{:S(2)}, u32[]{:S(2)}) collective-permute-start(bf16[560,128]{1,0:T(8,128)(2,1)S(1)} %collective-permute-done.7.refs_2_), channel_id=1, source_target_pairs={{0,1},{1,2},{2,3},{3,4},{4,5},{5,6},{6,7},{7,0},{8,15},{9,8},{10,9... | collective-permute-start | bytes 430088 | tf_op jit(solution)/shard_map/ppermute | solution.py:487
  79.9 8.4 %collective-permute-start.11 = (bf16[560,128]{1,0:T(8,128)(2,1)S(1)}, bf16[560,128]{1,0:T(8,128)(2,1)S(1)}, u32[]{:S(2)}, u32[]{:S(2)}) collective-permute-start(bf16[560,128]{1,0:T(8,128)(2,1)S(1)} %get-tuple-element.61.refs_1_), channel_id=1, source_target_pairs={{0,7},{1,0},{2,1},{3,2},{4,3},{5,4},{6,5},{7,6},{8,9},{9,10},{10,1... | collective-permute-start | bytes 430088 | tf_op jit(solution)/shard_map/ppermute | solution.py:490
  85.1 19.4 %copy-start.1 = (bf16[2,128,2560]{2,1,0:T(8,128)(2,1)S(1)}, bf16[2,128,2560]{2,1,0:T(8,128)(2,1)}, u32[]{:S(2)}) copy-start(bf16[2,128,2560]{2,1,0:T(8,128)(2,1)} %param.16) | copy-start | bytes 3932164
  85.1 19.4 %copy-start.2 = (bf16[2,128,2560]{2,1,0:T(8,128)(2,1)S(1)}, bf16[2,128,2560]{2,1,0:T(8,128)(2,1)}, u32[]{:S(2)}) copy-start(bf16[2,128,2560]{2,1,0:T(8,128)(2,1)} %param.17) | copy-start | bytes 3932164
  85.5 19.1 %copy-start = (bf16[2,128,2560]{2,1,0:T(8,128)(2,1)S(1)}, bf16[2,128,2560]{2,1,0:T(8,128)(2,1)}, u32[]{:S(2)}) copy-start(bf16[2,128,2560]{2,1,0:T(8,128)(2,1)} %param.15) | copy-start | bytes 3932164
  86.2 8.4 %collective-permute-start.9 = (bf16[560,128]{1,0:T(8,128)(2,1)S(1)}, bf16[560,128]{1,0:T(8,128)(2,1)S(1)}, u32[]{:S(2)}, u32[]{:S(2)}) collective-permute-start(bf16[560,128]{1,0:T(8,128)(2,1)S(1)} %collective-permute-done.8.refs_4_), channel_id=1, source_target_pairs={{0,1},{1,2},{2,3},{3,4},{4,5},{5,6},{6,7},{7,0},{8,15},{9,8},{10,9... | collective-permute-start | bytes 430088 | tf_op jit(solution)/shard_map/ppermute | solution.py:487
  88.3 8.2 %collective-permute-start.12 = (bf16[560,128]{1,0:T(8,128)(2,1)S(1)}, bf16[560,128]{1,0:T(8,128)(2,1)S(1)}, u32[]{:S(2)}, u32[]{:S(2)}) collective-permute-start(bf16[560,128]{1,0:T(8,128)(2,1)S(1)} %collective-permute-done.11.refs_3_), channel_id=1, source_target_pairs={{0,7},{1,0},{2,1},{3,2},{4,3},{5,4},{6,5},{7,6},{8,9},{9,10},{10,1... | collective-permute-start | bytes 430088 | tf_op jit(solution)/shard_map/ppermute | solution.py:490
  94.6 9.4 %collective-permute-start.10 = (bf16[560,128]{1,0:T(8,128)(2,1)S(1)}, bf16[560,128]{1,0:T(8,128)(2,1)S(1)}, u32[]{:S(2)}, u32[]{:S(2)}) collective-permute-start(bf16[560,128]{1,0:T(8,128)(2,1)S(1)} %collective-permute-done.9.refs_6_), channel_id=1, source_target_pairs={{0,1},{1,2},{2,3},{3,4},{4,5},{5,6},{6,7},{7,0},{8,15},{9,8},{10,9... | collective-permute-start | bytes 430088 | tf_op jit(solution)/shard_map/ppermute | solution.py:487
  96.5 8.0 %collective-permute-start.13 = (bf16[560,128]{1,0:T(8,128)(2,1)S(1)}, bf16[560,128]{1,0:T(8,128)(2,1)S(1)}, u32[]{:S(2)}, u32[]{:S(2)}) collective-permute-start(bf16[560,128]{1,0:T(8,128)(2,1)S(1)} %collective-permute-done.12.refs_5_), channel_id=1, source_target_pairs={{0,7},{1,0},{2,1},{3,2},{4,3},{5,4},{6,5},{7,6},{8,9},{9,10},{10,1... | collective-permute-start | bytes 430088 | tf_op jit(solution)/shard_map/ppermute | solution.py:490
